TPU v7x, 128 devices: a whole 4x4x4 slice. The times are simulated.
128 devices in a mesh: lon: 8 (over y, x_lo), lat: 16 (over x_hi, z, core).
Axes of the slice: x: 4 (x_hi: 2, x_lo: 2; x = x_hi * 2 + x_lo), y: 4, z: 4, core: 2. Of those that a mesh axis runs over, the one named last changes fastest.
Arguments:
- tracers: float32 [4, 16, 2048, 1024], P(None, None, 'lat', 'lon'), may hold values from -6 to 6
- fill_fraction: float32 [16, 2048, 1024], P(None, 'lat', 'lon'), may hold values from 0.3 to 1
- ocean_mask: int32 [16, 2048, 1024], P(None, 'lat', 'lon'), may hold values 0 or 1
- east_speed: float32 [16, 2048, 1024], P(None, 'lat', 'lon'), may hold values from -3 to 3
- north_speed: float32 [16, 2048, 1024], P(None, 'lat', 'lon'), may hold values from -3 to 3
- diffusivity: float32 [16], replicated, may hold values from 0.1 to 1
- cell_area: float32 [2048, 1024], P('lat', 'lon'), may hold values from 0.25 to 1
- owner_map: int32 [16384, 1], P(('lon', 'lat')), may hold values from 0 to 127; in each aligned block of 128 rows (0 to 127, 128 to 255, ...) at most 2 rows name the same one
Outputs:
- updated: float32 [4, 16, 2048, 1024], P(None, None, 'lat', 'lon')
- received_two: float32 [128, 256, 2048], P(('lon', 'lat'))
- received_four: float32 [128, 256, 512], P(('lon', 'lat'))
Inputs may be any that keep to these rules, and one draw needn't show every extreme that they name: `owner_map`: owner device numbers in lon-major order. Of the 128 rows of one device, at most 2 name the same owner, and in some device exactly 2 do.
All inputs are finite; a program needn't handle non-finite values. No bound on the sum of `ocean_mask` on one device may be relied on, other than what follows from the above.
Results may differ from a plain program's by a relative error of at most 0.00007.
Values sent between devices are 32-bit elements; how exact they have to be, the bound alone decides.
No kernel may reach another device: no remote copies, remote signals or barrier semaphores. Data moves between devices by JAX's collectives and lax.ppermute only.
A program may use at most 128 MiB of HBM per device.

v0:
```python
import jax
import jax.numpy as jnp
from jax import lax
from jax.sharding import PartitionSpec as P

BAND_ROWS = 16


time_step = 0.05
depth_floor = 0.25
weight_floor = 0.25


def padded(block, sides, width, periodic):
    for axis, dim in sides:
        count = lax.axis_size(axis)
        forward = [(i, i + 1) for i in range(count - 1)]
        if periodic:
            forward.append((count - 1, 0))
        backward = [(target, source) for source, target in forward]
        low = lax.ppermute(
            lax.slice_in_dim(block, block.shape[dim] - width, None, axis=dim), axis, forward
        )
        high = lax.ppermute(lax.slice_in_dim(block, 0, width, axis=dim), axis, backward)
        block = jnp.concatenate([low, block, high], axis=dim)
    return block


def partner_2(block, axis, stride):
    count = lax.axis_size(axis)
    route = []
    for low in range(count):
        high = low | 1 << stride
        if high != low and high < count:
            route += [(low, high), (high, low)]
    return lax.ppermute(block, axis, route)


def sent_together(arrays, axis, split_dim, concat_dim, along):
    widths = [a.shape[along] for a in arrays]
    both = jnp.concatenate(arrays, axis=along)
    whole = lax.all_to_all(both, axis, split_axis=split_dim, concat_axis=concat_dim, tiled=True)
    return tuple(jnp.split(whole, [sum(widths[:k]) for k in range(1, len(widths))], axis=along))


def face_flux(lower_val, upper_val, lower_h, upper_h, lower_speed, upper_speed, mixing):
    open_depth = jnp.minimum(lower_h, upper_h)
    face_speed = 0.5 * (lower_speed + upper_speed)
    return open_depth * (
        0.5 * face_speed * (lower_val + upper_val)
        - 0.5 * jnp.abs(face_speed) * (upper_val - lower_val)
        - mixing * (upper_val - lower_val)
    )


def pool_pairs(field):
    old_shape = field.shape
    return field.reshape(old_shape[:-2] + (old_shape[-2] // 2, 2, old_shape[-1] // 2, 2)).sum(
        axis=(-3, -1)
    )


def coarsen(updated, weight):
    weighted = pool_pairs(updated * weight[None])
    weight_two = pool_pairs(weight)
    weighted_four = pool_pairs(weighted)
    weight_four = pool_pairs(weight_two)
    coarse_two = weighted / jnp.maximum(weight_two, weight_floor)[None]
    coarse_four = weighted_four / jnp.maximum(weight_four, weight_floor)[None]
    return (coarse_two, coarse_four)


def band_blocks(field, band):
    shape_of = field.shape
    bands = shape_of[2] // band
    split = field.reshape(shape_of[0], shape_of[1], bands, band, shape_of[3])
    return split.transpose(1, 2, 0, 3, 4).reshape(
        shape_of[1] * bands, shape_of[0] * band * shape_of[3]
    )


def column_edges(field):
    return jnp.concatenate([field[..., :1], field[..., -1:]], axis=-1)


def row_edges(field):
    return jnp.concatenate([field[..., :1, :], field[..., -1:, :]], axis=-2)


def shifted_east(field, column):
    return jnp.concatenate([field[..., 1:], column[..., None]], axis=-1)


def shifted_north(field, row):
    return jnp.concatenate([field[..., 1:, :], row[..., None, :]], axis=-2)


def local(
    tracers, fill_fraction, ocean_mask, east_speed, north_speed, diffusivity, cell_area, owner_map
):
    wet_depth = fill_fraction * ocean_mask.astype(jnp.float32)
    mixing = diffusivity[:, None, None]
    mixing_edge = diffusivity[:, None]
    count_tr = tracers.shape[0]
    lon_pack = jnp.concatenate(
        [column_edges(tracers), column_edges(wet_depth)[None], column_edges(east_speed)[None]],
        axis=0,
    )
    lon_got = padded(lon_pack, (("lon", 3),), 1, True)
    west_col = lon_got[..., 0]
    east_col = lon_got[..., 3]
    lat_pack = jnp.concatenate(
        [row_edges(tracers), row_edges(wet_depth)[None], row_edges(north_speed)[None]], axis=0
    )
    lat_got = padded(lat_pack, (("lat", 2),), 1, False)
    south_row = lat_got[:, :, 0, :]
    north_row = lat_got[:, :, 3, :]
    partner = lat_pack[:, :, 1, :]
    for bit_index in range(lax.axis_size("lon").bit_length() - 1):
        partner = partner_2(partner, "lon", bit_index)
    folded = jnp.flip(partner, axis=-1)
    fold_sign = jnp.concatenate(
        [jnp.ones((count_tr + 1,), jnp.float32), -jnp.ones((1,), jnp.float32)]
    )
    folded = folded * fold_sign[:, None, None]
    at_fold = lax.axis_index("lat") == lax.axis_size("lat") - 1
    north_row = jnp.where(at_fold, folded, north_row)
    east_flux = face_flux(
        tracers,
        shifted_east(tracers, east_col[:count_tr]),
        wet_depth,
        shifted_east(wet_depth, east_col[count_tr]),
        east_speed,
        shifted_east(east_speed, east_col[count_tr + 1]),
        mixing,
    )
    west_face = face_flux(
        west_col[:count_tr],
        tracers[..., 0],
        west_col[count_tr],
        wet_depth[..., 0],
        west_col[count_tr + 1],
        east_speed[..., 0],
        mixing_edge,
    )
    west_flux = jnp.concatenate([west_face[..., None], east_flux[..., :-1]], axis=-1)
    north_flux = face_flux(
        tracers,
        shifted_north(tracers, north_row[:count_tr]),
        wet_depth,
        shifted_north(wet_depth, north_row[count_tr]),
        north_speed,
        shifted_north(north_speed, north_row[count_tr + 1]),
        mixing,
    )
    south_face = face_flux(
        south_row[:count_tr],
        tracers[:, :, 0, :],
        south_row[count_tr],
        wet_depth[:, 0, :],
        south_row[count_tr + 1],
        north_speed[:, 0, :],
        mixing_edge,
    )
    south_flux = jnp.concatenate([south_face[:, :, None, :], north_flux[:, :, :-1, :]], axis=-2)
    volume = cell_area[None] * jnp.maximum(wet_depth, depth_floor)
    updated = tracers + time_step * (west_flux - east_flux + (south_flux - north_flux)) / volume
    coarse_two, coarse_four = coarsen(updated, cell_area[None] * wet_depth)
    blocks_two = band_blocks(coarse_two, BAND_ROWS // 2)
    blocks_four = band_blocks(coarse_four, BAND_ROWS // 4)
    lon_count = lax.axis_size("lon")
    lat_count = lax.axis_size("lat")
    devices = lon_count * lat_count
    capacity = max(2, 2 * blocks_two.shape[0] // devices)
    owners = owner_map[:, 0]
    onehot = (owners[:, None] == jnp.arange(devices, dtype=jnp.int32)[None, :]).astype(jnp.int32)
    rank_in = jnp.sum((jnp.cumsum(onehot, axis=0) - onehot) * onehot, axis=1)
    slot_index = owners * capacity + rank_in
    placing = (
        slot_index[:, None] == jnp.arange(devices * capacity, dtype=jnp.int32)[None, :]
    ).astype(jnp.float32)
    contract = (((0,), (0,)), ((), ()))
    send_two = lax.dot_general(
        placing,
        blocks_two,
        contract,
        precision=lax.Precision.HIGHEST,
        preferred_element_type=jnp.float32,
    )
    send_four = lax.dot_general(
        placing,
        blocks_four,
        contract,
        precision=lax.Precision.HIGHEST,
        preferred_element_type=jnp.float32,
    )
    received_two, received_four = sent_together((send_two, send_four), ("lon", "lat"), 0, 0, 1)
    return (updated, received_two[None], received_four[None])


def solution(mesh):
    in_specs = (
        P(None, None, "lat", "lon"),
        P(None, "lat", "lon"),
        P(None, "lat", "lon"),
        P(None, "lat", "lon"),
        P(None, "lat", "lon"),
        P(),
        P("lat", "lon"),
        P(("lon", "lat"), None),
    )
    out_specs = (
        P(None, None, "lat", "lon"),
        P(("lon", "lat"), None, None),
        P(("lon", "lat"), None, None),
    )
    return jax.shard_map(local, mesh=mesh, in_specs=in_specs, out_specs=out_specs, check_vma=False)
```

profile of v0, /device:TPU:0, one launch (start us, length us, event | category | flops | bytes accessed | tf_op | source)
XLA Modules:
  0.0 277.4 jit_solution(59611734136146359)
XLA Ops:
  5.3 2.6 copy.121
  18.7 8.2 %fusion.15 = (f32[4,16,128,1]{3,2,1,0:T(8,128)}, f32[4,16,128,1]{3,2,1,0:T(8,128)}) fusion(f32[4,16,128,128]{3,2,1,0:T(8,128)} %param.8), kind=kLoop, calls=%fused_computation.65 | loop fusion | bytes 131072 | tf_op jit(solution)/shard_map/slice | solution.py:83
  28.6 3.2 %copy.160 = f32[4,16,128,1]{2,1,3,0:T(8,128)S(1)} copy(f32[4,16,128,1]{3,2,1,0:T(8,128)} %get-tuple-element.9) | data formatting | bytes 65536
  31.8 2.8 %copy.161 = f32[4,16,128,1]{2,1,3,0:T(8,128)S(1)} copy(f32[4,16,128,1]{3,2,1,0:T(8,128)} %get-tuple-element.10) | data formatting | bytes 65536
  35.3 4.1 %collective-permute-start.1 = (f32[6,16,128,1]{2,1,3,0:T(8,128)}, f32[6,16,128,1]{2,1,3,0:T(8,128)}, u32[]{:S(2)}, u32[]{:S(2)}) collective-permute-start(f32[6,16,128,1]{2,1,3,0:T(8,128)} %get-tuple-element.31), channel_id=1, source_target_pairs={{16,0},{32,16},{48,32},{64,48},{80,64},{96,80},{112,96},{0,112},{1... | collective-permute-start | bytes 147464 | tf_op jit(solution)/shard_map/ppermute | solution.py:24
  39.9 7.5 %copy.154 = f32[16,128,128]{0,2,1:T(8,128)} copy(f32[16,128,128]{1,0,2:T(8,128)S(1)} %get-tuple-element.5) | data formatting | bytes 2097152 | tf_op jit(solution)/shard_map/mul | solution.py:168
  47.4 9.6 %reduce_sum.55 = f32[16,64,64]{0,2,1:T(8,128)S(1)} reduce(f32[16,64,2,64,2]{0,4,3,2,1:T(2,128)} %bitcast.102, f32[]{:T(128)} %constant.31.clone.1), dimensions={2,4}, to_apply=%region_3.4 | reduce | flops 196608 | bytes 1310724 | tf_op jit(solution)/shard_map/reduce_sum | solution.py:58
  58.5 2.8 reduce_sum.58
  63.7 2.6 copy.145
  70.1 5.4 %slice.139 = f32[4,16,128,127]{3,2,1,0:T(8,128)} slice(f32[4,16,128,128]{3,2,1,0:T(8,128)} %param.8), slice={[0:4], [0:16], [0:128], [1:128]} | slice | bytes 8323072 | tf_op jit(solution)/shard_map/slice | solution.py:91
  75.5 2.6 slice.157
  78.2 2.7 slice.184
  82.1 3.0 %copy.155 = f32[16,8,8,64]{3,2,1,0:T(8,128)} copy(f32[16,8,8,64]{0,3,2,1:T(8,128)} %bitcast.104) | data formatting | bytes 524288 | tf_op jit(solution)/shard_map/max | solution.py:68
  95.3 2.6 copy.128
  97.8 2.6 copy.130
  101.1 2.7 copy.129
  103.8 2.7 copy.131
  110.3 3.4 %broadcast_multiply_fusion.2 = (f32[16,128,128]{1,0,2:T(8,128)}, f32[16,128,128]{1,0,2:T(8,128)}) fusion(f32[16,128,128]{1,0,2:T(8,128)S(1)} %copy-done.5, f32[16,1,128]{1,0,2:T(8,128)} %copy.144, f32[16,127,128]{1,0,2:T(8,128)} %slice.184), kind=kLoop, calls=%fused_computation.26 | loop fusion | flops 1572864 | bytes 4194304 | tf_op jit(solution)/shard_map/mul | solution.py:50
  113.7 2.7 copy.146
  116.3 2.5 copy.148
  118.9 3.2 %maximum_minimum_fusion = (f32[16,128,128]{1,0,2:T(8,128)}, f32[16,128,128]{1,0,2:T(8,128)}, f32[16,128,128]{1,0,2:T(8,128)}) fusion(f32[16,128,128]{1,0,2:T(8,128)S(1)} %get-tuple-element.6, f32[16,128,1]{1,0,2:T(8,128)S(1)} %copy-done.16, f32[16,128,127]{1,0,2:T(8,128)} %slice.168, f32[128,128]{0,1:T(8,128)S(1)} %copy.150, ...), kind=kLoop, calls=%fused_computation.14 | loop fusion | flops 1572864 | bytes 6356992 | tf_op jit(solution)/shard_map/min | solution.py:47
  122.1 2.7 copy.125
  124.8 2.5 copy.151
  128.9 9.0 %subtract_multiply_fusion.1 = (f32[4,16,128,128]{3,2,1,0:T(8,128)S(1)}, f32[4,16,128,128]{3,2,1,0:T(8,128)S(1)}) fusion(f32[4,16,128,128]{3,2,1,0:T(8,128)} %param.8, f32[4,16,128,1]{3,2,1,0:T(8,128)} %copy.129, f32[4,16,128,127]{3,2,1,0:T(8,128)} %slice.139, f32[16]{0:T(128)S(1)} %copy-done.17, f32[16,128,128]{2,1,0:T(8,128)} %copy.130, ...), kind=kLoop, calls=%fused_computation.9 | loop fusion | flops 18874368 | bytes 27263040 | tf_op jit(solution)/shard_map/mul | solution.py:49
  138.8 6.3 %broadcast_multiply_fusion = (f32[4,16,128,128]{3,2,1,0:T(8,128)}, f32[4,16,128,128]{3,2,1,0:T(8,128)}) fusion(f32[16,128,128]{2,1,0:T(8,128)S(1)} %copy-done.8, f32[4,16,128,128]{3,2,1,0:T(8,128)S(1)} %copy-done.1, f32[16,128,128]{2,1,0:T(8,128)} %copy.151, f32[4,16,128,128]{3,2,1,0:T(8,128)S(1)} %get-tuple-element.8, f32[4,16,127,128]{3,2,1,0:T(8,128)S(1)} %bitcast.101, ...), kind=kLoop, calls=%fused_computation.13 | loop fusion | flops 9437184 | bytes 31457280 | tf_op jit(solution)/shard_map/mul | solution.py:64
  145.1 18.4 %copy.153 = f32[4,16,128,128]{1,3,2,0:T(8,128)} copy(f32[4,16,128,128]{3,2,1,0:T(8,128)} %get-tuple-element.3) | data formatting | bytes 8388608 | tf_op jit(solution)/shard_map/mul | solution.py:64
  163.5 33.4 %reduce_sum.53 = f32[4,16,64,64]{1,3,2,0:T(8,128)} reduce(f32[4,16,64,2,64,2]{1,5,4,3,2,0:T(2,128)} %bitcast.97, f32[]{:T(128)} %constant.31.clone.1), dimensions={3,5}, to_apply=%region_2.3 | reduce | flops 786432 | bytes 5242884 | tf_op jit(solution)/shard_map/reduce_sum | solution.py:58
  196.9 5.6 %copy.156 = f32[4,16,8,8,64]{4,3,0,2,1:T(8,128)S(1)} copy(f32[4,16,8,8,64]{1,4,3,2,0:T(8,128)} %bitcast.98) | data formatting | bytes 2097152 | tf_op jit(solution)/shard_map/reduce_sum | solution.py:58
  206.3 9.9 %reduce_sum.56 = f32[4,16,32,32]{1,3,2,0:T(8,128)S(1)} reduce(f32[4,16,32,2,32,2]{1,5,4,3,2,0:T(2,128)} %bitcast.99, f32[]{:T(128)} %constant.31.clone.1), dimensions={3,5}, to_apply=%region_4.5 | reduce | flops 196608 | bytes 1310724 | tf_op jit(solution)/shard_map/reduce_sum | solution.py:58
  222.3 2.7 all_to_all.8
  225.0 46.7 %all_to_all.12 = f32[128,2,2560]{2,1,0:T(2,128)} all-to-all(f32[128,2,2560]{2,1,0:T(2,128)} %all_to_all.8), channel_id=1, replica_groups=mesh['lon'=8,'lat'=16] {'lon','lat'}, dimensions={0} | all-to-all | bytes 5242880 | tf_op jit(solution)/shard_map/all_to_all | solution.py:42
  271.7 3.4 %all_to_all.10 = f32[256,2560]{1,0:T(8,128)S(1)} reshape(f32[128,2,2560]{2,1,0:T(2,128)} %all_to_all.12) | data formatting | bytes 5242880 | tf_op jit(solution)/shard_map/all_to_all | solution.py:42
  (110 shorter events, 56.5 us)
Async XLA Ops:
  9.3 30.6 %copy-start.6 = (f32[16,128,128]{1,0,2:T(8,128)}, f32[16,128,128]{1,0,2:T(8,128)S(1)}, u32[]{:S(2)}) copy-start(f32[16,128,128]{1,0,2:T(8,128)S(1)} %get-tuple-element.5) | copy-start | bytes 3145732
  13.4 74.9 %collective-permute-start.2 = (f32[6,16,1,128]{3,1,2,0:T(8,128)}, f32[6,16,1,128]{3,1,2,0:T(8,128)}, u32[]{:S(2)}, u32[]{:S(2)}) collective-permute-start(f32[6,16,1,128]{3,1,2,0:T(8,128)} %get-tuple-element.32), channel_id=1, source_target_pairs={{0,1},{1,2},{2,3},{3,4},{4,5},{5,6},{6,7},{7,8},{8,9},{9,10},{10,1... | collective-permute-start | bytes 147464 | tf_op jit(solution)/shard_map/ppermute | solution.py:21
  15.3 72.7 %collective-permute-start.3 = (f32[6,16,128]{2,1,0:T(8,128)}, f32[6,16,128]{2,1,0:T(8,128)}, u32[]{:S(2)}, u32[]{:S(2)}) collective-permute-start(f32[6,16,128]{2,1,0:T(8,128)} %get-tuple-element.33), channel_id=1, source_target_pairs={{0,16},{16,0},{32,48},{48,32},{64,80},{80,64},{96,112},{112,96},{1... | collective-permute-start | bytes 147464 | tf_op jit(solution)/shard_map/ppermute | solution.py:36
  17.4 89.2 %collective-permute-start.6 = (f32[6,16,1,128]{3,1,2,0:T(8,128)}, f32[6,16,1,128]{3,1,2,0:T(8,128)}, u32[]{:S(2)}, u32[]{:S(2)}) collective-permute-start(f32[6,16,1,128]{3,1,2,0:T(8,128)} %get-tuple-element.34), channel_id=1, source_target_pairs={{1,0},{2,1},{3,2},{4,3},{5,4},{6,5},{7,6},{8,7},{9,8},{10,9},{11,1... | collective-permute-start | bytes 147464 | tf_op jit(solution)/shard_map/ppermute | solution.py:24
  28.5 6.1 %copy-start.3 = (f32[16,128,128]{1,0,2:T(8,128)}, f32[16,128,128]{1,0,2:T(8,128)S(1)}, u32[]{:S(2)}) copy-start(f32[16,128,128]{1,0,2:T(8,128)S(1)} %copy.123) | copy-start | bytes 3145732
  28.6 10.9 %copy-start.18 = (s32[128,1]{0,1:T(1,128)S(1)}, s32[128,1]{0,1:T(1,128)}, u32[]{:S(2)}) copy-start(s32[128,1]{0,1:T(1,128)} %param.15) | copy-start | bytes 1540
  35.3 55.2 %collective-permute-start = (f32[6,16,128,1]{2,1,3,0:T(8,128)}, f32[6,16,128,1]{2,1,3,0:T(8,128)}, u32[]{:S(2)}, u32[]{:S(2)}) collective-permute-start(f32[6,16,128,1]{2,1,3,0:T(8,128)} %get-tuple-element.30), channel_id=1, source_target_pairs={{0,16},{16,32},{32,48},{48,64},{64,80},{80,96},{96,112},{112,0},{1... | collective-permute-start | bytes 147464 | tf_op jit(solution)/shard_map/ppermute | solution.py:21
  35.3 49.8 %collective-permute-start.1 = (f32[6,16,128,1]{2,1,3,0:T(8,128)}, f32[6,16,128,1]{2,1,3,0:T(8,128)}, u32[]{:S(2)}, u32[]{:S(2)}) collective-permute-start(f32[6,16,128,1]{2,1,3,0:T(8,128)} %get-tuple-element.31), channel_id=1, source_target_pairs={{16,0},{32,16},{48,32},{64,48},{80,64},{96,80},{112,96},{0,112},{1... | collective-permute-start | bytes 147464 | tf_op jit(solution)/shard_map/ppermute | solution.py:24
  61.2 6.1 %copy-start.7 = (f32[16,128,128]{1,0,2:T(8,128)S(1)}, f32[16,128,128]{1,0,2:T(8,128)}, u32[]{:S(2)}) copy-start(f32[16,128,128]{1,0,2:T(8,128)} %copy-done.6) | copy-start | bytes 3145732
  70.1 5.4 %copy-start = (f32[4,16,128,128]{3,2,1,0:T(8,128)S(1)}, f32[4,16,128,128]{3,2,1,0:T(8,128)}, u32[]{:S(2)}) copy-start(f32[4,16,128,128]{3,2,1,0:T(8,128)} %param.8) | copy-start | bytes 12582916
  78.2 8.3 %copy-start.4 = (f32[16,128,128]{1,0,2:T(8,128)S(1)}, f32[16,128,128]{1,0,2:T(8,128)}, u32[]{:S(2)}) copy-start(f32[16,128,128]{1,0,2:T(8,128)} %copy-done.3) | copy-start | bytes 3145732
  78.2 8.3 %slice-start = ((f32[16,128,128]{1,0,2:T(8,128)}), f32[16,128,127]{1,0,2:T(8,128)S(1)}, s32[]{:S(2)}) async-start(f32[16,128,128]{1,0,2:T(8,128)} %copy-done.3), calls=%async_computation.1 | async-start | bytes 2080768 | tf_op jit(solution)/shard_map/slice | solution.py:91
  88.0 4.5 %collective-permute-start.4 = (f32[6,16,128]{2,1,0:T(8,128)}, f32[6,16,128]{2,1,0:T(8,128)}, u32[]{:S(2)}, u32[]{:S(2)}) collective-permute-start(f32[6,16,128]{2,1,0:T(8,128)} %collective-permute-done.3), channel_id=1, source_target_pairs={{0,32},{32,0},{16,48},{48,16},{64,96},{96,64},{80,112},{112,80},{1... | collective-permute-start | bytes 147464 | tf_op jit(solution)/shard_map/ppermute | solution.py:36
  92.4 14.0 %collective-permute-start.5 = (f32[6,16,128]{2,1,0:T(8,128)}, f32[6,16,128]{2,1,0:T(8,128)S(1)}, u32[]{:S(2)}, u32[]{:S(2)}) collective-permute-start(f32[6,16,128]{2,1,0:T(8,128)} %collective-permute-done.4), channel_id=1, source_target_pairs={{0,64},{64,0},{16,80},{80,16},{32,96},{96,32},{48,112},{112,48},{1... | collective-permute-start | bytes 147464 | tf_op jit(solution)/shard_map/ppermute | solution.py:36
  101.1 5.4 %copy-start.20 = (f32[6]{0:T(128)S(1)}, f32[6]{0:T(128)}, u32[]{:S(2)}) copy-start(f32[6]{0:T(128)} %constant.13.clone.1) | copy-start | bytes 76
  103.8 6.5 %copy-start.5 = (f32[16,128,128]{1,0,2:T(8,128)S(1)}, f32[16,128,128]{1,0,2:T(8,128)}, u32[]{:S(2)}) copy-start(f32[16,128,128]{1,0,2:T(8,128)} %copy.145) | copy-start | bytes 3145732
  107.4 8.9 %copy-start.14 = (f32[6,16,128]{2,1,0:T(8,128)}, f32[6,16,128]{2,1,0:T(8,128)S(1)}, u32[]{:S(2)}) copy-start(f32[6,16,128]{2,1,0:T(8,128)S(1)} %bitcast_select_fusion) | copy-start | bytes 147460
  110.3 8.6 %copy-start.9 = (f32[16,127,128]{1,0,2:T(8,128)S(1)}, f32[16,127,128]{1,0,2:T(8,128)}, u32[]{:S(2)}) copy-start(f32[16,127,128]{1,0,2:T(8,128)} %slice.181) | copy-start | bytes 3121156
  110.3 8.6 %copy-start.16 = (f32[16,128,1]{1,0,2:T(8,128)S(1)}, f32[16,128,1]{1,0,2:T(8,128)}, u32[]{:S(2)}) copy-start(f32[16,128,1]{1,0,2:T(8,128)} %get-tuple-element.38) | copy-start | bytes 24580
  113.7 5.2 %copy-start.11 = (f32[16,1,128]{1,0,2:T(8,128)S(1)}, f32[16,1,128]{1,0,2:T(8,128)}, u32[]{:S(2)}) copy-start(f32[16,1,128]{1,0,2:T(8,128)} %copy.141) | copy-start | bytes 24580
  122.1 5.3 %copy-start.12 = (f32[16,128,128]{1,0,2:T(8,128)S(1)}, f32[16,128,128]{1,0,2:T(8,128)}, u32[]{:S(2)}) copy-start(f32[16,128,128]{1,0,2:T(8,128)} %get-tuple-element.21) | copy-start | bytes 3145732
  122.1 6.7 %copy-start.10 = (f32[16,128,128]{2,1,0:T(8,128)S(1)}, f32[16,128,128]{2,1,0:T(8,128)}, u32[]{:S(2)}) copy-start(f32[16,128,128]{2,1,0:T(8,128)} %copy.128) | copy-start | bytes 3145732
  122.1 6.7 %slice-start.1 = ((f32[6,16,128]{2,1,0:T(8,128)}), f32[4,16,128]{2,1,0:T(8,128)S(1)}, s32[]{:S(2)}) async-start(f32[6,16,128]{2,1,0:T(8,128)} %copy-done.14), calls=%async_computation.2 | async-start | bytes 65536 | tf_op jit(solution)/shard_map/slice | solution.py:149
  122.1 6.7 %copy-start.17 = (f32[16]{0:T(128)S(1)}, f32[16]{0:T(128)}, u32[]{:S(2)}) copy-start(f32[16]{0:T(128)} %param.13) | copy-start | bytes 196
  128.8 9.0 %copy-start.1 = (f32[4,16,128,128]{3,2,1,0:T(8,128)S(1)}, f32[4,16,128,128]{3,2,1,0:T(8,128)}, u32[]{:S(2)}) copy-start(f32[4,16,128,128]{3,2,1,0:T(8,128)} %param.8) | copy-start | bytes 12582916
  128.8 9.8 %copy-start.2 = (f32[4,16,128,1]{3,2,1,0:T(8,128)S(1)}, f32[4,16,128,1]{3,2,1,0:T(8,128)}, u32[]{:S(2)}) copy-start(f32[4,16,128,1]{3,2,1,0:T(8,128)} %copy.131) | copy-start | bytes 98308
  128.8 10.0 %copy-start.8 = (f32[16,128,128]{2,1,0:T(8,128)S(1)}, f32[16,128,128]{2,1,0:T(8,128)}, u32[]{:S(2)}) copy-start(f32[16,128,128]{2,1,0:T(8,128)} %copy.152) | copy-start | bytes 3145732
  128.8 10.0 %copy-start.15 = (f32[4,16,1,128]{3,1,2,0:T(8,128)S(1)}, f32[4,16,1,128]{3,1,2,0:T(8,128)}, u32[]{:S(2)}) copy-start(f32[4,16,1,128]{3,1,2,0:T(8,128)} %subtract_multiply_fusion.2) | copy-start | bytes 98308
  196.9 5.6 %copy-start.13 = (f32[16,8,8,64]{3,2,1,0:T(8,128)S(1)}, f32[16,8,8,64]{3,2,1,0:T(8,128)}, u32[]{:S(2)}) copy-start(f32[16,8,8,64]{3,2,1,0:T(8,128)} %copy.155) | copy-start | bytes 786436
  216.2 4.3 %copy-start.19 = (s32[128]{0:T(128)S(1)}, s32[128]{0:T(128)}, u32[]{:S(2)}) copy-start(s32[128]{0:T(128)} %fusion.13) | copy-start | bytes 1540
where the time goes:
time: 280 us; the launch traced here: 277 us
  local copies, waits for them, and re-layouts  123 us (44%)
  other arithmetic  92.7 us (33%)
  blocking collectives  46.7 us (17%)
  starting transfers between devices  11.8 us (4%)
    reduce_sum x4, other arithmetic, pool_pairs(): field.reshape(old_shape[:-2] + (old_shape[-2] // 2, 2, old_shape[-1] // 2...  55.6 us
    all_to_all x1, blocking collectives, sent_together(): lax.all_to_all(both, axis, split_axis=split_dim, concat_axis=concat_dim,...  46.7 us
    mul x1, local copies, waits for them, and re-layouts, coarsen(): weighted = pool_pairs(updated * weight[None])  18.4 us
    unnamed x49, local copies, waits for them, and re-layouts  16.7 us
    mul x3, other arithmetic, face_flux(): open_depth * (0.5 * face_speed * (lower_val + upper_val) - 0.5 * jnp.abs(...  11.3 us
    mul x2, local copies, waits for them, and re-layouts, local(): coarse_two, coarse_four = coarsen(updated, cell_area[None] * wet_depth)  8.88 us
    slice x3, local copies, waits for them, and re-layouts, column_edges(): return jnp.concatenate([field[..., :1], field[..., -1:]], axis=-1)  8.16 us
    reduce_sum x2, local copies, waits for them, and re-layouts, pool_pairs(): field.reshape(old_shape[:-2] + (old_shape[-2] // 2, 2, old_shape[-1] // 2...  7.18 us
  transfers between devices with their start and end apart: 7, of which 1 were waited for; matrix products, arithmetic and copies ran while one was open for 29% of the time, Pallas kernels for 0%

commit v1 on v0

v1 whole, which is shorter than its diff:
```python
import jax
import jax.numpy as jnp
from jax import lax
from jax.experimental import pallas as pl
from jax.experimental.pallas import tpu as pltpu
from jax.sharding import PartitionSpec as P

time_step = 0.05
depth_floor = 0.25
weight_floor = 0.25

TR, LV = 4, 16
ROWS, LANES = 128, 128
GROUPS = 8
DEV, CAP = 128, 2
CHUNKS = 20
F32, BF16 = jnp.float32, jnp.bfloat16
MIB = 1 << 20


def lane_iota(shape=(8, 128)):
    return lax.broadcasted_iota(jnp.int32, shape, len(shape) - 1)


def sub_iota(shape=(8, 128)):
    return lax.broadcasted_iota(jnp.int32, shape, len(shape) - 2)


def face(lower_h, upper_h, lower_speed, upper_speed, mixing):
    open_depth = jnp.minimum(lower_h, upper_h)
    speed = 0.5 * (lower_speed + upper_speed)
    ahead = jnp.maximum(speed, 0.0)
    back = ahead - speed
    return open_depth * (ahead + mixing), open_depth * (back + mixing)


def split_dot(left, right, split_left=True):
    values = left if split_left else right
    high = values.astype(BF16)
    low = (values - high.astype(F32)).astype(BF16)
    if split_left:
        return jnp.dot(high, right, preferred_element_type=F32) + jnp.dot(
            low, right, preferred_element_type=F32
        )
    return jnp.dot(left, high, preferred_element_type=F32) + jnp.dot(
        left, low, preferred_element_type=F32
    )


def input_copies(hbm, vmem, sems):
    per = LV // GROUPS

    def copies(group):
        levels = pl.ds(group * per, per)
        out = [pltpu.make_async_copy(hbm[0].at[:, levels], vmem[0].at[:, levels], sems.at[0, group])]
        for n in range(1, 5):
            out.append(
                pltpu.make_async_copy(hbm[n].at[levels], vmem[n].at[levels], sems.at[n, group])
            )
        return out

    return copies


def strided(ref, *lead, i):
    return ref[(*lead, pl.ds(i, 8, stride=16), slice(None))]


def level_coefficients(k, mixing, refs, area_ref, coef, visit):
    fill, mask, east, north = refs
    lane, sub = lane_iota(), sub_iota()

    def depth(i):
        return strided(fill, k, i=i) * strided(mask, k, i=i).astype(F32)

    h_first, v_first = depth(0), strided(north, k, i=0)
    h, v = h_first, v_first
    for i in range(16):
        if i < 15:
            h_next, v_next = depth(i + 1), strided(north, k, i=i + 1)
        else:
            h_next, v_next = pltpu.roll(h_first, 7, 0), pltpu.roll(v_first, 7, 0)
        u = strided(east, k, i=i)
        p_e, q_e = face(h, pltpu.roll(h, 127, 1), u, pltpu.roll(u, 127, 1), mixing)
        coef[0, i] = jnp.where(lane < 127, p_e, 0.0)
        coef[1, i] = jnp.where(lane < 127, q_e, 0.0)
        p_n, q_n = face(h, h_next, v, v_next, mixing)
        if i == 15:
            p_n, q_n = jnp.where(sub < 7, p_n, 0.0), jnp.where(sub < 7, q_n, 0.0)
        coef[2, i] = p_n
        coef[3, i] = q_n
        visit(i, h, u, v, strided(area_ref, i=i))
        h, v = h_next, v_next


def interior(k, tracers, coef, visit):
    p15, q15 = coef[2, 15], coef[3, 15]
    cells, south, last = [], [], []
    for t in range(TR):
        first = strided(tracers, t, k, i=0)
        top = strided(tracers, t, k, i=15)
        flux = p15 * top - q15 * pltpu.roll(first, 7, 0)
        cells.append(first)
        last.append(flux)
        south.append(pltpu.roll(flux, 1, 0))
    for i in range(16):
        p_e, q_e = coef[0, i], coef[1, i]
        if i < 15:
            p_n, q_n = coef[2, i], coef[3, i]
        divs, after = [], []
        for t in range(TR):
            cell = cells[t]
            if i < 15:
                nxt = strided(tracers, t, k, i=i + 1)
                north = p_n * cell - q_n * nxt
                after.append(nxt)
            else:
                north = last[t]
            east = p_e * cell - q_e * pltpu.roll(cell, 127, 1)
            divs.append((pltpu.roll(east, 1, 1) - east) + (south[t] - north))
            south[t] = north
        visit(i, cells, divs)
        cells = after


def kernel_first(
    tr, fill, mask, east, north, diff, area, owner,
    sums, weights, ew, ns, placing,
    tr_s, fill_s, mask_s, east_s, north_s, area_s, coef, sems, area_sem,
):
    hbm, vmem = (tr, fill, mask, east, north), (tr_s, fill_s, mask_s, east_s, north_s)
    copies = input_copies(hbm, vmem, sems)
    area_copy = pltpu.make_async_copy(area, area_s, area_sem)
    for group in range(GROUPS):
        for copy in copies(group):
            copy.start()
        if group == 0:
            area_copy.start()
    flip = jnp.where(lax.axis_index("lon") < lax.axis_size("lon") // 2, 0, 1)

    across = lane_iota((DEV, DEV))
    down = sub_iota((DEV, DEV))
    who_row = owner[...]
    who = jnp.sum(jnp.where(down == across, who_row, 0), axis=1, keepdims=True)
    same = jnp.where((who == who_row) & (down < across), 1, 0)
    rank = jnp.sum(same, axis=0, keepdims=True)
    row_of = who_row * CAP + rank
    for part in range(CAP):
        here = jnp.where(down + part * DEV == row_of, 1.0, 0.0).astype(BF16)
        placing[pl.ds(part * DEV, DEV), 0:DEV] = here
        placing[pl.ds(part * DEV, DEV), DEV : 2 * DEV] = here

    area_copy.wait()
    lane = lane_iota()
    per = LV // GROUPS

    def level(k):
        mixing = diff[k]
        rows = pl.ds(pl.multiple_of(k * 8, 8), 8)
        pending = {}

        def seen(i, h, u, v, cell_area):
            w = cell_area * h
            coef[4, i] = w
            coef[5, i] = (time_step * h) / jnp.maximum(h, depth_floor)
            base = 64 * (i % 2)
            packed = ew[16 + i // 2]
            packed = jnp.where(
                (lane >> 1) == k + base // 2, pltpu.roll(h, 2 * k + 1 + base, 1), packed
            )
            packed = jnp.where(
                (lane >> 1) == k + 16 + base // 2, pltpu.roll(u, 2 * k + 33 + base, 1), packed
            )
            ew[16 + i // 2] = packed
            if i == 0:
                ns[1 - flip, pl.ds(64 + k, 1), :] = h[0:1]
                ns[1 - flip, pl.ds(80 + k, 1), :] = v[0:1]
            if i == 15:
                ns[flip, pl.ds(64 + k, 1), :] = h[7:8]
                ns[flip, pl.ds(80 + k, 1), :] = v[7:8]
            if i % 2 == 0:
                pending["w"] = w
            else:
                weights[i // 2, rows, :] = pending["w"] + w

        level_coefficients(k, mixing, (fill_s, mask_s, east_s, north_s), area_s, coef, seen)
        where_t = [(lane >> 1) == t * 16 + k for t in range(TR)]

        def done(i, cells, divs):
            w, g = coef[4, i], coef[5, i]
            packed = ew[i]
            for t in range(TR):
                cell = cells[t]
                packed = jnp.where(where_t[t], pltpu.roll(cell, 2 * k + 32 * t + 1, 1), packed)
                value = w * cell + g * divs[t]
                if i == 0:
                    ns[1 - flip, pl.ds(t * 16 + k, 1), :] = cell[0:1]
                if i == 15:
                    ns[flip, pl.ds(t * 16 + k, 1), :] = cell[7:8]
                if i % 2 == 0:
                    pending[t] = value
                else:
                    sums[t, i // 2, rows, :] = pending[t] + value
            ew[i] = packed

        interior(k, tr_s, coef, done)

    def group_body(group, carry):
        for copy in copies(group):
            copy.wait()
        for n in range(per):
            level(group * per + n)
        return carry

    lax.fori_loop(0, GROUPS, group_body, 0)


def kernel_first_call(tracers, fill, mask, east, north, diff, area, owner):
    any_spec = pl.BlockSpec(memory_space=pltpu.HBM)
    vmem = pl.BlockSpec(memory_space=pltpu.VMEM)
    return pl.pallas_call(
        kernel_first,
        name="first",
        out_shape=(
            jax.ShapeDtypeStruct((TR, 8, 128, 128), F32),
            jax.ShapeDtypeStruct((8, 128, 128), F32),
            jax.ShapeDtypeStruct((24, 8, 128), F32),
            jax.ShapeDtypeStruct((2, 96, 128), F32),
            jax.ShapeDtypeStruct((CAP * DEV, 2 * DEV), BF16),
        ),
        in_specs=[any_spec] * 5
        + [pl.BlockSpec(memory_space=pltpu.SMEM), any_spec, vmem],
        out_specs=(vmem,) * 5,
        scratch_shapes=[
            pltpu.VMEM((TR, LV, ROWS, LANES), F32),
            pltpu.VMEM((LV, ROWS, LANES), F32),
            pltpu.VMEM((LV, ROWS, LANES), jnp.int32),
            pltpu.VMEM((LV, ROWS, LANES), F32),
            pltpu.VMEM((LV, ROWS, LANES), F32),
            pltpu.VMEM((ROWS, LANES), F32),
            pltpu.VMEM((6, 16, 8, 128), F32),
            pltpu.SemaphoreType.DMA((5, GROUPS)),
            pltpu.SemaphoreType.DMA,
        ],
        compiler_params=pltpu.CompilerParams(vmem_limit_bytes=24 * MIB),
        cost_estimate=pl.CostEstimate(flops=60_000_000, bytes_accessed=11 * MIB, transcendentals=0),
    )(tracers, fill, mask, east, north, diff, area, owner)


def spread(values, offset):
    index = (lane_iota() & 31) + offset
    return jnp.take_along_axis(values, index, axis=1)


def kernel_second(
    sums, weights, ew, from_east, from_west, ns, got_fwd, got_bwd, diff, placing,
    send, d_ew, d_ns,
    work, acc, chunks,
):
    lane, sub = lane_iota(), sub_iota()
    flip = jnp.where(lax.axis_index("lon") < lax.axis_size("lon") // 2, 0, 1)
    at_fold = lax.axis_index("lat") == lax.axis_size("lat") - 1
    is_east = (lane & 1) == 0
    level_of = (lane >> 1) & 15
    mixing = jnp.zeros((8, 128), F32)
    for k in range(LV):
        mixing = jnp.where(level_of == k, diff[k], mixing)

    def neighbour(n):
        return jnp.where(
            is_east, pltpu.roll(from_east[n], 127, 1), pltpu.roll(from_west[n], 1, 1)
        )

    pending = None
    for i in range(16):
        own_hu, near_hu = ew[16 + i // 2], neighbour(16 + i // 2)
        base = 64 * (i % 2)
        h = spread(own_hu, base)
        p, q = face(
            h, spread(near_hu, base), spread(own_hu, base + 32), spread(near_hu, base + 32), mixing
        )
        div = jnp.where(is_east, q, p) * neighbour(i) - jnp.where(is_east, p, q) * ew[i]
        d_ew[i] = div
        value = (time_step * h) / jnp.maximum(h, depth_floor) * div
        if i % 2 == 0:
            pending = value
        else:
            work[i // 2] = pending + value

    ends = (lane == 0) | (lane == 127)

    def add_ends(k, carry):
        rows = pl.ds(pl.multiple_of(k * 8, 8), 8)
        for t in range(TR):
            for pair in range(8):
                at = (t, pair, rows, slice(None))
                moved = pltpu.roll(work[pair], 127 - 2 * k + (128 - 32 * t), 1)
                acc[at] = sums[at] + jnp.where(ends, moved, 0.0)
        return carry

    lax.fori_loop(0, LV, add_ends, 0)

    back = 127 - lane
    for half in range(2):
        rows = pl.ds(8 * half, 8)
        levels = sub + 8 * half
        mix = jnp.zeros((8, 128), F32)
        for k in range(8):
            mix = jnp.where(sub == k, diff[8 * half + k], mix)

        def far(ref, n, sign=None):
            value = ref[pl.ds(n * 16 + 8 * half, 8), :]
            turned = jnp.take_along_axis(value, back, axis=1)
            if sign is not None:
                turned = -turned
            return jnp.where(at_fold, turned, value)

        for side in range(2):
            own = lambda n: ns[flip if side == 0 else 1 - flip, pl.ds(n * 16 + 8 * half, 8), :]
            if side == 0:
                near = lambda n, sign=None: jnp.where(
                    flip == 1, far(got_fwd, n, sign), far(got_bwd, n, sign)
                )
            else:
                near = lambda n, sign=None: jnp.where(
                    flip == 1,
                    got_bwd[pl.ds(n * 16 + 8 * half, 8), :],
                    got_fwd[pl.ds(n * 16 + 8 * half, 8), :],
                )
            h = own(4)
            p, q = face(h, near(4), own(5), near(5, -1), mix)
            gain = (time_step * h) / jnp.maximum(h, depth_floor)
            for t in range(TR):
                if side == 0:
                    div = q * near(t) - p * own(t)
                    at = (t, 7, pl.ds(64 * half + 7, 8, stride=8), slice(None))
                else:
                    div = p * near(t) - q * own(t)
                    at = (t, 0, pl.ds(64 * half, 8, stride=8), slice(None))
                d_ns[side, pl.ds(t * 16 + 8 * half, 8), :] = div
                acc[at] = acc[at] + gain * div

    source = sub_iota((256, 128))
    target = lane_iota((256, 128))
    pool = jnp.where(target == (source >> 7) * 64 + ((source & 127) >> 1), 1.0, 0.0).astype(BF16)
    source = sub_iota((128, 128))
    target = lane_iota((128, 128))
    quarter = [
        jnp.where(target == j * 32 + ((source & 63) >> 1), 1.0, 0.0).astype(BF16) for j in range(4)
    ]

    def both_rows(ref, *lead, j):
        return jnp.concatenate([ref[(*lead, 2 * j)], ref[(*lead, 2 * j + 1)]], axis=1)

    def keep(n, values):
        high = values.astype(BF16)
        chunks[0:128, pl.ds(n * 128, 128)] = high
        chunks[128:256, pl.ds(n * 128, 128)] = (values - high.astype(F32)).astype(BF16)

    gains = []
    den4 = jnp.zeros((128, 128), F32)
    for j in range(4):
        den2 = split_dot(both_rows(weights, j=j), pool)
        gains.append(1.0 / jnp.maximum(den2, weight_floor))
        den4 = den4 + split_dot(den2, quarter[j])
    gain4 = 1.0 / jnp.maximum(den4, weight_floor)
    for t in range(TR):
        num4 = jnp.zeros((128, 128), F32)
        for j in range(4):
            num2 = split_dot(both_rows(acc, t, j=j), pool)
            keep(t * 4 + j, num2 * gains[j])
            num4 = num4 + split_dot(num2, quarter[j])
        keep(16 + t, num4 * gain4)

    for n in range(CHUNKS // 2):
        placed = jnp.dot(
            placing[...], chunks[:, pl.ds(n * 256, 256)], preferred_element_type=F32
        )
        for part in range(2):
            for m in range(32):
                send[pl.ds(m * 8 * CHUNKS + 2 * n + part, 8, stride=CHUNKS), :] = placed[
                    m * 8 : m * 8 + 8, part * 128 : part * 128 + 128
                ]


def kernel_second_call(*args):
    vmem = pl.BlockSpec(memory_space=pltpu.VMEM)
    return pl.pallas_call(
        kernel_second,
        name="second",
        out_shape=(
            jax.ShapeDtypeStruct((DEV * CAP * CHUNKS, 128), F32),
            jax.ShapeDtypeStruct((16, 8, 128), F32),
            jax.ShapeDtypeStruct((2, 64, 128), F32),
        ),
        in_specs=[vmem] * 8 + [pl.BlockSpec(memory_space=pltpu.SMEM), vmem],
        out_specs=(vmem,) * 3,
        scratch_shapes=[
            pltpu.VMEM((8, 8, 128), F32),
            pltpu.VMEM((TR, 8, 128, 128), F32),
            pltpu.VMEM((256, 2560), BF16),
        ],
        compiler_params=pltpu.CompilerParams(vmem_limit_bytes=16 * MIB),
        cost_estimate=pl.CostEstimate(flops=60_000_000, bytes_accessed=6 * MIB, transcendentals=0),
    )(*args)


def kernel_third(
    tr, fill, mask, east, north, diff, area, d_ew, d_ns,
    out,
    tr_s, fill_s, mask_s, east_s, north_s, area_s, out_s, coef, sems, area_sem, out_sems,
):
    hbm, vmem = (tr, fill, mask, east, north), (tr_s, fill_s, mask_s, east_s, north_s)
    copies = input_copies(hbm, vmem, sems)
    area_copy = pltpu.make_async_copy(area, area_s, area_sem)
    for group in range(GROUPS):
        for copy in copies(group):
            copy.start()
        if group == 0:
            area_copy.start()
    area_copy.wait()
    lane, sub = lane_iota(), sub_iota()
    ends = (lane == 0) | (lane == 127)
    per = LV // GROUPS

    def out_copy(group):
        levels = pl.ds(group * per, per)
        return pltpu.make_async_copy(out_s.at[:, levels], out.at[:, levels], out_sems.at[group])

    def level(k):
        mixing = diff[k]

        def seen(i, h, u, v, cell_area):
            coef[4, i] = time_step / (cell_area * jnp.maximum(h, depth_floor))

        level_coefficients(k, mixing, (fill_s, mask_s, east_s, north_s), area_s, coef, seen)

        def done(i, cells, divs):
            rate = coef[4, i]
            edge = d_ew[i]
            for t in range(TR):
                moved = pltpu.roll(edge, 127 - 2 * k + (128 - 32 * t), 1)
                div = divs[t] + jnp.where(ends, moved, 0.0)
                if i == 0:
                    div = div + jnp.where(sub == 0, d_ns[1, pl.ds(t * 16 + k, 1), :], 0.0)
                if i == 15:
                    div = div + jnp.where(sub == 7, d_ns[0, pl.ds(t * 16 + k, 1), :], 0.0)
                out_s[t, k, pl.ds(i, 8, stride=16), :] = cells[t] + rate * div

        interior(k, tr_s, coef, done)

    def group_body(group, carry):
        for copy in copies(group):
            copy.wait()
        for n in range(per):
            level(group * per + n)
        out_copy(group).start()
        return carry

    lax.fori_loop(0, GROUPS, group_body, 0)
    for group in range(GROUPS):
        out_copy(group).wait()


def kernel_third_call(tracers, fill, mask, east, north, diff, area, d_ew, d_ns):
    any_spec = pl.BlockSpec(memory_space=pltpu.HBM)
    vmem = pl.BlockSpec(memory_space=pltpu.VMEM)
    return pl.pallas_call(
        kernel_third,
        name="third",
        out_shape=jax.ShapeDtypeStruct((TR, LV, ROWS, LANES), F32),
        in_specs=[any_spec] * 5
        + [pl.BlockSpec(memory_space=pltpu.SMEM), any_spec, vmem, vmem],
        out_specs=any_spec,
        scratch_shapes=[
            pltpu.VMEM((TR, LV, ROWS, LANES), F32),
            pltpu.VMEM((LV, ROWS, LANES), F32),
            pltpu.VMEM((LV, ROWS, LANES), jnp.int32),
            pltpu.VMEM((LV, ROWS, LANES), F32),
            pltpu.VMEM((LV, ROWS, LANES), F32),
            pltpu.VMEM((ROWS, LANES), F32),
            pltpu.VMEM((TR, LV, ROWS, LANES), F32),
            pltpu.VMEM((5, 16, 8, 128), F32),
            pltpu.SemaphoreType.DMA((5, GROUPS)),
            pltpu.SemaphoreType.DMA,
            pltpu.SemaphoreType.DMA((GROUPS,)),
        ],
        compiler_params=pltpu.CompilerParams(vmem_limit_bytes=24 * MIB),
        cost_estimate=pl.CostEstimate(flops=60_000_000, bytes_accessed=12 * MIB, transcendentals=0),
    )(tracers, fill, mask, east, north, diff, area, d_ew, d_ns)


SPLITS = 4


def kernel_last(got, two, four):
    for m in range(32 // SPLITS):
        for n in range(CHUNKS):
            value = got[pl.ds(m * 8 * CHUNKS + n, 8, stride=CHUNKS), :]
            if n < 16:
                two[pl.ds(m * 8, 8), pl.ds(n * 128, 128)] = value
            else:
                four[pl.ds(m * 8, 8), pl.ds((n - 16) * 128, 128)] = value


def kernel_last_call(got):
    return pl.pallas_call(
        kernel_last,
        name="last",
        grid=(SPLITS,),
        out_shape=(
            jax.ShapeDtypeStruct((DEV * CAP, 2048), F32),
            jax.ShapeDtypeStruct((DEV * CAP, 512), F32),
        ),
        in_specs=[pl.BlockSpec((DEV * 40 // SPLITS, 128), lambda s: (s, 0))],
        out_specs=(
            pl.BlockSpec((DEV * CAP // SPLITS, 2048), lambda s: (s, 0)),
            pl.BlockSpec((DEV * CAP // SPLITS, 512), lambda s: (s, 0)),
        ),
        compiler_params=pltpu.CompilerParams(vmem_limit_bytes=8 * MIB),
    )(got)


def local(
    tracers, fill_fraction, ocean_mask, east_speed, north_speed, diffusivity, cell_area, owner_map
):
    lon_count = lax.axis_size("lon")
    lat_count = lax.axis_size("lat")
    *fields, diffusivity, cell_area = (
        pltpu.with_memory_space_constraint(x, pltpu.HBM)
        for x in (
            tracers, fill_fraction, ocean_mask, east_speed, north_speed, diffusivity, cell_area
        )
    )
    sums, weights, ew, ns, placing = kernel_first_call(
        *fields, diffusivity, cell_area, owner_map.reshape(1, DEV)
    )
    ring = [(i, (i + 1) % lon_count) for i in range(lon_count)]
    from_west = lax.ppermute(ew, "lon", ring)
    from_east = lax.ppermute(ew, "lon", [(b, a) for a, b in ring])
    chain = []
    for low in range(lon_count // 2):
        high = lon_count - 1 - low
        up = [low * lat_count + a for a in range(lat_count)]
        path = up + [high * lat_count + a for a in reversed(range(lat_count))]
        chain += list(zip(path[:-1], path[1:]))
    both = ("lon", "lat")
    got_fwd = lax.ppermute(ns[0], both, chain)
    got_bwd = lax.ppermute(ns[1], both, [(b, a) for a, b in chain])
    send, d_ew, d_ns = kernel_second_call(
        sums, weights, ew, from_east, from_west, ns, got_fwd, got_bwd, diffusivity, placing
    )
    got = lax.all_to_all(
        send.reshape(DEV, CAP * CHUNKS, 128), both, split_axis=0, concat_axis=0, tiled=True
    )
    updated = kernel_third_call(*fields, diffusivity, cell_area, d_ew, d_ns)
    two, four = kernel_last_call(got.reshape(DEV * CAP * CHUNKS, 128))
    return (updated, two[None], four[None])


def solution(mesh):
    in_specs = (
        P(None, None, "lat", "lon"),
        P(None, "lat", "lon"),
        P(None, "lat", "lon"),
        P(None, "lat", "lon"),
        P(None, "lat", "lon"),
        P(),
        P("lat", "lon"),
        P(("lon", "lat"), None),
    )
    out_specs = (
        P(None, None, "lat", "lon"),
        P(("lon", "lat"), None, None),
        P(("lon", "lat"), None, None),
    )
    return jax.shard_map(local, mesh=mesh, in_specs=in_specs, out_specs=out_specs, check_vma=False)
```

time: 280 us -> 80.9 us (0.29)
  local copies, waits for them, and re-layouts: 123 us -> 2.17 us
  other arithmetic: 92.7 us -> 0 us
  blocking collectives: 46.7 us -> 0 us
  Pallas kernels: 0 us -> 30 us
  waiting for transfers between devices: 1.21 us -> 24.6 us
  starting transfers between devices: 11.8 us -> 23.1 us
    reduce_sum x5 -> x0, other arithmetic: 55.8 us -> none  [the longest x4 55.6 us: pool_pairs(): field.reshape(old_shape[:-2] + (old_shape[-2] // 2, 2, old_shape[-1] // 2...]
    all_to_all x1 -> x0, blocking collectives: 46.7 us -> none  [sent_together(): lax.all_to_all(both, axis, split_axis=split_dim, concat_axis=concat_dim,...]
    mul x9 -> x0, local copies, waits for them, and re-layouts: 42.8 us -> none  [the longest x1 18.4 us: coarsen(): weighted = pool_pairs(updated * weight[None])]
    slice x21 -> x0, local copies, waits for them, and re-layouts: 31.4 us -> none  [the longest x3 8.16 us: column_edges(): return jnp.concatenate([field[..., :1], field[..., -1:]], axis=-1)]
    pallas_call x0 -> x4, Pallas kernels: none -> 30 us  [the longest x1 12 us: kernel_third_call(): pl.pallas_call(kernel_third, name='third', out_shape=jax.ShapeDtypeStruct...]
    mul x9 -> x0, other arithmetic: 25.3 us -> none  [the longest x3 11.3 us: face_flux(): open_depth * (0.5 * face_speed * (lower_val + upper_val) - 0.5 * jnp.abs(...]
    all_to_all x0 -> x1, waiting for transfers between devices: none -> 23.7 us  [local(): lax.all_to_all(send.reshape(DEV, CAP * CHUNKS, 128), both, split_axis=0,...]
    all_to_all x0 -> x1, starting transfers between devices: none -> 14.6 us  [local(): lax.all_to_all(send.reshape(DEV, CAP * CHUNKS, 128), both, split_axis=0,...]
  transfers between devices with their start and end apart: 7 -> 5, of which waited for: 1 -> 2; matrix products, arithmetic and copies ran while one was open for 29% -> 0% of each run, Pallas kernels for 0% -> 15%
where the time goes in v1:
time: 80.9 us; the launch traced here: 80.7 us
  Pallas kernels  30 us (37%)
  waiting for transfers between devices  24.6 us (30%)
  starting transfers between devices  23.1 us (29%)
  local copies, waits for them, and re-layouts  2.17 us (3%)
    all_to_all x1, waiting for transfers between devices, local(): lax.all_to_all(send.reshape(DEV, CAP * CHUNKS, 128), both, split_axis=0,...  23.7 us
    all_to_all x1, starting transfers between devices, local(): lax.all_to_all(send.reshape(DEV, CAP * CHUNKS, 128), both, split_axis=0,...  14.6 us
    pallas_call x1, Pallas kernels, kernel_third_call(): pl.pallas_call(kernel_third, name='third', out_shape=jax.ShapeDtypeStruct...  12 us
    pallas_call x1, Pallas kernels, kernel_first_call(): pl.pallas_call(kernel_first, name='first', out_shape=(jax.ShapeDtypeStruc...  10.5 us
    pallas_call x1, Pallas kernels, kernel_second_call(): pl.pallas_call(kernel_second, name='second', out_shape=(jax.ShapeDtypeStr...  5.65 us
    ppermute x1, starting transfers between devices, local(): got_fwd = lax.ppermute(ns[0], both, chain)  3.03 us
    ppermute x1, starting transfers between devices, local(): from_east = lax.ppermute(ew, 'lon', [(b, a) for a, b in ring])  2.53 us
    unnamed x4, local copies, waits for them, and re-layouts  2.16 us
  transfers between devices with their start and end apart: 5, of which 2 were waited for; matrix products, arithmetic and copies ran while one was open for 0% of the time, Pallas kernels for 15%

profile of v1, /device:TPU:0, one launch (start us, length us, event | category | flops | bytes accessed | tf_op | source)
XLA Modules:
  0.0 80.7 jit_solution(5638965724120714886)
XLA Ops:
  0.6 0.0 copy-start.1
  0.6 0.6 copy-done.1
  1.3 10.5 %first.1 = (f32[4,8,128,128]{3,2,1,0:T(8,128)S(1)}, f32[8,128,128]{2,1,0:T(8,128)S(1)}, f32[24,8,128]{2,1,0:T(8,128)S(1)}, f32[2,96,128]{2,1,0:T(8,128)S(1)}, bf16[256,256]{1,0:T(8,128)(2,1)S(1)}) custom-call(f32[4,16,128,128]{3,2,1,0:T(8,128)} %tr.3, f32[16,128,128]{2,1,0:T(8,128)} %fill.3, s32[16,128,128]{2,1,0:T(8,128)} %mask.3, f32[16,128,128]{2,1,0:T(8,128)} %east.3, ...), custom_call_target="tpu_custom_call" | custom-call | flops 60000000 | bytes 11534336 | tf_op jit(solution)/shard_map/first/pallas_call | solution.py:221
  11.8 1.7 %collective-permute-start.1 = (f32[24,8,128]{2,1,0:T(8,128)S(1)}, f32[24,8,128]{2,1,0:T(8,128)S(1)}, u32[]{:S(2)}, u32[]{:S(2)}) collective-permute-start(f32[24,8,128]{2,1,0:T(8,128)S(1)} %get-tuple-element.15.ew), channel_id=1, source_target_pairs={{0,16},{16,32},{32,48},{48,64},{64,80},{80,96},{96,112},{112,0},{1... | collective-permute-start | bytes 294920 | tf_op jit(solution)/shard_map/ppermute | solution.py:539
  13.4 2.5 %collective-permute-start = (f32[24,8,128]{2,1,0:T(8,128)S(1)}, f32[24,8,128]{2,1,0:T(8,128)S(1)}, u32[]{:S(2)}, u32[]{:S(2)}) collective-permute-start(f32[24,8,128]{2,1,0:T(8,128)S(1)} %get-tuple-element.15.ew), channel_id=1, source_target_pairs={{16,0},{32,16},{48,32},{64,48},{80,64},{96,80},{112,96},{0,112},{1... | collective-permute-start | bytes 294920 | tf_op jit(solution)/shard_map/ppermute | solution.py:540
  16.0 1.3 %collective-permute-start.3 = (f32[96,128]{1,0:T(8,128)S(1)}, f32[96,128]{1,0:T(8,128)S(1)}, u32[]{:S(2)}, u32[]{:S(2)}) collective-permute-start(f32[96,128]{1,0:T(8,128)S(1)} %get-tuple-element.23), channel_id=1, source_target_pairs={{1,0},{2,1},{3,2},{4,3},{5,4},{6,5},{7,6},{8,7},{9,8},{10,9},{11,1... | collective-permute-start | bytes 147464 | tf_op jit(solution)/shard_map/ppermute | solution.py:549
  17.3 3.0 %collective-permute-start.2 = (f32[96,128]{1,0:T(8,128)S(1)}, f32[96,128]{1,0:T(8,128)S(1)}, u32[]{:S(2)}, u32[]{:S(2)}) collective-permute-start(f32[96,128]{1,0:T(8,128)S(1)} %get-tuple-element.24), channel_id=1, source_target_pairs={{0,1},{1,2},{2,3},{3,4},{4,5},{5,6},{6,7},{7,8},{8,9},{9,10},{10,1... | collective-permute-start | bytes 147464 | tf_op jit(solution)/shard_map/ppermute | solution.py:548
  20.3 0.0 collective-permute-done.3.got_bwd
  20.3 0.9 %collective-permute-done.2.got_fwd = f32[96,128]{1,0:T(8,128)S(1)} collective-permute-done((f32[96,128]{1,0:T(8,128)S(1)}, f32[96,128]{1,0:T(8,128)S(1)}, u32[]{:S(2)}, u32[]{:S(2)}) %collective-permute-start.2) | collective-permute-done | bytes 49184 | tf_op jit(solution)/shard_map/ppermute | solution.py:548
  21.2 0.0 collective-permute-done.1.from_west
  21.2 0.0 collective-permute-done.from_east
  21.2 5.6 %second.1 = (f32[5120,128]{1,0:T(8,128)S(1)}, f32[16,8,128]{2,1,0:T(8,128)S(1)}, f32[2,64,128]{2,1,0:T(8,128)S(1)}) custom-call(f32[4,8,128,128]{3,2,1,0:T(8,128)S(1)} %get-tuple-element.13.sums, f32[8,128,128]{2,1,0:T(8,128)S(1)} %get-tuple-element.14.weights, f32[24,8,128]{2,1,0:T(8,128)S(1)} %get-tuple-element.15.ew, ...), custom_call_target="tpu_custom_call" | custom-call | flops 60000000 | bytes 6291456 | tf_op jit(solution)/shard_map/second/pallas_call | solution.py:388
  26.8 0.0 copy-start
  26.8 1.5 %copy-done = f32[5120,128]{1,0:T(8,128)} copy-done((f32[5120,128]{1,0:T(8,128)}, f32[5120,128]{1,0:T(8,128)S(1)}, u32[]{:S(2)}) %copy-start) | copy-done | bytes 2621464
  28.4 14.6 %all-to-all-start = ((f32[128,40,128]{2,1,0:T(8,128)}), f32[128,40,128]{2,1,0:T(8,128)S(1)}, u32[]{:S(2)}, u32[]{:S(2)}) async-start(f32[128,40,128]{2,1,0:T(8,128)} %bitcast.10), calls=%async_computation | async-start | bytes 5242880 | tf_op jit(solution)/shard_map/all_to_all | solution.py:553
  43.0 12.0 %third.1 = f32[4,16,128,128]{3,2,1,0:T(8,128)} custom-call(f32[4,16,128,128]{3,2,1,0:T(8,128)} %tr.3, f32[16,128,128]{2,1,0:T(8,128)} %fill.3, s32[16,128,128]{2,1,0:T(8,128)} %mask.3, f32[16,128,128]{2,1,0:T(8,128)} %east.3, f32[16,128,128]{2,1,0:T(8,128)} %north.3, f32[16]{0:T(128)} %diff.5, f32[128,128]{1,0:T(8,128)} %area.3, ...), custom_call_target="tpu_custom_call" | custom-call | flops 60000000 | bytes 12582912 | tf_op jit(solution)/shard_map/third/pallas_call | solution.py:468
  55.0 23.7 %all-to-all-done = f32[128,40,128]{2,1,0:T(8,128)S(1)} async-done(((f32[128,40,128]{2,1,0:T(8,128)}), f32[128,40,128]{2,1,0:T(8,128)S(1)}, u32[]{:S(2)}, u32[]{:S(2)}) %all-to-all-start) | async-done | bytes 2621472 | tf_op jit(solution)/shard_map/all_to_all | solution.py:553
  78.7 2.0 %last.1 = (f32[256,2048]{1,0:T(8,128)}, f32[256,512]{1,0:T(8,128)}) custom-call(f32[5120,128]{1,0:T(8,128)S(1)} %bitcast.9), custom_call_target="tpu_custom_call" | custom-call | tf_op jit(solution)/shard_map/last/pallas_call | solution.py:507
  (1 shorter events, 0.0 us)
Async XLA Ops:
  0.6 0.7 copy-start.1
  11.8 9.4 %collective-permute-start.1 = (f32[24,8,128]{2,1,0:T(8,128)S(1)}, f32[24,8,128]{2,1,0:T(8,128)S(1)}, u32[]{:S(2)}, u32[]{:S(2)}) collective-permute-start(f32[24,8,128]{2,1,0:T(8,128)S(1)} %get-tuple-element.15.ew), channel_id=1, source_target_pairs={{0,16},{16,32},{32,48},{48,64},{64,80},{80,96},{96,112},{112,0},{1... | collective-permute-start | bytes 294920 | tf_op jit(solution)/shard_map/ppermute | solution.py:539
  13.4 7.7 %collective-permute-start = (f32[24,8,128]{2,1,0:T(8,128)S(1)}, f32[24,8,128]{2,1,0:T(8,128)S(1)}, u32[]{:S(2)}, u32[]{:S(2)}) collective-permute-start(f32[24,8,128]{2,1,0:T(8,128)S(1)} %get-tuple-element.15.ew), channel_id=1, source_target_pairs={{16,0},{32,16},{48,32},{64,48},{80,64},{96,80},{112,96},{0,112},{1... | collective-permute-start | bytes 294920 | tf_op jit(solution)/shard_map/ppermute | solution.py:540
  16.0 4.3 %collective-permute-start.3 = (f32[96,128]{1,0:T(8,128)S(1)}, f32[96,128]{1,0:T(8,128)S(1)}, u32[]{:S(2)}, u32[]{:S(2)}) collective-permute-start(f32[96,128]{1,0:T(8,128)S(1)} %get-tuple-element.23), channel_id=1, source_target_pairs={{1,0},{2,1},{3,2},{4,3},{5,4},{6,5},{7,6},{8,7},{9,8},{10,9},{11,1... | collective-permute-start | bytes 147464 | tf_op jit(solution)/shard_map/ppermute | solution.py:549
  17.3 3.9 %collective-permute-start.2 = (f32[96,128]{1,0:T(8,128)S(1)}, f32[96,128]{1,0:T(8,128)S(1)}, u32[]{:S(2)}, u32[]{:S(2)}) collective-permute-start(f32[96,128]{1,0:T(8,128)S(1)} %get-tuple-element.24), channel_id=1, source_target_pairs={{0,1},{1,2},{2,3},{3,4},{4,5},{5,6},{6,7},{7,8},{8,9},{9,10},{10,1... | collective-permute-start | bytes 147464 | tf_op jit(solution)/shard_map/ppermute | solution.py:548
  26.8 1.5 %copy-start = (f32[5120,128]{1,0:T(8,128)}, f32[5120,128]{1,0:T(8,128)S(1)}, u32[]{:S(2)}) copy-start(f32[5120,128]{1,0:T(8,128)S(1)} %get-tuple-element.20) | copy-start | bytes 7864324
  28.4 50.3 %all-to-all-start = ((f32[128,40,128]{2,1,0:T(8,128)}), f32[128,40,128]{2,1,0:T(8,128)S(1)}, u32[]{:S(2)}, u32[]{:S(2)}) async-start(f32[128,40,128]{2,1,0:T(8,128)} %bitcast.10), calls=%async_computation | async-start | bytes 5242880 | tf_op jit(solution)/shard_map/all_to_all | solution.py:553

commit v2 on v1

v2 whole, which is shorter than its diff:
```python
import jax
import jax.numpy as jnp
from jax import lax
from jax.experimental import pallas as pl
from jax.experimental.pallas import tpu as pltpu
from jax.sharding import PartitionSpec as P


time_step = 0.05
depth_floor = 0.25
weight_floor = 0.25

TR, LV = 4, 16
ROWS, LANES = 128, 128
GROUPS = 8
DEV, CAP = 128, 2
CHUNKS = 20
PARTS = 2
F32, BF16 = jnp.float32, jnp.bfloat16
MIB = 1 << 20


def lane_iota(shape=(8, 128)):
    return lax.broadcasted_iota(jnp.int32, shape, len(shape) - 1)


def sub_iota(shape=(8, 128)):
    return lax.broadcasted_iota(jnp.int32, shape, len(shape) - 2)


def face(lower_h, upper_h, lower_speed, upper_speed, mixing, keep=None):
    open_depth = jnp.minimum(lower_h, upper_h)
    if keep is not None:
        open_depth = jnp.where(keep, open_depth, 0.0)
    speed = 0.5 * (lower_speed + upper_speed)
    ahead = jnp.maximum(speed, 0.0)
    back = ahead - speed
    return open_depth * (ahead + mixing), open_depth * (back + mixing)


def halves(values):
    high = values.astype(BF16)
    return high, (values - high.astype(F32)).astype(BF16)


def split_dot(left, right):
    high, low = halves(left)
    return jnp.dot(high, right, preferred_element_type=F32) + jnp.dot(
        low, right, preferred_element_type=F32
    )


def input_copies(hbm, vmem, sems):
    per = LV // GROUPS

    def copies(group):
        levels = pl.ds(group * per, per)
        out = [pltpu.make_async_copy(hbm[0].at[:, levels], vmem[0].at[:, levels], sems.at[0, group])]
        for n in range(1, 5):
            out.append(
                pltpu.make_async_copy(hbm[n].at[levels], vmem[n].at[levels], sems.at[n, group])
            )
        return out

    return copies


def row_set(start):
    return (pl.ds(start, 8, stride=4), slice(None))


def kernel_rows(tr, fill, mask, north, ns_fwd, ns_bwd, tr_s, fill_s, mask_s, north_s, sems):
    copies = []
    for n, (src, dst) in enumerate(((tr, tr_s), (fill, fill_s), (mask, mask_s), (north, north_s))):
        for side in range(2):
            rows = pl.ds(side * (ROWS - 8), 8)
            if n == 0:
                copies.append(
                    pltpu.make_async_copy(src.at[:, :, rows], dst.at[side], sems.at[n, side])
                )
            else:
                copies.append(
                    pltpu.make_async_copy(src.at[:, rows], dst.at[side], sems.at[n, side])
                )
            copies[-1].start()
    for copy in copies:
        copy.wait()
    flip = lax.axis_index("lon") >= lax.axis_size("lon") // 2
    for n in range(6):
        for half in range(2):
            levels = range(8 * half, 8 * half + 8)
            lines = []
            for side in range(2):
                row = 7 * side
                pick = lambda ref, k: ref[side, k, pl.ds(row, 1), :]
                if n < TR:
                    parts = [tr_s[side, n, k, pl.ds(row, 1), :] for k in levels]
                elif n == TR:
                    parts = [pick(fill_s, k) * pick(mask_s, k).astype(F32) for k in levels]
                else:
                    parts = [pick(north_s, k) for k in levels]
                lines.append(jnp.concatenate(parts, axis=0))
            at = pl.ds(n * 16 + 8 * half, 8)
            ns_fwd[at, :] = jnp.where(flip, lines[0], lines[1])
            ns_bwd[at, :] = jnp.where(flip, lines[1], lines[0])


def kernel_rows_call(tracers, fill, mask, north):
    hbm = pl.BlockSpec(memory_space=pltpu.HBM)
    vmem = pl.BlockSpec(memory_space=pltpu.VMEM)
    return pl.pallas_call(
        kernel_rows,
        name="rows",
        out_shape=(jax.ShapeDtypeStruct((96, 128), F32),) * 2,
        in_specs=[hbm] * 4,
        out_specs=(vmem,) * 2,
        scratch_shapes=[
            pltpu.VMEM((2, TR, LV, 8, LANES), F32),
            pltpu.VMEM((2, LV, 8, LANES), F32),
            pltpu.VMEM((2, LV, 8, LANES), jnp.int32),
            pltpu.VMEM((2, LV, 8, LANES), F32),
            pltpu.SemaphoreType.DMA((4, 2)),
        ],
        compiler_params=pltpu.CompilerParams(vmem_limit_bytes=4 * MIB),
        cost_estimate=pl.CostEstimate(flops=1_000_000, bytes_accessed=MIB, transcendentals=0),
    )(tracers, fill, mask, north)


def kernel_first(
    tr, fill, mask, east, north, diff, area, owner,
    num2, den2, ew, placing,
    tr_s, fill_s, mask_s, east_s, north_s, area_s, owner_s, even_s, odd_s, sems, area_sem, owner_sem,
):
    hbm, vmem = (tr, fill, mask, east, north), (tr_s, fill_s, mask_s, east_s, north_s)
    copies = input_copies(hbm, vmem, sems)
    area_copy = pltpu.make_async_copy(area, area_s, area_sem)
    owner_copy = pltpu.make_async_copy(owner, owner_s, owner_sem)
    owner_copy.start()
    for group in range(GROUPS):
        for copy in copies(group):
            copy.start()
        if group == 0:
            area_copy.start()

    across = lane_iota((DEV, DEV))
    down = sub_iota((DEV, DEV))
    source = sub_iota((256, 128))
    target = lane_iota((256, 128))
    pool = jnp.where(target == (source >> 7) * 64 + ((source & 127) >> 1), 1.0, 0.0).astype(BF16)
    owner_copy.wait()
    who_row = owner_s[...]
    who = jnp.sum(jnp.where(down == across, who_row, 0), axis=1, keepdims=True)
    same = jnp.where((who == who_row) & (down < across), 1, 0)
    rank = jnp.sum(same, axis=0, keepdims=True)
    row_of = who_row * CAP + rank
    for part in range(CAP):
        here = jnp.where(down + part * DEV == row_of, 1.0, 0.0).astype(BF16)
        placing[pl.ds(part * DEV, DEV), 0:DEV] = here
        placing[pl.ds(part * DEV, DEV), DEV : 2 * DEV] = here

    area_copy.wait()
    lane, sub = lane_iota(), sub_iota()
    is_even = (lane & 1) == 0
    not_last = lane < 127
    not_top = sub < 7
    swap = jnp.where(is_even, lane + 127, lane + 1) & 127

    def level(k, store):
        mixing = diff[k]

        def load(ref, start):
            return ref[(k, *row_set(start))]

        def depth(start):
            return load(fill_s, start) * load(mask_s, start).astype(F32)

        def north_face(q, h, v):
            if q < 3:
                return face(h, depth(32 * q + 4), v, load(north_s, 32 * q + 4), mixing)
            h_up, v_up = pltpu.roll(depth(96), 7, 0), pltpu.roll(load(north_s, 96), 7, 0)
            return face(h, h_up, v, v_up, mixing, keep=not_top)

        where_t = [(lane >> 1) == t * 16 + k for t in range(TR)]
        before = jnp.zeros((8, 128), F32), jnp.zeros((8, 128), F32)
        for q in range(4):
            hs = [depth(32 * q + j) for j in range(4)]
            vs = [load(north_s, 32 * q + j) for j in range(4)]
            norths = [face(hs[j], hs[j + 1], vs[j], vs[j + 1], mixing) for j in range(3)]
            norths.append(north_face(q, hs[3], vs[3]))
            turned = tuple(pltpu.roll(x, 1, 0) for x in norths[3])
            south = tuple(jnp.where(sub > 0, a, b) for a, b in zip(turned, before))
            before = turned
            centre, cross, gain_n, gain_s, weights = [], [], [], [], []
            for j in range(4):
                v = 4 * q + j
                h = hs[j]
                u = load(east_s, 32 * q + j)
                base = 64 * (v % 2)
                packed = ew[16 + v // 2]
                packed = jnp.where(
                    (lane >> 1) == k + base // 2, pltpu.roll(h, 2 * k + 1 + base, 1), packed
                )
                ew[16 + v // 2] = jnp.where(
                    (lane >> 1) == k + 16 + base // 2, pltpu.roll(u, 2 * k + 33 + base, 1), packed
                )
                w = area_s[row_set(32 * q + j)] * h
                g = (time_step * h) / jnp.maximum(h, depth_floor)
                p_e, q_e = face(
                    h, pltpu.roll(h, 127, 1), u, pltpu.roll(u, 127, 1), mixing, keep=not_last
                )
                q_w = pltpu.roll(q_e, 1, 1)
                p_n, q_n = norths[j]
                p_s, q_s = norths[j - 1] if j else south
                to_west = pltpu.roll(g, 1, 1) * q_w
                to_east = pltpu.roll(g, 127, 1) * p_e
                own = w - g * ((p_e + q_w) + (p_n + q_s))
                centre.append(own + jnp.where(is_even, to_east, to_west))
                cross.append(jnp.where(is_even, to_west, to_east))
                gain_n.append(g * q_n)
                gain_s.append(g * p_s)
                weights.append(w)
            for j in range(4):
                packed = ew[4 * q + j]
                for t in range(TR):
                    cell = tr_s[(t, k, *row_set(32 * q + j))]
                    packed = jnp.where(where_t[t], pltpu.roll(cell, 2 * k + 32 * t + 1, 1), packed)
                ew[4 * q + j] = packed
            first = [centre[2 * par] + gain_s[2 * par + 1] for par in range(2)]
            second = [centre[2 * par + 1] + gain_n[2 * par] for par in range(2)]
            for t in range(TR):
                cells = [tr_s[(t, k, *row_set(32 * q + j))] for j in range(4)]
                if q:
                    below = tr_s[(t, k, *row_set(32 * q - 1))]
                else:
                    below = pltpu.roll(cells[3], 1, 0)
                if q < 3:
                    above = tr_s[(t, k, *row_set(32 * q + 4))]
                else:
                    above = pltpu.roll(cells[0], 7, 0)
                around = [below, *cells, above]
                for par in range(2):
                    low, a, b, high = around[2 * par : 2 * par + 4]
                    value = (first[par] * a + second[par] * b) + (
                        gain_s[2 * par] * low + gain_n[2 * par + 1] * high
                    )
                    side = cross[2 * par] * a + cross[2 * par + 1] * b
                    value = value + jnp.take_along_axis(side, swap, axis=1)
                    store[pl.ds(t * 32 + q * 8, 8), pl.ds(par * 128, 128)] = value
            for par in range(2):
                store[pl.ds(128 + q * 8, 8), pl.ds(par * 128, 128)] = (
                    weights[2 * par] + weights[2 * par + 1]
                )

    def pooled(k, store):
        values = split_dot(store[...], pool)
        rows = pl.ds(pl.multiple_of(k * 32, 32), 32)
        for t in range(TR):
            num2[t, rows, :] = values[t * 32 : t * 32 + 32]
        den2[rows, :] = values[128:160]

    def group_body(group, carry):
        for copy in copies(group):
            copy.wait()
        pooled((group * 2 + LV - 1) % LV, odd_s)
        level(group * 2, even_s)
        pooled(group * 2, even_s)
        level(group * 2 + 1, odd_s)
        return carry

    odd_s[...] = jnp.zeros_like(odd_s)
    lax.fori_loop(0, GROUPS, group_body, 0)
    pooled(LV - 1, odd_s)


def kernel_first_call(tracers, fill, mask, east, north, diff, area, owner):
    hbm = pl.BlockSpec(memory_space=pltpu.HBM)
    vmem = pl.BlockSpec(memory_space=pltpu.VMEM)
    return pl.pallas_call(
        kernel_first,
        name="first",
        out_shape=(
            jax.ShapeDtypeStruct((TR, 512, 128), F32),
            jax.ShapeDtypeStruct((512, 128), F32),
            jax.ShapeDtypeStruct((24, 8, 128), F32),
            jax.ShapeDtypeStruct((CAP * DEV, 2 * DEV), BF16),
        ),
        in_specs=[hbm] * 5 + [pl.BlockSpec(memory_space=pltpu.SMEM), hbm, hbm],
        out_specs=(vmem,) * 4,
        scratch_shapes=[
            pltpu.VMEM((TR, LV, ROWS, LANES), F32),
            pltpu.VMEM((LV, ROWS, LANES), F32),
            pltpu.VMEM((LV, ROWS, LANES), jnp.int32),
            pltpu.VMEM((LV, ROWS, LANES), F32),
            pltpu.VMEM((LV, ROWS, LANES), F32),
            pltpu.VMEM((ROWS, LANES), F32),
            pltpu.VMEM((1, DEV), jnp.int32),
            pltpu.VMEM((160, 256), F32),
            pltpu.VMEM((160, 256), F32),
            pltpu.SemaphoreType.DMA((5, GROUPS)),
            pltpu.SemaphoreType.DMA,
            pltpu.SemaphoreType.DMA,
        ],
        compiler_params=pltpu.CompilerParams(vmem_limit_bytes=24 * MIB),
        cost_estimate=pl.CostEstimate(flops=60_000_000, bytes_accessed=11 * MIB, transcendentals=0),
    )(tracers, fill, mask, east, north, diff, area, owner)


def spread(values, offset):
    index = (lane_iota() & 31) + offset
    return jnp.take_along_axis(values, index, axis=1)


def kernel_second(
    num2, den2, ew, from_east, from_west, ns_fwd, ns_bwd, got_fwd, got_bwd, diff, placing,
    send, d_ew, d_ns,
    work, acc, chunks, send_s, sems,
):
    lane, sub = lane_iota(), sub_iota()
    flip = lax.axis_index("lon") >= lax.axis_size("lon") // 2
    at_fold = lax.axis_index("lat") == lax.axis_size("lat") - 1
    is_east = (lane & 1) == 0
    level_of = (lane >> 1) & 15
    mixing = jnp.zeros((8, 128), F32)
    for k in range(LV):
        mixing = jnp.where(level_of == k, diff[k], mixing)

    def neighbour(n):
        return jnp.where(
            is_east, pltpu.roll(from_east[n], 127, 1), pltpu.roll(from_west[n], 1, 1)
        )

    pending = None
    for v in range(16):
        own_hu, near_hu = ew[16 + v // 2], neighbour(16 + v // 2)
        base = 64 * (v % 2)
        h = spread(own_hu, base)
        p, q = face(
            h, spread(near_hu, base), spread(own_hu, base + 32), spread(near_hu, base + 32), mixing
        )
        div = jnp.where(is_east, q, p) * neighbour(v) - jnp.where(is_east, p, q) * ew[v]
        d_ew[v] = div
        value = (time_step * h) / jnp.maximum(h, depth_floor) * div
        if v % 2 == 0:
            pending = value
        else:
            value = pending + value
            work[v // 2] = jnp.where(is_east, value, pltpu.roll(value, 64, 1))

    low_ends = (lane == 0) | (lane == 63)
    high_ends = (lane == 64) | (lane == 127)

    def add_ends(k, carry):
        for t in range(TR):
            for q in range(4):
                rows = pl.ds(pl.multiple_of(k * 32 + q * 8, 8), 8)
                shift = 127 - 2 * k + (128 - 32 * t)
                low = pltpu.roll(work[2 * q], shift - 64, 1)
                high = pltpu.roll(work[2 * q + 1], shift, 1)
                edge = jnp.where(low_ends, low, jnp.where(high_ends, high, 0.0))
                acc[t, rows, :] = num2[t, rows, :] + edge
        return carry

    lax.fori_loop(0, LV, add_ends, 0)

    source = sub_iota((128, 128))
    target = lane_iota((128, 128))
    pools = [
        jnp.where(target == par * 64 + (source >> 1), 1.0, 0.0).astype(BF16) for par in range(2)
    ]
    quarter = [
        jnp.where(target == j * 32 + ((source & 63) >> 1), 1.0, 0.0).astype(BF16) for j in range(4)
    ]

    back = 127 - lane
    for half in range(2):
        mix = jnp.zeros((8, 128), F32)
        for k in range(8):
            mix = jnp.where(sub == k, diff[8 * half + k], mix)

        def rows_of(ref, n):
            return ref[pl.ds(n * 16 + 8 * half, 8), :]

        def own(n, top):
            pair = (ns_bwd, ns_fwd) if top else (ns_fwd, ns_bwd)
            return jnp.where(flip, rows_of(pair[0], n), rows_of(pair[1], n))

        def near(n, top, sign=1.0):
            if not top:
                return jnp.where(flip, rows_of(got_bwd, n), rows_of(got_fwd, n))
            value = jnp.where(flip, rows_of(got_fwd, n), rows_of(got_bwd, n))
            turned = sign * jnp.take_along_axis(value, back, axis=1)
            return jnp.where(at_fold, turned, value)

        for top in (False, True):
            h = own(4, top)
            p, q = face(h, near(4, top), own(5, top), near(5, top, -1.0), mix)
            gain = (time_step * h) / jnp.maximum(h, depth_floor)
            for t in range(TR):
                if top:
                    div = q * near(t, top) - p * own(t, top)
                else:
                    div = p * near(t, top) - q * own(t, top)
                d_ns[int(top), pl.ds(t * 16 + 8 * half, 8), :] = div
                at = (t, pl.ds(256 * half + 31 * int(top), 8, stride=32), slice(None))
                acc[at] = acc[at] + split_dot(gain * div, pools[int(top)])

    def keep(n, values):
        high, low = halves(values)
        chunks[0:128, pl.ds(n * 128, 128)] = high
        chunks[128:256, pl.ds(n * 128, 128)] = low

    def every_fourth(ref, *lead, j):
        return jnp.concatenate(
            [ref[(*lead, pl.ds(32 * m + j, 8, stride=4), slice(None))] for m in range(16)], axis=0
        )

    gains = []
    den4 = jnp.zeros((128, 128), F32)
    for j in range(4):
        den = every_fourth(den2, j=j)
        gains.append(1.0 / jnp.maximum(den, weight_floor))
        den4 = den4 + split_dot(den, quarter[j])
    gain4 = 1.0 / jnp.maximum(den4, weight_floor)
    for t in range(TR):
        num4 = jnp.zeros((128, 128), F32)
        for j in range(4):
            num = every_fourth(acc, t, j=j)
            keep(t * 4 + j, num * gains[j])
            num4 = num4 + split_dot(num, quarter[j])
        keep(16 + t, num4 * gain4)

    each = CAP * DEV // PARTS
    copies = []
    for part in range(PARTS):
        left = placing[pl.ds(part * each, each), :]
        for n in range(CHUNKS // 2):
            placed = jnp.dot(left, chunks[:, pl.ds(n * 256, 256)], preferred_element_type=F32)
            for c in range(2):
                for m in range(each // 8):
                    start = (part * each + m * 8) * CHUNKS + 2 * n + c
                    send_s[pl.ds(start, 8, stride=CHUNKS), :] = placed[
                        m * 8 : m * 8 + 8, c * 128 : c * 128 + 128
                    ]
        rows = pl.ds(part * each * CHUNKS, each * CHUNKS)
        copies.append(pltpu.make_async_copy(send_s.at[rows], send.at[rows], sems.at[part]))
        copies[-1].start()
    for copy in copies:
        copy.wait()


def kernel_second_call(*args):
    vmem = pl.BlockSpec(memory_space=pltpu.VMEM)
    return pl.pallas_call(
        kernel_second,
        name="second",
        out_shape=(
            pltpu.HBM((DEV * CAP * CHUNKS, 128), F32),
            jax.ShapeDtypeStruct((16, 8, 128), F32),
            jax.ShapeDtypeStruct((2, 64, 128), F32),
        ),
        in_specs=[vmem] * 9 + [pl.BlockSpec(memory_space=pltpu.SMEM), vmem],
        out_specs=(pl.BlockSpec(memory_space=pltpu.HBM), vmem, vmem),
        scratch_shapes=[
            pltpu.VMEM((8, 8, 128), F32),
            pltpu.VMEM((TR, 512, 128), F32),
            pltpu.VMEM((256, 2560), BF16),
            pltpu.VMEM((DEV * CAP * CHUNKS, 128), F32),
            pltpu.SemaphoreType.DMA((PARTS,)),
        ],
        compiler_params=pltpu.CompilerParams(vmem_limit_bytes=16 * MIB),
        cost_estimate=pl.CostEstimate(flops=60_000_000, bytes_accessed=6 * MIB, transcendentals=0),
    )(*args)


def kernel_third(
    tr, fill, mask, east, north, diff, area, d_ew, d_ns,
    out,
    tr_s, fill_s, mask_s, east_s, north_s, area_s, out_s, sems, area_sem, out_sems,
):
    hbm, vmem = (tr, fill, mask, east, north), (tr_s, fill_s, mask_s, east_s, north_s)
    copies = input_copies(hbm, vmem, sems)
    area_copy = pltpu.make_async_copy(area, area_s, area_sem)
    for group in range(GROUPS):
        for copy in copies(group):
            copy.start()
        if group == 0:
            area_copy.start()
    area_copy.wait()
    lane, sub = lane_iota(), sub_iota()
    ends = (lane == 0) | (lane == 127)
    not_last, not_top = lane < 127, sub < 7
    per = LV // GROUPS

    def out_copy(group):
        levels = pl.ds(group * per, per)
        return pltpu.make_async_copy(out_s.at[:, levels], out.at[:, levels], out_sems.at[group])

    def level(k):
        mixing = diff[k]

        def load(ref, start):
            return ref[(k, *row_set(start))]

        def depth(start):
            return load(fill_s, start) * load(mask_s, start).astype(F32)

        before = [jnp.zeros((8, 128), F32)] * TR
        for q in range(4):
            hs = [depth(32 * q + j) for j in range(4)]
            vs = [load(north_s, 32 * q + j) for j in range(4)]
            if q < 3:
                hs.append(depth(32 * q + 4))
                vs.append(load(north_s, 32 * q + 4))
            else:
                hs.append(pltpu.roll(hs[0], 7, 0))
                vs.append(pltpu.roll(vs[0], 7, 0))
            coefs = []
            for j in range(4):
                top = q == 3 and j == 3
                h, u = hs[j], load(east_s, 32 * q + j)
                rate = time_step / (area_s[row_set(32 * q + j)] * jnp.maximum(h, depth_floor))
                coefs.append(
                    face(h, pltpu.roll(h, 127, 1), u, pltpu.roll(u, 127, 1), mixing, keep=not_last)
                    + face(h, hs[j + 1], vs[j], vs[j + 1], mixing, keep=not_top if top else None)
                    + (rate,)
                )
            for t in range(TR):
                cells = [tr_s[(t, k, *row_set(32 * q + j))] for j in range(4)]
                if q < 3:
                    cells.append(tr_s[(t, k, *row_set(32 * q + 4))])
                else:
                    cells.append(pltpu.roll(cells[0], 7, 0))
                norths = [coefs[j][2] * cells[j] - coefs[j][3] * cells[j + 1] for j in range(4)]
                turned = pltpu.roll(norths[3], 1, 0)
                souths = [jnp.where(sub > 0, turned, before[t])] + norths[:3]
                before[t] = turned
                for j in range(4):
                    p_e, q_e, _, _, rate = coefs[j]
                    cell = cells[j]
                    flux = p_e * cell - q_e * pltpu.roll(cell, 127, 1)
                    div = (pltpu.roll(flux, 1, 1) - flux) + (souths[j] - norths[j])
                    moved = pltpu.roll(d_ew[4 * q + j], 127 - 2 * k + (128 - 32 * t), 1)
                    div = div + jnp.where(ends, moved, 0.0)
                    if q == 0 and j == 0:
                        div = div + jnp.where(sub == 0, d_ns[0, pl.ds(t * 16 + k, 1), :], 0.0)
                    if q == 3 and j == 3:
                        div = div + jnp.where(sub == 7, d_ns[1, pl.ds(t * 16 + k, 1), :], 0.0)
                    out_s[(t, k, *row_set(32 * q + j))] = cell + rate * div

    def group_body(group, carry):
        for copy in copies(group):
            copy.wait()
        for n in range(per):
            level(group * per + n)
        out_copy(group).start()
        return carry

    lax.fori_loop(0, GROUPS, group_body, 0)
    for group in range(GROUPS):
        out_copy(group).wait()


def kernel_third_call(tracers, fill, mask, east, north, diff, area, d_ew, d_ns):
    hbm = pl.BlockSpec(memory_space=pltpu.HBM)
    vmem = pl.BlockSpec(memory_space=pltpu.VMEM)
    return pl.pallas_call(
        kernel_third,
        name="third",
        out_shape=jax.ShapeDtypeStruct((TR, LV, ROWS, LANES), F32),
        in_specs=[hbm] * 5 + [pl.BlockSpec(memory_space=pltpu.SMEM), hbm, vmem, vmem],
        out_specs=hbm,
        scratch_shapes=[
            pltpu.VMEM((TR, LV, ROWS, LANES), F32),
            pltpu.VMEM((LV, ROWS, LANES), F32),
            pltpu.VMEM((LV, ROWS, LANES), jnp.int32),
            pltpu.VMEM((LV, ROWS, LANES), F32),
            pltpu.VMEM((LV, ROWS, LANES), F32),
            pltpu.VMEM((ROWS, LANES), F32),
            pltpu.VMEM((TR, LV, ROWS, LANES), F32),
            pltpu.SemaphoreType.DMA((5, GROUPS)),
            pltpu.SemaphoreType.DMA,
            pltpu.SemaphoreType.DMA((GROUPS,)),
        ],
        compiler_params=pltpu.CompilerParams(vmem_limit_bytes=24 * MIB),
        cost_estimate=pl.CostEstimate(flops=60_000_000, bytes_accessed=12 * MIB, transcendentals=0),
    )(tracers, fill, mask, east, north, diff, area, d_ew, d_ns)


SPLITS = 4


def kernel_last(got, two, four):
    for m in range(32 // SPLITS):
        for n in range(CHUNKS):
            value = got[pl.ds(m * 8 * CHUNKS + n, 8, stride=CHUNKS), :]
            if n < 16:
                two[pl.ds(m * 8, 8), pl.ds(n * 128, 128)] = value
            else:
                four[pl.ds(m * 8, 8), pl.ds((n - 16) * 128, 128)] = value


def kernel_last_call(got):
    return pl.pallas_call(
        kernel_last,
        name="last",
        grid=(SPLITS,),
        out_shape=(
            jax.ShapeDtypeStruct((DEV * CAP, 2048), F32),
            jax.ShapeDtypeStruct((DEV * CAP, 512), F32),
        ),
        in_specs=[pl.BlockSpec((DEV * 40 // SPLITS, 128), lambda s: (s, 0))],
        out_specs=(
            pl.BlockSpec((DEV * CAP // SPLITS, 2048), lambda s: (s, 0)),
            pl.BlockSpec((DEV * CAP // SPLITS, 512), lambda s: (s, 0)),
        ),
        compiler_params=pltpu.CompilerParams(vmem_limit_bytes=8 * MIB),
    )(got)


def local(
    tracers, fill_fraction, ocean_mask, east_speed, north_speed, diffusivity, cell_area, owner_map
):
    lon_count = lax.axis_size("lon")
    lat_count = lax.axis_size("lat")
    *fields, diffusivity, cell_area, owners = (
        pltpu.with_memory_space_constraint(x, pltpu.HBM)
        for x in (
            tracers, fill_fraction, ocean_mask, east_speed, north_speed, diffusivity, cell_area,
            owner_map.reshape(1, DEV),
        )
    )
    tracers, fill_fraction, ocean_mask, east_speed, north_speed = fields
    ns_fwd, ns_bwd = kernel_rows_call(tracers, fill_fraction, ocean_mask, north_speed)
    both = ("lon", "lat")
    chain = []
    for low in range(lon_count // 2):
        high = lon_count - 1 - low
        up = [low * lat_count + a for a in range(lat_count)]
        path = up + [high * lat_count + a for a in reversed(range(lat_count))]
        chain += list(zip(path[:-1], path[1:]))
    got_fwd = lax.ppermute(ns_fwd, both, chain)
    got_bwd = lax.ppermute(ns_bwd, both, [(b, a) for a, b in chain])
    num2, den2, ew, placing = kernel_first_call(*fields, diffusivity, cell_area, owners)
    ring = [(i, (i + 1) % lon_count) for i in range(lon_count)]
    from_west = lax.ppermute(ew, "lon", ring)
    from_east = lax.ppermute(ew, "lon", [(b, a) for a, b in ring])
    send, d_ew, d_ns = kernel_second_call(
        num2, den2, ew, from_east, from_west, ns_fwd, ns_bwd, got_fwd, got_bwd, diffusivity, placing
    )
    got = lax.all_to_all(
        send.reshape(DEV, CAP * CHUNKS, 128), both, split_axis=0, concat_axis=0, tiled=True
    )
    updated = kernel_third_call(*fields, diffusivity, cell_area, d_ew, d_ns)
    two, four = kernel_last_call(got.reshape(DEV * CAP * CHUNKS, 128))
    return (updated, two[None], four[None])


def solution(mesh):
    in_specs = (
        P(None, None, "lat", "lon"),
        P(None, "lat", "lon"),
        P(None, "lat", "lon"),
        P(None, "lat", "lon"),
        P(None, "lat", "lon"),
        P(),
        P("lat", "lon"),
        P(("lon", "lat"), None),
    )
    out_specs = (
        P(None, None, "lat", "lon"),
        P(("lon", "lat"), None, None),
        P(("lon", "lat"), None, None),
    )
    return jax.shard_map(
        local,
        mesh=mesh, in_specs=in_specs, out_specs=out_specs, check_vma=False,
    )
```

time: 80.9 us -> 112 us (1.38)
  Pallas kernels: 30 us -> 86.5 us
  waiting for transfers between devices: 24.6 us -> 3.92 us
  starting transfers between devices: 23.1 us -> 20.6 us
  local copies, waits for them, and re-layouts: 2.17 us -> 0 us
    pallas_call x1, Pallas kernels: 12 us -> 55.8 us  [kernel_third_call(): pl.pallas_call(kernel_third, name='third', out_shape=jax.ShapeDtypeStruct...]
    all_to_all x1, waiting for transfers between devices: 23.7 us -> 0.01 us  [local(): lax.all_to_all(send.reshape(DEV, CAP * CHUNKS, 128), both, split_axis=0,...]
    pallas_call x1, Pallas kernels: 10.5 us -> 22.1 us  [kernel_first_call(): pl.pallas_call(kernel_first, name='first', out_shape=(jax.ShapeDtypeStruc...]
    ppermute x2, waiting for transfers between devices: 0.85 us -> 3.91 us  [the longest x1 3.91 us: local(): got_bwd = lax.ppermute(ns_bwd, both, [(b, a) for a, b in chain])]
    unnamed x4 -> x0, local copies, waits for them, and re-layouts: 2.16 us -> none
    ppermute x2, starting transfers between devices: 4.32 us -> 2.75 us  [the longest x1 1.46 us: local(): got_fwd = lax.ppermute(ns_fwd, both, chain)]
    pallas_call x1 -> x2, Pallas kernels: 5.65 us -> 6.7 us  [the longest x1 5.46 us: kernel_second_call(): pl.pallas_call(kernel_second, name='second', out_shape=(pltpu.HBM((DEV *...]
  transfers between devices with their start and end apart: 5 -> 5, of which waited for: 2 -> 1; matrix products, arithmetic and copies ran while one was open for 0% -> 0% of each run, Pallas kernels for 15% -> 51%
where the time goes in v2:
time: 112 us
  Pallas kernels  86.5 us (77%)
  starting transfers between devices  20.6 us (18%)
  waiting for transfers between devices  3.92 us (4%)
    pallas_call x1, Pallas kernels, kernel_third_call(): pl.pallas_call(kernel_third, name='third', out_shape=jax.ShapeDtypeStruct...  55.8 us
    pallas_call x1, Pallas kernels, kernel_first_call(): pl.pallas_call(kernel_first, name='first', out_shape=(jax.ShapeDtypeStruc...  22.1 us
    all_to_all x1, starting transfers between devices, local(): lax.all_to_all(send.reshape(DEV, CAP * CHUNKS, 128), both, split_axis=0,...  13.6 us
    pallas_call x1, Pallas kernels, kernel_second_call(): pl.pallas_call(kernel_second, name='second', out_shape=(pltpu.HBM((DEV *...  5.46 us
    ppermute x1, waiting for transfers between devices, local(): got_bwd = lax.ppermute(ns_bwd, both, [(b, a) for a, b in chain])  3.91 us
    ppermute x1, starting transfers between devices, local(): from_east = lax.ppermute(ew, 'lon', [(b, a) for a, b in ring])  2.53 us
  transfers between devices with their start and end apart: 5, of which 1 were waited for; matrix products, arithmetic and copies ran while one was open for 0% of the time, Pallas kernels for 51%

profile of v2, /device:TPU:0, one launch (start us, length us, event | category | flops | bytes accessed | tf_op | source)
XLA Modules:
  0.0 111.7 jit_solution(12857635629530421723)
XLA Ops:
  0.6 22.1 %first.1 = (f32[4,512,128]{2,1,0:T(8,128)S(1)}, f32[512,128]{1,0:T(8,128)S(1)}, f32[24,8,128]{2,1,0:T(8,128)S(1)}, bf16[256,256]{1,0:T(8,128)(2,1)S(1)}) custom-call(f32[4,16,128,128]{3,2,1,0:T(8,128)} %tr.5, f32[16,128,128]{2,1,0:T(8,128)} %fill.5, s32[16,128,128]{2,1,0:T(8,128)} %mask.5, f32[16,128,128]{2,1,0:T(8,128)} %east.3, f32[16,128,128]{2,1,0:T(8,128)} %north.5, ...), custom_call_target="tpu_custom_call" | custom-call | flops 60000000 | bytes 11534336 | tf_op jit(solution)/shard_map/first/pallas_call | solution.py:278
  22.7 1.7 %collective-permute-start.1 = (f32[24,8,128]{2,1,0:T(8,128)S(1)}, f32[24,8,128]{2,1,0:T(8,128)S(1)}, u32[]{:S(2)}, u32[]{:S(2)}) collective-permute-start(f32[24,8,128]{2,1,0:T(8,128)S(1)} %get-tuple-element.16.ew), channel_id=1, source_target_pairs={{0,16},{16,32},{32,48},{48,64},{64,80},{80,96},{96,112},{112,0},{1... | collective-permute-start | bytes 294920 | tf_op jit(solution)/shard_map/ppermute | solution.py:645
  24.4 2.5 %collective-permute-start = (f32[24,8,128]{2,1,0:T(8,128)S(1)}, f32[24,8,128]{2,1,0:T(8,128)S(1)}, u32[]{:S(2)}, u32[]{:S(2)}) collective-permute-start(f32[24,8,128]{2,1,0:T(8,128)S(1)} %get-tuple-element.16.ew), channel_id=1, source_target_pairs={{16,0},{32,16},{48,32},{64,48},{80,64},{96,80},{112,96},{0,112},{1... | collective-permute-start | bytes 294920 | tf_op jit(solution)/shard_map/ppermute | solution.py:646
  26.9 1.2 %rows.1 = (f32[96,128]{1,0:T(8,128)S(1)}, f32[96,128]{1,0:T(8,128)S(1)}) custom-call(f32[4,16,128,128]{3,2,1,0:T(8,128)} %tr.5, f32[16,128,128]{2,1,0:T(8,128)} %fill.5, s32[16,128,128]{2,1,0:T(8,128)} %mask.5, f32[16,128,128]{2,1,0:T(8,128)} %north.5), custom_call_target="tpu_custom_call" | custom-call | flops 1000000 | bytes 1048576 | tf_op jit(solution)/shard_map/rows/pallas_call | solution.py:111
  28.2 1.5 %collective-permute-start.2 = (f32[96,128]{1,0:T(8,128)S(1)}, f32[96,128]{1,0:T(8,128)S(1)}, u32[]{:S(2)}, u32[]{:S(2)}) collective-permute-start(f32[96,128]{1,0:T(8,128)S(1)} %get-tuple-element.17.ns_fwd), channel_id=1, source_target_pairs={{0,1},{1,2},{2,3},{3,4},{4,5},{5,6},{6,7},{7,8},{8,9},{9,10},{10,1... | collective-permute-start | bytes 147464 | tf_op jit(solution)/shard_map/ppermute | solution.py:641
  29.7 1.3 %collective-permute-start.3 = (f32[96,128]{1,0:T(8,128)S(1)}, f32[96,128]{1,0:T(8,128)S(1)}, u32[]{:S(2)}, u32[]{:S(2)}) collective-permute-start(f32[96,128]{1,0:T(8,128)S(1)} %get-tuple-element.18.ns_bwd), channel_id=1, source_target_pairs={{1,0},{2,1},{3,2},{4,3},{5,4},{6,5},{7,6},{8,7},{9,8},{10,9},{11,1... | collective-permute-start | bytes 147464 | tf_op jit(solution)/shard_map/ppermute | solution.py:642
  31.0 0.0 collective-permute-done.2.got_fwd
  31.0 3.9 %collective-permute-done.3.got_bwd = f32[96,128]{1,0:T(8,128)S(1)} collective-permute-done((f32[96,128]{1,0:T(8,128)S(1)}, f32[96,128]{1,0:T(8,128)S(1)}, u32[]{:S(2)}, u32[]{:S(2)}) %collective-permute-start.3) | collective-permute-done | bytes 49184 | tf_op jit(solution)/shard_map/ppermute | solution.py:642
  34.9 0.0 collective-permute-done.1.from_west
  34.9 0.0 collective-permute-done.from_east
  34.9 5.5 %second.1 = (f32[5120,128]{1,0:T(8,128)}, f32[16,8,128]{2,1,0:T(8,128)S(1)}, f32[2,64,128]{2,1,0:T(8,128)S(1)}) custom-call(f32[4,512,128]{2,1,0:T(8,128)S(1)} %get-tuple-element.14.num2, f32[512,128]{1,0:T(8,128)S(1)} %get-tuple-element.15.den2, f32[24,8,128]{2,1,0:T(8,128)S(1)} %get-tuple-element.16.ew, f32[24,8,128]{2,1,0:T(8,128)S(1)} %collective-permute-done.from_east, ...), custom_call_target="tpu_custom_call" | custom-call | flops 60000000 | bytes 6291456 | tf_op jit(solution)/shard_map/second/pallas_call | solution.py:453
  40.4 13.6 %all-to-all-start = ((f32[128,40,128]{2,1,0:T(8,128)}), f32[128,40,128]{2,1,0:T(8,128)S(1)}, u32[]{:S(2)}, u32[]{:S(2)}) async-start(f32[128,40,128]{2,1,0:T(8,128)} %bitcast.6), calls=%async_computation | async-start | bytes 5242880 | tf_op jit(solution)/shard_map/all_to_all | solution.py:650
  54.0 55.8 %third.1 = f32[4,16,128,128]{3,2,1,0:T(8,128)} custom-call(f32[4,16,128,128]{3,2,1,0:T(8,128)} %tr.5, f32[16,128,128]{2,1,0:T(8,128)} %fill.5, s32[16,128,128]{2,1,0:T(8,128)} %mask.5, f32[16,128,128]{2,1,0:T(8,128)} %east.3, f32[16,128,128]{2,1,0:T(8,128)} %north.5, f32[16]{0:T(128)} %diff.5, f32[128,128]{1,0:T(8,128)} %area.3, ...), custom_call_target="tpu_custom_call" | custom-call | flops 60000000 | bytes 12582912 | tf_op jit(solution)/shard_map/third/pallas_call | solution.py:566
  109.7 0.0 all-to-all-done
  109.7 2.0 %last.1 = (f32[256,2048]{1,0:T(8,128)}, f32[256,512]{1,0:T(8,128)}) custom-call(f32[5120,128]{1,0:T(8,128)S(1)} %bitcast.5), custom_call_target="tpu_custom_call" | custom-call | tf_op jit(solution)/shard_map/last/pallas_call | solution.py:603
Async XLA Ops:
  22.7 12.1 %collective-permute-start.1 = (f32[24,8,128]{2,1,0:T(8,128)S(1)}, f32[24,8,128]{2,1,0:T(8,128)S(1)}, u32[]{:S(2)}, u32[]{:S(2)}) collective-permute-start(f32[24,8,128]{2,1,0:T(8,128)S(1)} %get-tuple-element.16.ew), channel_id=1, source_target_pairs={{0,16},{16,32},{32,48},{48,64},{64,80},{80,96},{96,112},{112,0},{1... | collective-permute-start | bytes 294920 | tf_op jit(solution)/shard_map/ppermute | solution.py:645
  24.4 10.5 %collective-permute-start = (f32[24,8,128]{2,1,0:T(8,128)S(1)}, f32[24,8,128]{2,1,0:T(8,128)S(1)}, u32[]{:S(2)}, u32[]{:S(2)}) collective-permute-start(f32[24,8,128]{2,1,0:T(8,128)S(1)} %get-tuple-element.16.ew), channel_id=1, source_target_pairs={{16,0},{32,16},{48,32},{64,48},{80,64},{96,80},{112,96},{0,112},{1... | collective-permute-start | bytes 294920 | tf_op jit(solution)/shard_map/ppermute | solution.py:646
  28.2 2.8 %collective-permute-start.2 = (f32[96,128]{1,0:T(8,128)S(1)}, f32[96,128]{1,0:T(8,128)S(1)}, u32[]{:S(2)}, u32[]{:S(2)}) collective-permute-start(f32[96,128]{1,0:T(8,128)S(1)} %get-tuple-element.17.ns_fwd), channel_id=1, source_target_pairs={{0,1},{1,2},{2,3},{3,4},{4,5},{5,6},{6,7},{7,8},{8,9},{9,10},{10,1... | collective-permute-start | bytes 147464 | tf_op jit(solution)/shard_map/ppermute | solution.py:641
  29.7 5.2 %collective-permute-start.3 = (f32[96,128]{1,0:T(8,128)S(1)}, f32[96,128]{1,0:T(8,128)S(1)}, u32[]{:S(2)}, u32[]{:S(2)}) collective-permute-start(f32[96,128]{1,0:T(8,128)S(1)} %get-tuple-element.18.ns_bwd), channel_id=1, source_target_pairs={{1,0},{2,1},{3,2},{4,3},{5,4},{6,5},{7,6},{8,7},{9,8},{10,9},{11,1... | collective-permute-start | bytes 147464 | tf_op jit(solution)/shard_map/ppermute | solution.py:642
  40.4 69.4 %all-to-all-start = ((f32[128,40,128]{2,1,0:T(8,128)}), f32[128,40,128]{2,1,0:T(8,128)S(1)}, u32[]{:S(2)}, u32[]{:S(2)}) async-start(f32[128,40,128]{2,1,0:T(8,128)} %bitcast.6), calls=%async_computation | async-start | bytes 5242880 | tf_op jit(solution)/shard_map/all_to_all | solution.py:650

commit v3 on v2

--- a/solution.py
+++ b/solution.py
@@ -12,7 +12,7 @@
 
 TR, LV = 4, 16
 ROWS, LANES = 128, 128
-GROUPS = 8
+GROUPS = 16
 DEV, CAP = 128, 2
 CHUNKS = 20
 PARTS = 2
@@ -129,7 +129,8 @@
 def kernel_first(
     tr, fill, mask, east, north, diff, area, owner,
     num2, den2, ew, placing,
-    tr_s, fill_s, mask_s, east_s, north_s, area_s, owner_s, even_s, odd_s, sems, area_sem, owner_sem,
+    tr_s, fill_s, mask_s, east_s, north_s, area_s, owner_s, h_s, g_s, face_s, coef, store, cross,
+    sems, area_sem, owner_sem,
 ):
     hbm, vmem = (tr, fill, mask, east, north), (tr_s, fill_s, mask_s, east_s, north_s)
     copies = input_copies(hbm, vmem, sems)
@@ -147,6 +148,9 @@
     source = sub_iota((256, 128))
     target = lane_iota((256, 128))
     pool = jnp.where(target == (source >> 7) * 64 + ((source & 127) >> 1), 1.0, 0.0).astype(BF16)
+    beside = (source >> 7) * 64 + (((source & 127) + 1) >> 1) - jnp.where((source & 1) == 0, 1, 0)
+    inside = ((source & 127) != 0) & ((source & 127) != 127)
+    pool_cross = jnp.where((target == beside) & inside, 1.0, 0.0).astype(BF16)
     owner_copy.wait()
     who_row = owner_s[...]
     who = jnp.sum(jnp.where(down == across, who_row, 0), axis=1, keepdims=True)
@@ -163,9 +167,8 @@
     is_even = (lane & 1) == 0
     not_last = lane < 127
     not_top = sub < 7
-    swap = jnp.where(is_even, lane + 127, lane + 1) & 127
-
-    def level(k, store):
+
+    def level(k):
         mixing = diff[k]
 
         def load(ref, start):
@@ -174,102 +177,111 @@
         def depth(start):
             return load(fill_s, start) * load(mask_s, start).astype(F32)
 
-        def north_face(q, h, v):
-            if q < 3:
-                return face(h, depth(32 * q + 4), v, load(north_s, 32 * q + 4), mixing)
-            h_up, v_up = pltpu.roll(depth(96), 7, 0), pltpu.roll(load(north_s, 96), 7, 0)
-            return face(h, h_up, v, v_up, mixing, keep=not_top)
+        for v in range(16):
+            start = 32 * (v // 4) + v % 4
+            h, u = depth(start), load(east_s, start)
+            base = 64 * (v % 2)
+            packed = ew[16 + v // 2]
+            packed = jnp.where(
+                (lane >> 1) == k + base // 2, pltpu.roll(h, 2 * k + 1 + base, 1), packed
+            )
+            ew[16 + v // 2] = jnp.where(
+                (lane >> 1) == k + 16 + base // 2, pltpu.roll(u, 2 * k + 33 + base, 1), packed
+            )
+            p_e, q_e = face(
+                h, pltpu.roll(h, 127, 1), u, pltpu.roll(u, 127, 1), mixing, keep=not_last
+            )
+            h_s[v] = h
+            g_s[v] = (time_step * h) / jnp.maximum(h, depth_floor)
+            face_s[0, v] = p_e
+            face_s[1, v] = q_e
+
+        for v in range(16):
+            q, j = v // 4, v % 4
+            start = 32 * q + j
+            h, speed = h_s[v], load(north_s, start)
+            if j < 3:
+                p_n, q_n = face(h, h_s[v + 1], speed, load(north_s, start + 1), mixing)
+            elif q < 3:
+                p_n, q_n = face(h, depth(start + 1), speed, load(north_s, start + 1), mixing)
+            else:
+                h_up, speed_up = pltpu.roll(h_s[12], 7, 0), pltpu.roll(load(north_s, 96), 7, 0)
+                p_n, q_n = face(h, h_up, speed, speed_up, mixing, keep=not_top)
+            face_s[2, v] = p_n
+            face_s[3, v] = q_n
+
+        for q in range(4):
+            south = []
+            for n in (2, 3):
+                low = pltpu.roll(face_s[n, 4 * q + 3], 1, 0)
+                under = pltpu.roll(face_s[n, 4 * q - 1], 1, 0) if q else 0.0
+                south.append(jnp.where(sub > 0, low, under))
+            for par in range(2):
+                centre, weight = [], 0.0
+                for n in range(2):
+                    v = 4 * q + 2 * par + n
+                    h, g = h_s[v], g_s[v]
+                    w = area_s[row_set(32 * q + 2 * par + n)] * h
+                    p_e, q_w = face_s[0, v], pltpu.roll(face_s[1, v], 1, 1)
+                    p_n, q_n = face_s[2, v], face_s[3, v]
+                    p_s, q_s = south if v % 4 == 0 else (face_s[2, v - 1], face_s[3, v - 1])
+                    to_west = pltpu.roll(g, 1, 1) * q_w
+                    to_east = pltpu.roll(g, 127, 1) * p_e
+                    own = w - g * ((p_e + q_w) + (p_n + q_s))
+                    centre.append(own + jnp.where(is_even, to_east, to_west))
+                    coef[4 + n, 2 * q + par] = jnp.where(is_even, to_west, to_east)
+                    if n == 0:
+                        low, up = g * p_s, g * q_n
+                    else:
+                        down, high = g * p_s, g * q_n
+                    weight = weight + w
+                coef[0, 2 * q + par] = low
+                coef[1, 2 * q + par] = centre[0] + down
+                coef[2, 2 * q + par] = centre[1] + up
+                coef[3, 2 * q + par] = high
+                store[pl.ds(128 + q * 8, 8), pl.ds(par * 128, 128)] = weight
 
         where_t = [(lane >> 1) == t * 16 + k for t in range(TR)]
-        before = jnp.zeros((8, 128), F32), jnp.zeros((8, 128), F32)
         for q in range(4):
-            hs = [depth(32 * q + j) for j in range(4)]
-            vs = [load(north_s, 32 * q + j) for j in range(4)]
-            norths = [face(hs[j], hs[j + 1], vs[j], vs[j + 1], mixing) for j in range(3)]
-            norths.append(north_face(q, hs[3], vs[3]))
-            turned = tuple(pltpu.roll(x, 1, 0) for x in norths[3])
-            south = tuple(jnp.where(sub > 0, a, b) for a, b in zip(turned, before))
-            before = turned
-            centre, cross, gain_n, gain_s, weights = [], [], [], [], []
-            for j in range(4):
-                v = 4 * q + j
-                h = hs[j]
-                u = load(east_s, 32 * q + j)
-                base = 64 * (v % 2)
-                packed = ew[16 + v // 2]
-                packed = jnp.where(
-                    (lane >> 1) == k + base // 2, pltpu.roll(h, 2 * k + 1 + base, 1), packed
-                )
-                ew[16 + v // 2] = jnp.where(
-                    (lane >> 1) == k + 16 + base // 2, pltpu.roll(u, 2 * k + 33 + base, 1), packed
-                )
-                w = area_s[row_set(32 * q + j)] * h
-                g = (time_step * h) / jnp.maximum(h, depth_floor)
-                p_e, q_e = face(
-                    h, pltpu.roll(h, 127, 1), u, pltpu.roll(u, 127, 1), mixing, keep=not_last
-                )
-                q_w = pltpu.roll(q_e, 1, 1)
-                p_n, q_n = norths[j]
-                p_s, q_s = norths[j - 1] if j else south
-                to_west = pltpu.roll(g, 1, 1) * q_w
-                to_east = pltpu.roll(g, 127, 1) * p_e
-                own = w - g * ((p_e + q_w) + (p_n + q_s))
-                centre.append(own + jnp.where(is_even, to_east, to_west))
-                cross.append(jnp.where(is_even, to_west, to_east))
-                gain_n.append(g * q_n)
-                gain_s.append(g * p_s)
-                weights.append(w)
             for j in range(4):
                 packed = ew[4 * q + j]
                 for t in range(TR):
                     cell = tr_s[(t, k, *row_set(32 * q + j))]
                     packed = jnp.where(where_t[t], pltpu.roll(cell, 2 * k + 32 * t + 1, 1), packed)
                 ew[4 * q + j] = packed
-            first = [centre[2 * par] + gain_s[2 * par + 1] for par in range(2)]
-            second = [centre[2 * par + 1] + gain_n[2 * par] for par in range(2)]
-            for t in range(TR):
-                cells = [tr_s[(t, k, *row_set(32 * q + j))] for j in range(4)]
-                if q:
-                    below = tr_s[(t, k, *row_set(32 * q - 1))]
-                else:
-                    below = pltpu.roll(cells[3], 1, 0)
-                if q < 3:
-                    above = tr_s[(t, k, *row_set(32 * q + 4))]
-                else:
-                    above = pltpu.roll(cells[0], 7, 0)
-                around = [below, *cells, above]
-                for par in range(2):
-                    low, a, b, high = around[2 * par : 2 * par + 4]
-                    value = (first[par] * a + second[par] * b) + (
-                        gain_s[2 * par] * low + gain_n[2 * par + 1] * high
-                    )
-                    side = cross[2 * par] * a + cross[2 * par + 1] * b
-                    value = value + jnp.take_along_axis(side, swap, axis=1)
+            for par in range(2):
+                low_c, a_c, b_c, high_c, a_x, b_x = [coef[n, 2 * q + par] for n in range(6)]
+                for t in range(TR):
+                    cell = lambda start: tr_s[(t, k, *row_set(start))]
+                    start = 32 * q + 2 * par
+                    a, b = cell(start), cell(start + 1)
+                    low = cell(start - 1) if start else pltpu.roll(cell(3), 1, 0)
+                    high = cell(start + 2) if start < 98 else pltpu.roll(cell(96), 7, 0)
+                    side = a_x * a + b_x * b
+                    value = (a_c * a + b_c * b) + (low_c * low + high_c * high)
+                    cross[pl.ds(t * 32 + q * 8, 8), pl.ds(par * 128, 128)] = side
                     store[pl.ds(t * 32 + q * 8, 8), pl.ds(par * 128, 128)] = value
-            for par in range(2):
-                store[pl.ds(128 + q * 8, 8), pl.ds(par * 128, 128)] = (
-                    weights[2 * par] + weights[2 * par + 1]
-                )
-
-    def pooled(k, store):
+
+    def pooled(k):
         values = split_dot(store[...], pool)
+        sides = split_dot(cross[...], pool_cross)
         rows = pl.ds(pl.multiple_of(k * 32, 32), 32)
         for t in range(TR):
-            num2[t, rows, :] = values[t * 32 : t * 32 + 32]
+            part = slice(t * 32, t * 32 + 32)
+            num2[t, rows, :] = values[part] + sides[part]
         den2[rows, :] = values[128:160]
 
-    def group_body(group, carry):
-        for copy in copies(group):
+    def group_body(k, carry):
+        for copy in copies(k):
             copy.wait()
-        pooled((group * 2 + LV - 1) % LV, odd_s)
-        level(group * 2, even_s)
-        pooled(group * 2, even_s)
-        level(group * 2 + 1, odd_s)
+        pooled((k + LV - 1) % LV)
+        level(k)
         return carry
 
-    odd_s[...] = jnp.zeros_like(odd_s)
-    lax.fori_loop(0, GROUPS, group_body, 0)
-    pooled(LV - 1, odd_s)
+    store[...] = jnp.zeros_like(store)
+    cross[...] = jnp.zeros_like(cross)
+    lax.fori_loop(0, LV, group_body, 0)
+    pooled(LV - 1)
 
 
 def kernel_first_call(tracers, fill, mask, east, north, diff, area, owner):
@@ -294,8 +306,12 @@
             pltpu.VMEM((LV, ROWS, LANES), F32),
             pltpu.VMEM((ROWS, LANES), F32),
             pltpu.VMEM((1, DEV), jnp.int32),
+            pltpu.VMEM((16, 8, 128), F32),
+            pltpu.VMEM((16, 8, 128), F32),
+            pltpu.VMEM((4, 16, 8, 128), F32),
+            pltpu.VMEM((6, 8, 8, 128), F32),
             pltpu.VMEM((160, 256), F32),
-            pltpu.VMEM((160, 256), F32),
+            pltpu.VMEM((128, 256), F32),
             pltpu.SemaphoreType.DMA((5, GROUPS)),
             pltpu.SemaphoreType.DMA,
             pltpu.SemaphoreType.DMA,

time: 112 us -> 79.9 us (0.71)
  Pallas kernels: 86.5 us -> 51.7 us
  waiting for transfers between devices: 3.92 us -> 6.71 us
    pallas_call x1, Pallas kernels: 55.8 us -> 32.9 us  [kernel_third_call(): pl.pallas_call(kernel_third, name='third', out_shape=jax.ShapeDtypeStruct...]
    pallas_call x1, Pallas kernels: 22.1 us -> 10.1 us  [kernel_first_call(): pl.pallas_call(kernel_first, name='first', out_shape=(jax.ShapeDtypeStruc...]
    all_to_all x1, waiting for transfers between devices: 0.01 us -> 2.8 us  [local(): lax.all_to_all(send.reshape(DEV, CAP * CHUNKS, 128), both, split_axis=0,...]
  transfers between devices with their start and end apart: 5 -> 5, of which waited for: 1 -> 2; matrix products, arithmetic and copies ran while one was open for 0% -> 0% of each run, Pallas kernels for 51% -> 43%
where the time goes in v3:
time: 79.9 us; the launch traced here: 79.7 us
  Pallas kernels  51.7 us (65%)
  starting transfers between devices  20.6 us (26%)
  waiting for transfers between devices  6.71 us (8%)
    pallas_call x1, Pallas kernels, kernel_third_call(): pl.pallas_call(kernel_third, name='third', out_shape=jax.ShapeDtypeStruct...  32.9 us
    all_to_all x1, starting transfers between devices, local(): lax.all_to_all(send.reshape(DEV, CAP * CHUNKS, 128), both, split_axis=0,...  13.6 us
    pallas_call x1, Pallas kernels, kernel_first_call(): pl.pallas_call(kernel_first, name='first', out_shape=(jax.ShapeDtypeStruc...  10.1 us
    pallas_call x1, Pallas kernels, kernel_second_call(): pl.pallas_call(kernel_second, name='second', out_shape=(pltpu.HBM((DEV *...  5.46 us
    ppermute x1, waiting for transfers between devices, local(): got_bwd = lax.ppermute(ns_bwd, both, [(b, a) for a, b in chain])  3.91 us
    all_to_all x1, waiting for transfers between devices, local(): lax.all_to_all(send.reshape(DEV, CAP * CHUNKS, 128), both, split_axis=0,...  2.8 us
    ppermute x1, starting transfers between devices, local(): from_east = lax.ppermute(ew, 'lon', [(b, a) for a, b in ring])  2.53 us
    pallas_call x1, Pallas kernels, kernel_last_call(): pl.pallas_call(kernel_last, name='last', grid=(SPLITS,), out_shape=(jax.S...  1.96 us
  transfers between devices with their start and end apart: 5, of which 2 were waited for; matrix products, arithmetic and copies ran while one was open for 0% of the time, Pallas kernels for 43%

profile of v3, /device:TPU:0, one launch (start us, length us, event | category | flops | bytes accessed | tf_op | source)
XLA Modules:
  0.0 79.7 jit_solution(6860866878617009557)
XLA Ops:
  0.6 10.1 %first.1 = (f32[4,512,128]{2,1,0:T(8,128)S(1)}, f32[512,128]{1,0:T(8,128)S(1)}, f32[24,8,128]{2,1,0:T(8,128)S(1)}, bf16[256,256]{1,0:T(8,128)(2,1)S(1)}) custom-call(f32[4,16,128,128]{3,2,1,0:T(8,128)} %tr.5, f32[16,128,128]{2,1,0:T(8,128)} %fill.5, s32[16,128,128]{2,1,0:T(8,128)} %mask.5, f32[16,128,128]{2,1,0:T(8,128)} %east.3, f32[16,128,128]{2,1,0:T(8,128)} %north.5, ...), custom_call_target="tpu_custom_call" | custom-call | flops 60000000 | bytes 11534336 | tf_op jit(solution)/shard_map/first/pallas_call | solution.py:290
  10.7 1.7 %collective-permute-start.1 = (f32[24,8,128]{2,1,0:T(8,128)S(1)}, f32[24,8,128]{2,1,0:T(8,128)S(1)}, u32[]{:S(2)}, u32[]{:S(2)}) collective-permute-start(f32[24,8,128]{2,1,0:T(8,128)S(1)} %get-tuple-element.16.ew), channel_id=1, source_target_pairs={{0,16},{16,32},{32,48},{48,64},{64,80},{80,96},{96,112},{112,0},{1... | collective-permute-start | bytes 294920 | tf_op jit(solution)/shard_map/ppermute | solution.py:661
  12.4 2.5 %collective-permute-start = (f32[24,8,128]{2,1,0:T(8,128)S(1)}, f32[24,8,128]{2,1,0:T(8,128)S(1)}, u32[]{:S(2)}, u32[]{:S(2)}) collective-permute-start(f32[24,8,128]{2,1,0:T(8,128)S(1)} %get-tuple-element.16.ew), channel_id=1, source_target_pairs={{16,0},{32,16},{48,32},{64,48},{80,64},{96,80},{112,96},{0,112},{1... | collective-permute-start | bytes 294920 | tf_op jit(solution)/shard_map/ppermute | solution.py:662
  15.0 1.2 %rows.1 = (f32[96,128]{1,0:T(8,128)S(1)}, f32[96,128]{1,0:T(8,128)S(1)}) custom-call(f32[4,16,128,128]{3,2,1,0:T(8,128)} %tr.5, f32[16,128,128]{2,1,0:T(8,128)} %fill.5, s32[16,128,128]{2,1,0:T(8,128)} %mask.5, f32[16,128,128]{2,1,0:T(8,128)} %north.5), custom_call_target="tpu_custom_call" | custom-call | flops 1000000 | bytes 1048576 | tf_op jit(solution)/shard_map/rows/pallas_call | solution.py:111
  16.2 1.5 %collective-permute-start.2 = (f32[96,128]{1,0:T(8,128)S(1)}, f32[96,128]{1,0:T(8,128)S(1)}, u32[]{:S(2)}, u32[]{:S(2)}) collective-permute-start(f32[96,128]{1,0:T(8,128)S(1)} %get-tuple-element.17.ns_fwd), channel_id=1, source_target_pairs={{0,1},{1,2},{2,3},{3,4},{4,5},{5,6},{6,7},{7,8},{8,9},{9,10},{10,1... | collective-permute-start | bytes 147464 | tf_op jit(solution)/shard_map/ppermute | solution.py:657
  17.7 1.3 %collective-permute-start.3 = (f32[96,128]{1,0:T(8,128)S(1)}, f32[96,128]{1,0:T(8,128)S(1)}, u32[]{:S(2)}, u32[]{:S(2)}) collective-permute-start(f32[96,128]{1,0:T(8,128)S(1)} %get-tuple-element.18.ns_bwd), channel_id=1, source_target_pairs={{1,0},{2,1},{3,2},{4,3},{5,4},{6,5},{7,6},{8,7},{9,8},{10,9},{11,1... | collective-permute-start | bytes 147464 | tf_op jit(solution)/shard_map/ppermute | solution.py:658
  19.0 0.0 collective-permute-done.2.got_fwd
  19.0 3.9 %collective-permute-done.3.got_bwd = f32[96,128]{1,0:T(8,128)S(1)} collective-permute-done((f32[96,128]{1,0:T(8,128)S(1)}, f32[96,128]{1,0:T(8,128)S(1)}, u32[]{:S(2)}, u32[]{:S(2)}) %collective-permute-start.3) | collective-permute-done | bytes 49184 | tf_op jit(solution)/shard_map/ppermute | solution.py:658
  22.9 0.0 collective-permute-done.1.from_west
  22.9 0.0 collective-permute-done.from_east
  22.9 5.5 %second.1 = (f32[5120,128]{1,0:T(8,128)}, f32[16,8,128]{2,1,0:T(8,128)S(1)}, f32[2,64,128]{2,1,0:T(8,128)S(1)}) custom-call(f32[4,512,128]{2,1,0:T(8,128)S(1)} %get-tuple-element.14.num2, f32[512,128]{1,0:T(8,128)S(1)} %get-tuple-element.15.den2, f32[24,8,128]{2,1,0:T(8,128)S(1)} %get-tuple-element.16.ew, f32[24,8,128]{2,1,0:T(8,128)S(1)} %collective-permute-done.from_east, ...), custom_call_target="tpu_custom_call" | custom-call | flops 60000000 | bytes 6291456 | tf_op jit(solution)/shard_map/second/pallas_call | solution.py:469
  28.4 13.6 %all-to-all-start = ((f32[128,40,128]{2,1,0:T(8,128)}), f32[128,40,128]{2,1,0:T(8,128)S(1)}, u32[]{:S(2)}, u32[]{:S(2)}) async-start(f32[128,40,128]{2,1,0:T(8,128)} %bitcast.6), calls=%async_computation | async-start | bytes 5242880 | tf_op jit(solution)/shard_map/all_to_all | solution.py:666
  42.0 32.9 %third.1 = f32[4,16,128,128]{3,2,1,0:T(8,128)} custom-call(f32[4,16,128,128]{3,2,1,0:T(8,128)} %tr.5, f32[16,128,128]{2,1,0:T(8,128)} %fill.5, s32[16,128,128]{2,1,0:T(8,128)} %mask.5, f32[16,128,128]{2,1,0:T(8,128)} %east.3, f32[16,128,128]{2,1,0:T(8,128)} %north.5, f32[16]{0:T(128)} %diff.5, f32[128,128]{1,0:T(8,128)} %area.3, ...), custom_call_target="tpu_custom_call" | custom-call | flops 60000000 | bytes 12582912 | tf_op jit(solution)/shard_map/third/pallas_call | solution.py:582
  74.9 2.8 %all-to-all-done = f32[128,40,128]{2,1,0:T(8,128)S(1)} async-done(((f32[128,40,128]{2,1,0:T(8,128)}), f32[128,40,128]{2,1,0:T(8,128)S(1)}, u32[]{:S(2)}, u32[]{:S(2)}) %all-to-all-start) | async-done | bytes 2621472 | tf_op jit(solution)/shard_map/all_to_all | solution.py:666
  77.7 2.0 %last.1 = (f32[256,2048]{1,0:T(8,128)}, f32[256,512]{1,0:T(8,128)}) custom-call(f32[5120,128]{1,0:T(8,128)S(1)} %bitcast.5), custom_call_target="tpu_custom_call" | custom-call | tf_op jit(solution)/shard_map/last/pallas_call | solution.py:619
Async XLA Ops:
  10.7 12.1 %collective-permute-start.1 = (f32[24,8,128]{2,1,0:T(8,128)S(1)}, f32[24,8,128]{2,1,0:T(8,128)S(1)}, u32[]{:S(2)}, u32[]{:S(2)}) collective-permute-start(f32[24,8,128]{2,1,0:T(8,128)S(1)} %get-tuple-element.16.ew), channel_id=1, source_target_pairs={{0,16},{16,32},{32,48},{48,64},{64,80},{80,96},{96,112},{112,0},{1... | collective-permute-start | bytes 294920 | tf_op jit(solution)/shard_map/ppermute | solution.py:661
  12.4 10.5 %collective-permute-start = (f32[24,8,128]{2,1,0:T(8,128)S(1)}, f32[24,8,128]{2,1,0:T(8,128)S(1)}, u32[]{:S(2)}, u32[]{:S(2)}) collective-permute-start(f32[24,8,128]{2,1,0:T(8,128)S(1)} %get-tuple-element.16.ew), channel_id=1, source_target_pairs={{16,0},{32,16},{48,32},{64,48},{80,64},{96,80},{112,96},{0,112},{1... | collective-permute-start | bytes 294920 | tf_op jit(solution)/shard_map/ppermute | solution.py:662
  16.2 2.8 %collective-permute-start.2 = (f32[96,128]{1,0:T(8,128)S(1)}, f32[96,128]{1,0:T(8,128)S(1)}, u32[]{:S(2)}, u32[]{:S(2)}) collective-permute-start(f32[96,128]{1,0:T(8,128)S(1)} %get-tuple-element.17.ns_fwd), channel_id=1, source_target_pairs={{0,1},{1,2},{2,3},{3,4},{4,5},{5,6},{6,7},{7,8},{8,9},{9,10},{10,1... | collective-permute-start | bytes 147464 | tf_op jit(solution)/shard_map/ppermute | solution.py:657
  17.7 5.2 %collective-permute-start.3 = (f32[96,128]{1,0:T(8,128)S(1)}, f32[96,128]{1,0:T(8,128)S(1)}, u32[]{:S(2)}, u32[]{:S(2)}) collective-permute-start(f32[96,128]{1,0:T(8,128)S(1)} %get-tuple-element.18.ns_bwd), channel_id=1, source_target_pairs={{1,0},{2,1},{3,2},{4,3},{5,4},{6,5},{7,6},{8,7},{9,8},{10,9},{11,1... | collective-permute-start | bytes 147464 | tf_op jit(solution)/shard_map/ppermute | solution.py:658
  28.4 49.3 %all-to-all-start = ((f32[128,40,128]{2,1,0:T(8,128)}), f32[128,40,128]{2,1,0:T(8,128)S(1)}, u32[]{:S(2)}, u32[]{:S(2)}) async-start(f32[128,40,128]{2,1,0:T(8,128)} %bitcast.6), calls=%async_computation | async-start | bytes 5242880 | tf_op jit(solution)/shard_map/all_to_all | solution.py:666

commit v4 on v3

--- a/solution.py
+++ b/solution.py
@@ -69,7 +69,7 @@
     return (pl.ds(start, 8, stride=4), slice(None))
 
 
-def kernel_rows(tr, fill, mask, north, ns_fwd, ns_bwd, tr_s, fill_s, mask_s, north_s, sems):
+def kernel_rows(tr, fill, mask, north, ns_one, ns_two, tr_s, fill_s, mask_s, north_s, sems):
     copies = []
     for n, (src, dst) in enumerate(((tr, tr_s), (fill, fill_s), (mask, mask_s), (north, north_s))):
         for side in range(2):
@@ -85,7 +85,7 @@
             copies[-1].start()
     for copy in copies:
         copy.wait()
-    flip = lax.axis_index("lon") >= lax.axis_size("lon") // 2
+    odd = lax.axis_index("lat") % 2 == 1
     for n in range(6):
         for half in range(2):
             levels = range(8 * half, 8 * half + 8)
@@ -101,8 +101,8 @@
                     parts = [pick(north_s, k) for k in levels]
                 lines.append(jnp.concatenate(parts, axis=0))
             at = pl.ds(n * 16 + 8 * half, 8)
-            ns_fwd[at, :] = jnp.where(flip, lines[0], lines[1])
-            ns_bwd[at, :] = jnp.where(flip, lines[1], lines[0])
+            ns_one[at, :] = jnp.where(odd, lines[0], lines[1])
+            ns_two[at, :] = jnp.where(odd, lines[1], lines[0])
 
 
 def kernel_rows_call(tracers, fill, mask, north):
@@ -327,12 +327,13 @@
 
 
 def kernel_second(
-    num2, den2, ew, from_east, from_west, ns_fwd, ns_bwd, got_fwd, got_bwd, diff, placing,
+    num2, den2, ew, ew_one, ew_two, ns_one, ns_two, got_one, got_two, diff, placing,
     send, d_ew, d_ns,
     work, acc, chunks, send_s, sems,
 ):
     lane, sub = lane_iota(), sub_iota()
-    flip = lax.axis_index("lon") >= lax.axis_size("lon") // 2
+    odd = lax.axis_index("lat") % 2 == 1
+    odd_lon = lax.axis_index("lon") % 2 == 1
     at_fold = lax.axis_index("lat") == lax.axis_size("lat") - 1
     is_east = (lane & 1) == 0
     level_of = (lane >> 1) & 15
@@ -341,9 +342,9 @@
         mixing = jnp.where(level_of == k, diff[k], mixing)
 
     def neighbour(n):
-        return jnp.where(
-            is_east, pltpu.roll(from_east[n], 127, 1), pltpu.roll(from_west[n], 1, 1)
-        )
+        one, two = ew_one[n], ew_two[n]
+        from_east, from_west = jnp.where(odd_lon, two, one), jnp.where(odd_lon, one, two)
+        return jnp.where(is_east, pltpu.roll(from_east, 127, 1), pltpu.roll(from_west, 1, 1))
 
     pending = None
     for v in range(16):
@@ -397,13 +398,13 @@
             return ref[pl.ds(n * 16 + 8 * half, 8), :]
 
         def own(n, top):
-            pair = (ns_bwd, ns_fwd) if top else (ns_fwd, ns_bwd)
-            return jnp.where(flip, rows_of(pair[0], n), rows_of(pair[1], n))
+            pair = (ns_two, ns_one) if top else (ns_one, ns_two)
+            return jnp.where(odd, rows_of(pair[0], n), rows_of(pair[1], n))
 
         def near(n, top, sign=1.0):
             if not top:
-                return jnp.where(flip, rows_of(got_bwd, n), rows_of(got_fwd, n))
-            value = jnp.where(flip, rows_of(got_fwd, n), rows_of(got_bwd, n))
+                return jnp.where(odd, rows_of(got_one, n), rows_of(got_two, n))
+            value = jnp.where(odd, rows_of(got_two, n), rows_of(got_one, n))
             turned = sign * jnp.take_along_axis(value, back, axis=1)
             return jnp.where(at_fold, turned, value)
 
@@ -646,22 +647,30 @@
         )
     )
     tracers, fill_fraction, ocean_mask, east_speed, north_speed = fields
-    ns_fwd, ns_bwd = kernel_rows_call(tracers, fill_fraction, ocean_mask, north_speed)
+    ns_one, ns_two = kernel_rows_call(tracers, fill_fraction, ocean_mask, north_speed)
     both = ("lon", "lat")
-    chain = []
-    for low in range(lon_count // 2):
-        high = lon_count - 1 - low
-        up = [low * lat_count + a for a in range(lat_count)]
-        path = up + [high * lat_count + a for a in reversed(range(lat_count))]
-        chain += list(zip(path[:-1], path[1:]))
-    got_fwd = lax.ppermute(ns_fwd, both, chain)
-    got_bwd = lax.ppermute(ns_bwd, both, [(b, a) for a, b in chain])
+
+    def swapped(pairs):
+        return [pair for a, b in pairs for pair in ((a, b), (b, a))]
+
+    def at(lon, lat):
+        return lon * lat_count + lat
+
+    lons = range(lon_count)
+    step_one = [(at(n, a), at(n, a + 1)) for n in lons for a in range(0, lat_count, 2)]
+    step_two = [(at(n, a), at(n, a + 1)) for n in lons for a in range(1, lat_count - 1, 2)]
+    fold = [
+        (at(n, lat_count - 1), at(lon_count - 1 - n, lat_count - 1)) for n in range(lon_count // 2)
+    ]
+    got_one = lax.ppermute(ns_one, both, swapped(step_one))
+    got_two = lax.ppermute(ns_two, both, swapped(step_two + fold))
     num2, den2, ew, placing = kernel_first_call(*fields, diffusivity, cell_area, owners)
-    ring = [(i, (i + 1) % lon_count) for i in range(lon_count)]
-    from_west = lax.ppermute(ew, "lon", ring)
-    from_east = lax.ppermute(ew, "lon", [(b, a) for a, b in ring])
+    ew_one = lax.ppermute(ew, "lon", swapped([(n, n + 1) for n in range(0, lon_count, 2)]))
+    ew_two = lax.ppermute(
+        ew, "lon", swapped([(n, (n + 1) % lon_count) for n in range(1, lon_count, 2)])
+    )
     send, d_ew, d_ns = kernel_second_call(
-        num2, den2, ew, from_east, from_west, ns_fwd, ns_bwd, got_fwd, got_bwd, diffusivity, placing
+        num2, den2, ew, ew_one, ew_two, ns_one, ns_two, got_one, got_two, diffusivity, placing
     )
     got = lax.all_to_all(
         send.reshape(DEV, CAP * CHUNKS, 128), both, split_axis=0, concat_axis=0, tiled=True

time: 79.9 us -> 76.3 us (0.955)
  starting transfers between devices: 20.6 us -> 18.3 us
  waiting for transfers between devices: 6.71 us -> 5.39 us
    ppermute x4, starting transfers between devices: 6.96 us -> 4.88 us  [the longest x1 4.13 us: local(): lax.ppermute(ew, 'lon', swapped([(n, (n + 1) % lon_count) for n in range(...]
    ppermute x4, waiting for transfers between devices: 3.92 us -> 2.6 us  [the longest x1 1.35 us: local(): lax.ppermute(ew, 'lon', swapped([(n, n + 1) for n in range(0, lon_count,...]
  transfers between devices with their start and end apart: 5 -> 5, of which waited for: 2 -> 4; matrix products, arithmetic and copies ran while one was open for 0% -> 0% of each run, Pallas kernels for 43% -> 45%
where the time goes in v4:
time: 76.3 us; the launch traced here: 76 us
  Pallas kernels  51.6 us (68%)
  starting transfers between devices  18.3 us (24%)
  waiting for transfers between devices  5.39 us (7%)
    pallas_call x1, Pallas kernels, kernel_third_call(): pl.pallas_call(kernel_third, name='third', out_shape=jax.ShapeDtypeStruct...  32.9 us
    all_to_all x1, starting transfers between devices, local(): lax.all_to_all(send.reshape(DEV, CAP * CHUNKS, 128), both, split_axis=0,...  13.5 us
    pallas_call x1, Pallas kernels, kernel_first_call(): pl.pallas_call(kernel_first, name='first', out_shape=(jax.ShapeDtypeStruc...  10.1 us
    pallas_call x1, Pallas kernels, kernel_second_call(): pl.pallas_call(kernel_second, name='second', out_shape=(pltpu.HBM((DEV *...  5.37 us
    ppermute x1, starting transfers between devices, local(): lax.ppermute(ew, 'lon', swapped([(n, (n + 1) % lon_count) for n in range(...  4.13 us
    all_to_all x1, waiting for transfers between devices, local(): lax.all_to_all(send.reshape(DEV, CAP * CHUNKS, 128), both, split_axis=0,...  2.8 us
    pallas_call x1, Pallas kernels, kernel_last_call(): pl.pallas_call(kernel_last, name='last', grid=(SPLITS,), out_shape=(jax.S...  1.96 us
  transfers between devices with their start and end apart: 5, of which 4 were waited for; matrix products, arithmetic and copies ran while one was open for 0% of the time, Pallas kernels for 45%

profile of v4, /device:TPU:0, one launch (start us, length us, event | category | flops | bytes accessed | tf_op | source)
XLA Modules:
  0.0 76.0 jit_solution(277586817723758634)
XLA Ops:
  0.6 10.1 %first.1 = (f32[4,512,128]{2,1,0:T(8,128)S(1)}, f32[512,128]{1,0:T(8,128)S(1)}, f32[24,8,128]{2,1,0:T(8,128)S(1)}, bf16[256,256]{1,0:T(8,128)(2,1)S(1)}) custom-call(f32[4,16,128,128]{3,2,1,0:T(8,128)} %tr.5, f32[16,128,128]{2,1,0:T(8,128)} %fill.5, s32[16,128,128]{2,1,0:T(8,128)} %mask.5, f32[16,128,128]{2,1,0:T(8,128)} %east.3, f32[16,128,128]{2,1,0:T(8,128)} %north.5, ...), custom_call_target="tpu_custom_call" | custom-call | flops 60000000 | bytes 11534336 | tf_op jit(solution)/shard_map/first/pallas_call | solution.py:290
  10.7 4.1 %collective-permute-start.1 = (f32[24,8,128]{2,1,0:T(8,128)S(1)}, f32[24,8,128]{2,1,0:T(8,128)S(1)}, u32[]{:S(2)}, u32[]{:S(2)}) collective-permute-start(f32[24,8,128]{2,1,0:T(8,128)S(1)} %get-tuple-element.16.ew), channel_id=1, source_target_pairs={{16,32},{32,16},{48,64},{64,48},{80,96},{96,80},{112,0},{0,112},{1... | collective-permute-start | bytes 294920 | tf_op jit(solution)/shard_map/ppermute | solution.py:669
  14.9 0.0 collective-permute-start
  14.9 1.2 %rows.1 = (f32[96,128]{1,0:T(8,128)S(1)}, f32[96,128]{1,0:T(8,128)S(1)}) custom-call(f32[4,16,128,128]{3,2,1,0:T(8,128)} %tr.5, f32[16,128,128]{2,1,0:T(8,128)} %fill.5, s32[16,128,128]{2,1,0:T(8,128)} %mask.5, f32[16,128,128]{2,1,0:T(8,128)} %north.5), custom_call_target="tpu_custom_call" | custom-call | flops 1000000 | bytes 1048576 | tf_op jit(solution)/shard_map/rows/pallas_call | solution.py:111
  16.1 0.1 collective-permute-start.2
  16.2 0.7 collective-permute-start.3
  16.9 0.5 collective-permute-done.2.got_one
  17.4 0.0 collective-permute-done.3.got_two
  17.4 0.7 collective-permute-done.1.ew_two
  18.1 1.4 %collective-permute-done.ew_one = f32[24,8,128]{2,1,0:T(8,128)S(1)} collective-permute-done((f32[24,8,128]{2,1,0:T(8,128)S(1)}, f32[24,8,128]{2,1,0:T(8,128)S(1)}, u32[]{:S(2)}, u32[]{:S(2)}) %collective-permute-start) | collective-permute-done | bytes 98336 | tf_op jit(solution)/shard_map/ppermute | solution.py:668
  19.5 5.4 %second.1 = (f32[5120,128]{1,0:T(8,128)}, f32[16,8,128]{2,1,0:T(8,128)S(1)}, f32[2,64,128]{2,1,0:T(8,128)S(1)}) custom-call(f32[4,512,128]{2,1,0:T(8,128)S(1)} %get-tuple-element.14.num2, f32[512,128]{1,0:T(8,128)S(1)} %get-tuple-element.15.den2, f32[24,8,128]{2,1,0:T(8,128)S(1)} %get-tuple-element.16.ew, f32[24,8,128]{2,1,0:T(8,128)S(1)} %collective-permute-done.ew_one, ...), custom_call_target="tpu_custom_call" | custom-call | flops 60000000 | bytes 6291456 | tf_op jit(solution)/shard_map/second/pallas_call | solution.py:470
  24.9 13.5 %all-to-all-start = ((f32[128,40,128]{2,1,0:T(8,128)}), f32[128,40,128]{2,1,0:T(8,128)S(1)}, u32[]{:S(2)}, u32[]{:S(2)}) async-start(f32[128,40,128]{2,1,0:T(8,128)} %bitcast.6), calls=%async_computation | async-start | bytes 5242880 | tf_op jit(solution)/shard_map/all_to_all | solution.py:675
  38.3 32.9 %third.1 = f32[4,16,128,128]{3,2,1,0:T(8,128)} custom-call(f32[4,16,128,128]{3,2,1,0:T(8,128)} %tr.5, f32[16,128,128]{2,1,0:T(8,128)} %fill.5, s32[16,128,128]{2,1,0:T(8,128)} %mask.5, f32[16,128,128]{2,1,0:T(8,128)} %east.3, f32[16,128,128]{2,1,0:T(8,128)} %north.5, f32[16]{0:T(128)} %diff.5, f32[128,128]{1,0:T(8,128)} %area.3, ...), custom_call_target="tpu_custom_call" | custom-call | flops 60000000 | bytes 12582912 | tf_op jit(solution)/shard_map/third/pallas_call | solution.py:583
  71.3 2.8 %all-to-all-done = f32[128,40,128]{2,1,0:T(8,128)S(1)} async-done(((f32[128,40,128]{2,1,0:T(8,128)}), f32[128,40,128]{2,1,0:T(8,128)S(1)}, u32[]{:S(2)}, u32[]{:S(2)}) %all-to-all-start) | async-done | bytes 2621472 | tf_op jit(solution)/shard_map/all_to_all | solution.py:675
  74.1 2.0 %last.1 = (f32[256,2048]{1,0:T(8,128)}, f32[256,512]{1,0:T(8,128)}) custom-call(f32[5120,128]{1,0:T(8,128)S(1)} %bitcast.5), custom_call_target="tpu_custom_call" | custom-call | tf_op jit(solution)/shard_map/last/pallas_call | solution.py:620
Async XLA Ops:
  10.7 7.4 %collective-permute-start.1 = (f32[24,8,128]{2,1,0:T(8,128)S(1)}, f32[24,8,128]{2,1,0:T(8,128)S(1)}, u32[]{:S(2)}, u32[]{:S(2)}) collective-permute-start(f32[24,8,128]{2,1,0:T(8,128)S(1)} %get-tuple-element.16.ew), channel_id=1, source_target_pairs={{16,32},{32,16},{48,64},{64,48},{80,96},{96,80},{112,0},{0,112},{1... | collective-permute-start | bytes 294920 | tf_op jit(solution)/shard_map/ppermute | solution.py:669
  14.9 4.6 %collective-permute-start = (f32[24,8,128]{2,1,0:T(8,128)S(1)}, f32[24,8,128]{2,1,0:T(8,128)S(1)}, u32[]{:S(2)}, u32[]{:S(2)}) collective-permute-start(f32[24,8,128]{2,1,0:T(8,128)S(1)} %get-tuple-element.16.ew), channel_id=1, source_target_pairs={{0,16},{16,0},{32,48},{48,32},{64,80},{80,64},{96,112},{112,96},{1... | collective-permute-start | bytes 294920 | tf_op jit(solution)/shard_map/ppermute | solution.py:668
  16.1 1.3 %collective-permute-start.2 = (f32[96,128]{1,0:T(8,128)S(1)}, f32[96,128]{1,0:T(8,128)S(1)}, u32[]{:S(2)}, u32[]{:S(2)}) collective-permute-start(f32[96,128]{1,0:T(8,128)S(1)} %get-tuple-element.17.ns_one), channel_id=1, source_target_pairs={{0,1},{1,0},{2,3},{3,2},{4,5},{5,4},{6,7},{7,6},{8,9},{9,8},{10,11... | collective-permute-start | bytes 147464 | tf_op jit(solution)/shard_map/ppermute | solution.py:665
  16.2 1.2 %collective-permute-start.3 = (f32[96,128]{1,0:T(8,128)S(1)}, f32[96,128]{1,0:T(8,128)S(1)}, u32[]{:S(2)}, u32[]{:S(2)}) collective-permute-start(f32[96,128]{1,0:T(8,128)S(1)} %get-tuple-element.18.ns_two), channel_id=1, source_target_pairs={{1,2},{2,1},{3,4},{4,3},{5,6},{6,5},{7,8},{8,7},{9,10},{10,9},{11,... | collective-permute-start | bytes 147464 | tf_op jit(solution)/shard_map/ppermute | solution.py:666
  24.9 49.2 %all-to-all-start = ((f32[128,40,128]{2,1,0:T(8,128)}), f32[128,40,128]{2,1,0:T(8,128)S(1)}, u32[]{:S(2)}, u32[]{:S(2)}) async-start(f32[128,40,128]{2,1,0:T(8,128)} %bitcast.6), calls=%async_computation | async-start | bytes 5242880 | tf_op jit(solution)/shard_map/all_to_all | solution.py:675

commit v5 on v4

--- a/solution.py
+++ b/solution.py
@@ -126,31 +126,24 @@
     )(tracers, fill, mask, north)
 
 
-def kernel_first(
-    tr, fill, mask, east, north, diff, area, owner,
-    num2, den2, ew, placing,
-    tr_s, fill_s, mask_s, east_s, north_s, area_s, owner_s, h_s, g_s, face_s, coef, store, cross,
-    sems, area_sem, owner_sem,
+def kernel_edges(
+    tr, fill, mask, east, north, area, owner,
+    tr_v, h_v, east_v, north_v, area_v, ew, placing,
+    fill_s, mask_s, owner_s, sems, area_sem, owner_sem,
 ):
-    hbm, vmem = (tr, fill, mask, east, north), (tr_s, fill_s, mask_s, east_s, north_s)
-    copies = input_copies(hbm, vmem, sems)
-    area_copy = pltpu.make_async_copy(area, area_s, area_sem)
+    copies = input_copies(
+        (tr, fill, mask, east, north), (tr_v, fill_s, mask_s, east_v, north_v), sems
+    )
+    area_copy = pltpu.make_async_copy(area, area_v, area_sem)
     owner_copy = pltpu.make_async_copy(owner, owner_s, owner_sem)
     owner_copy.start()
     for group in range(GROUPS):
         for copy in copies(group):
             copy.start()
-        if group == 0:
-            area_copy.start()
+    area_copy.start()
 
     across = lane_iota((DEV, DEV))
     down = sub_iota((DEV, DEV))
-    source = sub_iota((256, 128))
-    target = lane_iota((256, 128))
-    pool = jnp.where(target == (source >> 7) * 64 + ((source & 127) >> 1), 1.0, 0.0).astype(BF16)
-    beside = (source >> 7) * 64 + (((source & 127) + 1) >> 1) - jnp.where((source & 1) == 0, 1, 0)
-    inside = ((source & 127) != 0) & ((source & 127) != 127)
-    pool_cross = jnp.where((target == beside) & inside, 1.0, 0.0).astype(BF16)
     owner_copy.wait()
     who_row = owner_s[...]
     who = jnp.sum(jnp.where(down == across, who_row, 0), axis=1, keepdims=True)
@@ -162,36 +155,95 @@
         placing[pl.ds(part * DEV, DEV), 0:DEV] = here
         placing[pl.ds(part * DEV, DEV), DEV : 2 * DEV] = here
 
-    area_copy.wait()
-    lane, sub = lane_iota(), sub_iota()
-    is_even = (lane & 1) == 0
-    not_last = lane < 127
-    not_top = sub < 7
-
-    def level(k):
-        mixing = diff[k]
-
-        def load(ref, start):
-            return ref[(k, *row_set(start))]
-
-        def depth(start):
-            return load(fill_s, start) * load(mask_s, start).astype(F32)
-
+    lane = lane_iota()
+
+    def level(k, carry):
+        for copy in copies(k):
+            copy.wait()
+        where_t = [(lane >> 1) == t * 16 + k for t in range(TR)]
         for v in range(16):
-            start = 32 * (v // 4) + v % 4
-            h, u = depth(start), load(east_s, start)
+            at = row_set(32 * (v // 4) + v % 4)
+            h = fill_s[(k, *at)] * mask_s[(k, *at)].astype(F32)
+            h_v[k, v] = h
             base = 64 * (v % 2)
             packed = ew[16 + v // 2]
             packed = jnp.where(
                 (lane >> 1) == k + base // 2, pltpu.roll(h, 2 * k + 1 + base, 1), packed
             )
             ew[16 + v // 2] = jnp.where(
-                (lane >> 1) == k + 16 + base // 2, pltpu.roll(u, 2 * k + 33 + base, 1), packed
+                (lane >> 1) == k + 16 + base // 2,
+                pltpu.roll(east_v[(k, *at)], 2 * k + 33 + base, 1),
+                packed,
             )
+            packed = ew[v]
+            for t in range(TR):
+                moved = pltpu.roll(tr_v[(t, k, *at)], 2 * k + 32 * t + 1, 1)
+                packed = jnp.where(where_t[t], moved, packed)
+            ew[v] = packed
+        return carry
+
+    lax.fori_loop(0, LV, level, 0)
+    area_copy.wait()
+
+
+def kernel_edges_call(tracers, fill, mask, east, north, area, owner):
+    hbm = pl.BlockSpec(memory_space=pltpu.HBM)
+    vmem = pl.BlockSpec(memory_space=pltpu.VMEM)
+    return pl.pallas_call(
+        kernel_edges,
+        name="edges",
+        out_shape=(
+            jax.ShapeDtypeStruct((TR, LV, ROWS, LANES), F32),
+            jax.ShapeDtypeStruct((LV, 16, 8, LANES), F32),
+            jax.ShapeDtypeStruct((LV, ROWS, LANES), F32),
+            jax.ShapeDtypeStruct((LV, ROWS, LANES), F32),
+            jax.ShapeDtypeStruct((ROWS, LANES), F32),
+            jax.ShapeDtypeStruct((24, 8, 128), F32),
+            jax.ShapeDtypeStruct((CAP * DEV, 2 * DEV), BF16),
+        ),
+        in_specs=[hbm] * 7,
+        out_specs=(vmem,) * 7,
+        scratch_shapes=[
+            pltpu.VMEM((LV, ROWS, LANES), F32),
+            pltpu.VMEM((LV, ROWS, LANES), jnp.int32),
+            pltpu.VMEM((1, DEV), jnp.int32),
+            pltpu.SemaphoreType.DMA((5, GROUPS)),
+            pltpu.SemaphoreType.DMA,
+            pltpu.SemaphoreType.DMA,
+        ],
+        compiler_params=pltpu.CompilerParams(vmem_limit_bytes=24 * MIB),
+        cost_estimate=pl.CostEstimate(flops=60_000_000, bytes_accessed=11 * MIB, transcendentals=0),
+    )(tracers, fill, mask, east, north, area, owner)
+
+
+def kernel_first(
+    tr_s, h_v, east_s, north_s, area_s, diff,
+    num2, den2,
+    g_s, face_s, coef, store, cross,
+):
+    source = sub_iota((256, 128))
+    target = lane_iota((256, 128))
+    pool = jnp.where(target == (source >> 7) * 64 + ((source & 127) >> 1), 1.0, 0.0).astype(BF16)
+    beside = (source >> 7) * 64 + (((source & 127) + 1) >> 1) - jnp.where((source & 1) == 0, 1, 0)
+    inside = ((source & 127) != 0) & ((source & 127) != 127)
+    pool_cross = jnp.where((target == beside) & inside, 1.0, 0.0).astype(BF16)
+    lane, sub = lane_iota(), sub_iota()
+    is_even = (lane & 1) == 0
+    not_last = lane < 127
+    not_top = sub < 7
+
+    def level(k):
+        mixing = diff[k]
+
+        def load(ref, start):
+            return ref[(k, *row_set(start))]
+
+        for v in range(16):
+            start = 32 * (v // 4) + v % 4
+            h, u = h_v[k, v], load(east_s, start)
             p_e, q_e = face(
                 h, pltpu.roll(h, 127, 1), u, pltpu.roll(u, 127, 1), mixing, keep=not_last
             )
-            h_s[v] = h
             g_s[v] = (time_step * h) / jnp.maximum(h, depth_floor)
             face_s[0, v] = p_e
             face_s[1, v] = q_e
@@ -199,13 +251,16 @@
         for v in range(16):
             q, j = v // 4, v % 4
             start = 32 * q + j
-            h, speed = h_s[v], load(north_s, start)
+            h, speed = h_v[k, v], load(north_s, start)
             if j < 3:
-                p_n, q_n = face(h, h_s[v + 1], speed, load(north_s, start + 1), mixing)
+                p_n, q_n = face(h, h_v[k, v + 1], speed, load(north_s, start + 1), mixing)
             elif q < 3:
-                p_n, q_n = face(h, depth(start + 1), speed, load(north_s, start + 1), mixing)
+                h_up = jnp.where(
+                    sub < 7, pltpu.roll(h_v[k, v - 3], 7, 0), pltpu.roll(h_v[k, v + 1], 7, 0)
+                )
+                p_n, q_n = face(h, h_up, speed, load(north_s, start + 1), mixing)
             else:
-                h_up, speed_up = pltpu.roll(h_s[12], 7, 0), pltpu.roll(load(north_s, 96), 7, 0)
+                h_up, speed_up = pltpu.roll(h_v[k, 12], 7, 0), pltpu.roll(load(north_s, 96), 7, 0)
                 p_n, q_n = face(h, h_up, speed, speed_up, mixing, keep=not_top)
             face_s[2, v] = p_n
             face_s[3, v] = q_n
@@ -220,7 +275,7 @@
                 centre, weight = [], 0.0
                 for n in range(2):
                     v = 4 * q + 2 * par + n
-                    h, g = h_s[v], g_s[v]
+                    h, g = h_v[k, v], g_s[v]
                     w = area_s[row_set(32 * q + 2 * par + n)] * h
                     p_e, q_w = face_s[0, v], pltpu.roll(face_s[1, v], 1, 1)
                     p_n, q_n = face_s[2, v], face_s[3, v]
@@ -241,14 +296,7 @@
                 coef[3, 2 * q + par] = high
                 store[pl.ds(128 + q * 8, 8), pl.ds(par * 128, 128)] = weight
 
-        where_t = [(lane >> 1) == t * 16 + k for t in range(TR)]
         for q in range(4):
-            for j in range(4):
-                packed = ew[4 * q + j]
-                for t in range(TR):
-                    cell = tr_s[(t, k, *row_set(32 * q + j))]
-                    packed = jnp.where(where_t[t], pltpu.roll(cell, 2 * k + 32 * t + 1, 1), packed)
-                ew[4 * q + j] = packed
             for par in range(2):
                 low_c, a_c, b_c, high_c, a_x, b_x = [coef[n, 2 * q + par] for n in range(6)]
                 for t in range(TR):
@@ -272,8 +320,6 @@
         den2[rows, :] = values[128:160]
 
     def group_body(k, carry):
-        for copy in copies(k):
-            copy.wait()
         pooled((k + LV - 1) % LV)
         level(k)
         return carry
@@ -284,8 +330,7 @@
     pooled(LV - 1)
 
 
-def kernel_first_call(tracers, fill, mask, east, north, diff, area, owner):
-    hbm = pl.BlockSpec(memory_space=pltpu.HBM)
+def kernel_first_call(tr_v, h_v, east_v, north_v, area_v, diff):
     vmem = pl.BlockSpec(memory_space=pltpu.VMEM)
     return pl.pallas_call(
         kernel_first,
@@ -293,32 +338,19 @@
         out_shape=(
             jax.ShapeDtypeStruct((TR, 512, 128), F32),
             jax.ShapeDtypeStruct((512, 128), F32),
-            jax.ShapeDtypeStruct((24, 8, 128), F32),
-            jax.ShapeDtypeStruct((CAP * DEV, 2 * DEV), BF16),
         ),
-        in_specs=[hbm] * 5 + [pl.BlockSpec(memory_space=pltpu.SMEM), hbm, hbm],
-        out_specs=(vmem,) * 4,
+        in_specs=[vmem] * 5 + [pl.BlockSpec(memory_space=pltpu.SMEM)],
+        out_specs=(vmem,) * 2,
         scratch_shapes=[
-            pltpu.VMEM((TR, LV, ROWS, LANES), F32),
-            pltpu.VMEM((LV, ROWS, LANES), F32),
-            pltpu.VMEM((LV, ROWS, LANES), jnp.int32),
-            pltpu.VMEM((LV, ROWS, LANES), F32),
-            pltpu.VMEM((LV, ROWS, LANES), F32),
-            pltpu.VMEM((ROWS, LANES), F32),
-            pltpu.VMEM((1, DEV), jnp.int32),
-            pltpu.VMEM((16, 8, 128), F32),
             pltpu.VMEM((16, 8, 128), F32),
             pltpu.VMEM((4, 16, 8, 128), F32),
             pltpu.VMEM((6, 8, 8, 128), F32),
             pltpu.VMEM((160, 256), F32),
             pltpu.VMEM((128, 256), F32),
-            pltpu.SemaphoreType.DMA((5, GROUPS)),
-            pltpu.SemaphoreType.DMA,
-            pltpu.SemaphoreType.DMA,
         ],
-        compiler_params=pltpu.CompilerParams(vmem_limit_bytes=24 * MIB),
+        compiler_params=pltpu.CompilerParams(vmem_limit_bytes=16 * MIB),
         cost_estimate=pl.CostEstimate(flops=60_000_000, bytes_accessed=11 * MIB, transcendentals=0),
-    )(tracers, fill, mask, east, north, diff, area, owner)
+    )(tr_v, h_v, east_v, north_v, area_v, diff)
 
 
 def spread(values, offset):
@@ -492,7 +524,7 @@
 def kernel_third(
     tr, fill, mask, east, north, diff, area, d_ew, d_ns,
     out,
-    tr_s, fill_s, mask_s, east_s, north_s, area_s, out_s, sems, area_sem, out_sems,
+    tr_s, fill_s, mask_s, east_s, north_s, area_s, out_s, moved_s, sems, area_sem, out_sems,
 ):
     hbm, vmem = (tr, fill, mask, east, north), (tr_s, fill_s, mask_s, east_s, north_s)
     copies = input_copies(hbm, vmem, sems)
@@ -520,6 +552,12 @@
 
         def depth(start):
             return load(fill_s, start) * load(mask_s, start).astype(F32)
+
+        for v in range(16):
+            edge = d_ew[v]
+            for t in range(TR):
+                moved = pltpu.roll(edge, 127 - 2 * k + (128 - 32 * t), 1)
+                moved_s[v, t] = jnp.where(ends, moved, 0.0)
 
         before = [jnp.zeros((8, 128), F32)] * TR
         for q in range(4):
@@ -556,8 +594,7 @@
                     cell = cells[j]
                     flux = p_e * cell - q_e * pltpu.roll(cell, 127, 1)
                     div = (pltpu.roll(flux, 1, 1) - flux) + (souths[j] - norths[j])
-                    moved = pltpu.roll(d_ew[4 * q + j], 127 - 2 * k + (128 - 32 * t), 1)
-                    div = div + jnp.where(ends, moved, 0.0)
+                    div = div + moved_s[4 * q + j, t]
                     if q == 0 and j == 0:
                         div = div + jnp.where(sub == 0, d_ns[0, pl.ds(t * 16 + k, 1), :], 0.0)
                     if q == 3 and j == 3:
@@ -594,6 +631,7 @@
             pltpu.VMEM((LV, ROWS, LANES), F32),
             pltpu.VMEM((ROWS, LANES), F32),
             pltpu.VMEM((TR, LV, ROWS, LANES), F32),
+            pltpu.VMEM((16, TR, 8, 128), F32),
             pltpu.SemaphoreType.DMA((5, GROUPS)),
             pltpu.SemaphoreType.DMA,
             pltpu.SemaphoreType.DMA((GROUPS,)),
@@ -664,11 +702,12 @@
     ]
     got_one = lax.ppermute(ns_one, both, swapped(step_one))
     got_two = lax.ppermute(ns_two, both, swapped(step_two + fold))
-    num2, den2, ew, placing = kernel_first_call(*fields, diffusivity, cell_area, owners)
+    *held, ew, placing = kernel_edges_call(*fields, cell_area, owners)
     ew_one = lax.ppermute(ew, "lon", swapped([(n, n + 1) for n in range(0, lon_count, 2)]))
     ew_two = lax.ppermute(
         ew, "lon", swapped([(n, (n + 1) % lon_count) for n in range(1, lon_count, 2)])
     )
+    num2, den2 = kernel_first_call(*held, diffusivity)
     send, d_ew, d_ns = kernel_second_call(
         num2, den2, ew, ew_one, ew_two, ns_one, ns_two, got_one, got_two, diffusivity, placing
     )

time: 76.3 us -> 75.6 us (level)
  Pallas kernels: 51.6 us -> 34.2 us
  waiting for transfers between devices: 5.39 us -> 22.2 us
    all_to_all x1, waiting for transfers between devices: 2.8 us -> 22.2 us  [local(): lax.all_to_all(send.reshape(DEV, CAP * CHUNKS, 128), both, split_axis=0,...]
    pallas_call x1, Pallas kernels: 32.9 us -> 13.5 us  [kernel_third_call(): pl.pallas_call(kernel_third, name='third', out_shape=jax.ShapeDtypeStruct...]
    pallas_call x0 -> x1, Pallas kernels: none -> 6.85 us  [kernel_edges_call(): pl.pallas_call(kernel_edges, name='edges', out_shape=(jax.ShapeDtypeStruc...]
    pallas_call x1, Pallas kernels: 10.1 us -> 5.21 us  [kernel_first_call(): pl.pallas_call(kernel_first, name='first', out_shape=(jax.ShapeDtypeStruc...]
    ppermute x1, waiting for transfers between devices: 1.35 us -> 0.01 us  [local(): lax.ppermute(ew, 'lon', swapped([(n, n + 1) for n in range(0, lon_count,...]
  transfers between devices with their start and end apart: 5 -> 5, of which waited for: 4 -> 1; matrix products, arithmetic and copies ran while one was open for 0% -> 0% of each run, Pallas kernels for 45% -> 27%
where the time goes in v5:
time: 75.6 us; the launch traced here: 75.3 us
  Pallas kernels  34.2 us (45%)
  waiting for transfers between devices  22.2 us (29%)
  starting transfers between devices  18.2 us (24%)
    all_to_all x1, waiting for transfers between devices, local(): lax.all_to_all(send.reshape(DEV, CAP * CHUNKS, 128), both, split_axis=0,...  22.2 us
    pallas_call x1, Pallas kernels, kernel_third_call(): pl.pallas_call(kernel_third, name='third', out_shape=jax.ShapeDtypeStruct...  13.5 us
    all_to_all x1, starting transfers between devices, local(): lax.all_to_all(send.reshape(DEV, CAP * CHUNKS, 128), both, split_axis=0,...  13.3 us
    pallas_call x1, Pallas kernels, kernel_edges_call(): pl.pallas_call(kernel_edges, name='edges', out_shape=(jax.ShapeDtypeStruc...  6.85 us
    pallas_call x1, Pallas kernels, kernel_second_call(): pl.pallas_call(kernel_second, name='second', out_shape=(pltpu.HBM((DEV *...  5.39 us
    pallas_call x1, Pallas kernels, kernel_first_call(): pl.pallas_call(kernel_first, name='first', out_shape=(jax.ShapeDtypeStruc...  5.21 us
    ppermute x1, starting transfers between devices, local(): lax.ppermute(ew, 'lon', swapped([(n, (n + 1) % lon_count) for n in range(...  4.13 us
    pallas_call x1, Pallas kernels, kernel_last_call(): pl.pallas_call(kernel_last, name='last', grid=(SPLITS,), out_shape=(jax.S...  1.96 us
  transfers between devices with their start and end apart: 5, of which 1 were waited for; matrix products, arithmetic and copies ran while one was open for 0% of the time, Pallas kernels for 27%

profile of v5, /device:TPU:0, one launch (start us, length us, event | category | flops | bytes accessed | tf_op | source)
XLA Modules:
  0.0 75.3 jit_solution(6601756795108662214)
XLA Ops:
  0.6 6.8 %edges.1 = (f32[4,16,128,128]{3,2,1,0:T(8,128)S(1)}, f32[16,16,8,128]{3,2,1,0:T(8,128)S(1)}, f32[16,128,128]{2,1,0:T(8,128)S(1)}, f32[16,128,128]{2,1,0:T(8,128)...) custom-call(f32[4,16,128,128]{3,2,1,0:T(8,128)} %tr.5, ...), custom_call_target="tpu_custom_call" | custom-call | flops 60000000 | bytes 11534336 | tf_op jit(solution)/shard_map/edges/pallas_call | solution.py:192
  7.5 4.1 %collective-permute-start.1 = (f32[24,8,128]{2,1,0:T(8,128)S(1)}, f32[24,8,128]{2,1,0:T(8,128)S(1)}, u32[]{:S(2)}, u32[]{:S(2)}) collective-permute-start(f32[24,8,128]{2,1,0:T(8,128)S(1)} %get-tuple-element.26.ew), channel_id=1, source_target_pairs={{16,32},{32,16},{48,64},{64,48},{80,96},{96,80},{112,0},{0,112},{1... | collective-permute-start | bytes 294920 | tf_op jit(solution)/shard_map/ppermute | solution.py:707
  11.6 0.0 collective-permute-start
  11.6 1.2 %rows.1 = (f32[96,128]{1,0:T(8,128)S(1)}, f32[96,128]{1,0:T(8,128)S(1)}) custom-call(f32[4,16,128,128]{3,2,1,0:T(8,128)} %tr.5, f32[16,128,128]{2,1,0:T(8,128)} %fill.5, s32[16,128,128]{2,1,0:T(8,128)} %mask.5, f32[16,128,128]{2,1,0:T(8,128)} %north.5), custom_call_target="tpu_custom_call" | custom-call | flops 1000000 | bytes 1048576 | tf_op jit(solution)/shard_map/rows/pallas_call | solution.py:111
  12.9 0.1 collective-permute-start.2
  13.0 0.7 collective-permute-start.3
  13.6 5.2 %first.1 = (f32[4,512,128]{2,1,0:T(8,128)S(1)}, f32[512,128]{1,0:T(8,128)S(1)}) custom-call(f32[4,16,128,128]{3,2,1,0:T(8,128)S(1)} %get-tuple-element.19.tr_s, f32[16,16,8,128]{3,2,1,0:T(8,128)S(1)} %get-tuple-element.20.h_v, f32[16,128,128]{2,1,0:T(8,128)S(1)} %get-tuple-element.21.east_s, f32[16,128,128]{2,1,0:T(8,128)S(1)} %get-tuple-element.22.north_s, ...), custom_call_target="tpu_custom_call" | custom-call | flops 60000000 | bytes 11534336 | tf_op jit(solution)/shard_map/first/pallas_call | solution.py:335
  18.9 0.0 collective-permute-done.2.got_one
  18.9 0.0 collective-permute-done.3.got_two
  18.9 0.0 collective-permute-done.1.ew_two
  18.9 0.0 collective-permute-done.ew_one
  18.9 5.4 %second.1 = (f32[5120,128]{1,0:T(8,128)}, f32[16,8,128]{2,1,0:T(8,128)S(1)}, f32[2,64,128]{2,1,0:T(8,128)S(1)}) custom-call(f32[4,512,128]{2,1,0:T(8,128)S(1)} %get-tuple-element.24.num2, f32[512,128]{1,0:T(8,128)S(1)} %get-tuple-element.25.den2, f32[24,8,128]{2,1,0:T(8,128)S(1)} %get-tuple-element.26.ew, f32[24,8,128]{2,1,0:T(8,128)S(1)} %collective-permute-done.ew_one, ...), custom_call_target="tpu_custom_call" | custom-call | flops 60000000 | bytes 6291456 | tf_op jit(solution)/shard_map/second/pallas_call | solution.py:502
  24.3 13.3 %all-to-all-start = ((f32[128,40,128]{2,1,0:T(8,128)}), f32[128,40,128]{2,1,0:T(8,128)S(1)}, u32[]{:S(2)}, u32[]{:S(2)}) async-start(f32[128,40,128]{2,1,0:T(8,128)} %bitcast.6), calls=%async_computation | async-start | bytes 5242880 | tf_op jit(solution)/shard_map/all_to_all | solution.py:714
  37.6 13.5 %third.1 = f32[4,16,128,128]{3,2,1,0:T(8,128)} custom-call(f32[4,16,128,128]{3,2,1,0:T(8,128)} %tr.5, f32[16,128,128]{2,1,0:T(8,128)} %fill.5, s32[16,128,128]{2,1,0:T(8,128)} %mask.5, f32[16,128,128]{2,1,0:T(8,128)} %east.3, f32[16,128,128]{2,1,0:T(8,128)} %north.5, f32[16]{0:T(128)} %diff.5, f32[128,128]{1,0:T(8,128)} %area.3, ...), custom_call_target="tpu_custom_call" | custom-call | flops 60000000 | bytes 12582912 | tf_op jit(solution)/shard_map/third/pallas_call | solution.py:620
  51.1 22.2 %all-to-all-done = f32[128,40,128]{2,1,0:T(8,128)S(1)} async-done(((f32[128,40,128]{2,1,0:T(8,128)}), f32[128,40,128]{2,1,0:T(8,128)S(1)}, u32[]{:S(2)}, u32[]{:S(2)}) %all-to-all-start) | async-done | bytes 2621472 | tf_op jit(solution)/shard_map/all_to_all | solution.py:714
  73.4 2.0 %last.1 = (f32[256,2048]{1,0:T(8,128)}, f32[256,512]{1,0:T(8,128)}) custom-call(f32[5120,128]{1,0:T(8,128)S(1)} %bitcast.5), custom_call_target="tpu_custom_call" | custom-call | tf_op jit(solution)/shard_map/last/pallas_call | solution.py:658
Async XLA Ops:
  7.5 11.4 %collective-permute-start.1 = (f32[24,8,128]{2,1,0:T(8,128)S(1)}, f32[24,8,128]{2,1,0:T(8,128)S(1)}, u32[]{:S(2)}, u32[]{:S(2)}) collective-permute-start(f32[24,8,128]{2,1,0:T(8,128)S(1)} %get-tuple-element.26.ew), channel_id=1, source_target_pairs={{16,32},{32,16},{48,64},{64,48},{80,96},{96,80},{112,0},{0,112},{1... | collective-permute-start | bytes 294920 | tf_op jit(solution)/shard_map/ppermute | solution.py:707
  11.6 7.3 %collective-permute-start = (f32[24,8,128]{2,1,0:T(8,128)S(1)}, f32[24,8,128]{2,1,0:T(8,128)S(1)}, u32[]{:S(2)}, u32[]{:S(2)}) collective-permute-start(f32[24,8,128]{2,1,0:T(8,128)S(1)} %get-tuple-element.26.ew), channel_id=1, source_target_pairs={{0,16},{16,0},{32,48},{48,32},{64,80},{80,64},{96,112},{112,96},{1... | collective-permute-start | bytes 294920 | tf_op jit(solution)/shard_map/ppermute | solution.py:706
  12.9 6.0 %collective-permute-start.2 = (f32[96,128]{1,0:T(8,128)S(1)}, f32[96,128]{1,0:T(8,128)S(1)}, u32[]{:S(2)}, u32[]{:S(2)}) collective-permute-start(f32[96,128]{1,0:T(8,128)S(1)} %get-tuple-element.27.ns_one), channel_id=1, source_target_pairs={{0,1},{1,0},{2,3},{3,2},{4,5},{5,4},{6,7},{7,6},{8,9},{9,8},{10,11... | collective-permute-start | bytes 147464 | tf_op jit(solution)/shard_map/ppermute | solution.py:703
  13.0 5.9 %collective-permute-start.3 = (f32[96,128]{1,0:T(8,128)S(1)}, f32[96,128]{1,0:T(8,128)S(1)}, u32[]{:S(2)}, u32[]{:S(2)}) collective-permute-start(f32[96,128]{1,0:T(8,128)S(1)} %get-tuple-element.28.ns_two), channel_id=1, source_target_pairs={{1,2},{2,1},{3,4},{4,3},{5,6},{6,5},{7,8},{8,7},{9,10},{10,9},{11,... | collective-permute-start | bytes 147464 | tf_op jit(solution)/shard_map/ppermute | solution.py:704
  24.3 49.1 %all-to-all-start = ((f32[128,40,128]{2,1,0:T(8,128)}), f32[128,40,128]{2,1,0:T(8,128)S(1)}, u32[]{:S(2)}, u32[]{:S(2)}) async-start(f32[128,40,128]{2,1,0:T(8,128)} %bitcast.6), calls=%async_computation | async-start | bytes 5242880 | tf_op jit(solution)/shard_map/all_to_all | solution.py:714

commit v6 on v5

--- a/solution.py
+++ b/solution.py
@@ -126,26 +126,10 @@
     )(tracers, fill, mask, north)
 
 
-def kernel_edges(
-    tr, fill, mask, east, north, area, owner,
-    tr_v, h_v, east_v, north_v, area_v, ew, placing,
-    fill_s, mask_s, owner_s, sems, area_sem, owner_sem,
-):
-    copies = input_copies(
-        (tr, fill, mask, east, north), (tr_v, fill_s, mask_s, east_v, north_v), sems
-    )
-    area_copy = pltpu.make_async_copy(area, area_v, area_sem)
-    owner_copy = pltpu.make_async_copy(owner, owner_s, owner_sem)
-    owner_copy.start()
-    for group in range(GROUPS):
-        for copy in copies(group):
-            copy.start()
-    area_copy.start()
-
+def kernel_edges(tr_v, fill_v, mask_v, east_v, owner, h_v, ew, placing):
     across = lane_iota((DEV, DEV))
     down = sub_iota((DEV, DEV))
-    owner_copy.wait()
-    who_row = owner_s[...]
+    who_row = owner[...]
     who = jnp.sum(jnp.where(down == across, who_row, 0), axis=1, keepdims=True)
     same = jnp.where((who == who_row) & (down < across), 1, 0)
     rank = jnp.sum(same, axis=0, keepdims=True)
@@ -158,12 +142,10 @@
     lane = lane_iota()
 
     def level(k, carry):
-        for copy in copies(k):
-            copy.wait()
         where_t = [(lane >> 1) == t * 16 + k for t in range(TR)]
         for v in range(16):
             at = row_set(32 * (v // 4) + v % 4)
-            h = fill_s[(k, *at)] * mask_s[(k, *at)].astype(F32)
+            h = fill_v[(k, *at)] * mask_v[(k, *at)].astype(F32)
             h_v[k, v] = h
             base = 64 * (v % 2)
             packed = ew[16 + v // 2]
@@ -183,37 +165,23 @@
         return carry
 
     lax.fori_loop(0, LV, level, 0)
-    area_copy.wait()
-
-
-def kernel_edges_call(tracers, fill, mask, east, north, area, owner):
-    hbm = pl.BlockSpec(memory_space=pltpu.HBM)
+
+
+def kernel_edges_call(tracers, fill, mask, east, owner):
     vmem = pl.BlockSpec(memory_space=pltpu.VMEM)
     return pl.pallas_call(
         kernel_edges,
         name="edges",
         out_shape=(
-            jax.ShapeDtypeStruct((TR, LV, ROWS, LANES), F32),
             jax.ShapeDtypeStruct((LV, 16, 8, LANES), F32),
-            jax.ShapeDtypeStruct((LV, ROWS, LANES), F32),
-            jax.ShapeDtypeStruct((LV, ROWS, LANES), F32),
-            jax.ShapeDtypeStruct((ROWS, LANES), F32),
             jax.ShapeDtypeStruct((24, 8, 128), F32),
             jax.ShapeDtypeStruct((CAP * DEV, 2 * DEV), BF16),
         ),
-        in_specs=[hbm] * 7,
-        out_specs=(vmem,) * 7,
-        scratch_shapes=[
-            pltpu.VMEM((LV, ROWS, LANES), F32),
-            pltpu.VMEM((LV, ROWS, LANES), jnp.int32),
-            pltpu.VMEM((1, DEV), jnp.int32),
-            pltpu.SemaphoreType.DMA((5, GROUPS)),
-            pltpu.SemaphoreType.DMA,
-            pltpu.SemaphoreType.DMA,
-        ],
-        compiler_params=pltpu.CompilerParams(vmem_limit_bytes=24 * MIB),
+        in_specs=[vmem] * 5,
+        out_specs=(vmem,) * 3,
+        compiler_params=pltpu.CompilerParams(vmem_limit_bytes=16 * MIB),
         cost_estimate=pl.CostEstimate(flops=60_000_000, bytes_accessed=11 * MIB, transcendentals=0),
-    )(tracers, fill, mask, east, north, area, owner)
+    )(tracers, fill, mask, east, owner)
 
 
 def kernel_first(
@@ -677,15 +645,13 @@
 ):
     lon_count = lax.axis_size("lon")
     lat_count = lax.axis_size("lat")
-    *fields, diffusivity, cell_area, owners = (
+    *in_hbm, diffusivity, area_hbm = (
         pltpu.with_memory_space_constraint(x, pltpu.HBM)
         for x in (
-            tracers, fill_fraction, ocean_mask, east_speed, north_speed, diffusivity, cell_area,
-            owner_map.reshape(1, DEV),
+            tracers, fill_fraction, ocean_mask, east_speed, north_speed, diffusivity, cell_area
         )
     )
-    tracers, fill_fraction, ocean_mask, east_speed, north_speed = fields
-    ns_one, ns_two = kernel_rows_call(tracers, fill_fraction, ocean_mask, north_speed)
+    ns_one, ns_two = kernel_rows_call(in_hbm[0], in_hbm[1], in_hbm[2], in_hbm[4])
     both = ("lon", "lat")
 
     def swapped(pairs):
@@ -702,19 +668,21 @@
     ]
     got_one = lax.ppermute(ns_one, both, swapped(step_one))
     got_two = lax.ppermute(ns_two, both, swapped(step_two + fold))
-    *held, ew, placing = kernel_edges_call(*fields, cell_area, owners)
+    h_v, ew, placing = kernel_edges_call(
+        tracers, fill_fraction, ocean_mask, east_speed, owner_map.reshape(1, DEV)
+    )
     ew_one = lax.ppermute(ew, "lon", swapped([(n, n + 1) for n in range(0, lon_count, 2)]))
     ew_two = lax.ppermute(
         ew, "lon", swapped([(n, (n + 1) % lon_count) for n in range(1, lon_count, 2)])
     )
-    num2, den2 = kernel_first_call(*held, diffusivity)
+    num2, den2 = kernel_first_call(tracers, h_v, east_speed, north_speed, cell_area, diffusivity)
     send, d_ew, d_ns = kernel_second_call(
         num2, den2, ew, ew_one, ew_two, ns_one, ns_two, got_one, got_two, diffusivity, placing
     )
     got = lax.all_to_all(
         send.reshape(DEV, CAP * CHUNKS, 128), both, split_axis=0, concat_axis=0, tiled=True
     )
-    updated = kernel_third_call(*fields, diffusivity, cell_area, d_ew, d_ns)
+    updated = kernel_third_call(*in_hbm, diffusivity, area_hbm, d_ew, d_ns)
     two, four = kernel_last_call(got.reshape(DEV * CAP * CHUNKS, 128))
     return (updated, two[None], four[None])
 

time: 75.6 us -> 78.3 us (1.036)
  local copies, waits for them, and re-layouts: 0 us -> 6.54 us
  Pallas kernels: 34.2 us -> 30.1 us
    unnamed x0 -> x18, local copies, waits for them, and re-layouts: none -> 6.54 us
    pallas_call x1, Pallas kernels: 6.85 us -> 2.85 us  [kernel_edges_call(): pl.pallas_call(kernel_edges, name='edges', out_shape=(jax.ShapeDtypeStruc...]
  transfers between devices with their start and end apart: 5 -> 5, of which waited for: 1 -> 1; matrix products, arithmetic and copies ran while one was open for 0% -> 0% of each run, Pallas kernels for 27% -> 26%
where the time goes in v6:
time: 78.3 us; the launch traced here: 77.9 us
  Pallas kernels  30.1 us (38%)
  waiting for transfers between devices  22.2 us (28%)
  starting transfers between devices  18.2 us (23%)
  local copies, waits for them, and re-layouts  6.54 us (8%)
  between operations  0.8 us (1%)
    all_to_all x1, waiting for transfers between devices, local(): lax.all_to_all(send.reshape(DEV, CAP * CHUNKS, 128), both, split_axis=0,...  22.2 us
    pallas_call x1, Pallas kernels, kernel_third_call(): pl.pallas_call(kernel_third, name='third', out_shape=jax.ShapeDtypeStruct...  13.5 us
    all_to_all x1, starting transfers between devices, local(): lax.all_to_all(send.reshape(DEV, CAP * CHUNKS, 128), both, split_axis=0,...  13.3 us
    unnamed x18, local copies, waits for them, and re-layouts  6.54 us
    pallas_call x1, Pallas kernels, kernel_second_call(): pl.pallas_call(kernel_second, name='second', out_shape=(pltpu.HBM((DEV *...  5.36 us
    pallas_call x1, Pallas kernels, kernel_first_call(): pl.pallas_call(kernel_first, name='first', out_shape=(jax.ShapeDtypeStruc...  5.21 us
    ppermute x1, starting transfers between devices, local(): lax.ppermute(ew, 'lon', swapped([(n, (n + 1) % lon_count) for n in range(...  4.13 us
    pallas_call x1, Pallas kernels, kernel_edges_call(): pl.pallas_call(kernel_edges, name='edges', out_shape=(jax.ShapeDtypeStruc...  2.85 us
  transfers between devices with their start and end apart: 5, of which 1 were waited for; matrix products, arithmetic and copies ran while one was open for 0% of the time, Pallas kernels for 26%

profile of v6, /device:TPU:0, one launch (start us, length us, event | category | flops | bytes accessed | tf_op | source)
XLA Modules:
  0.0 77.9 jit_solution(18246243593003796545)
XLA Ops:
  0.6 0.0 copy-start
  0.6 2.2 %copy-done = f32[4,16,128,128]{3,2,1,0:T(8,128)S(1)} copy-done((f32[4,16,128,128]{3,2,1,0:T(8,128)S(1)}, f32[4,16,128,128]{3,2,1,0:T(8,128)}, u32[]{:S(2)}) %copy-start) | copy-done | bytes 4194328
  2.8 0.0 copy-start.2
  2.8 1.2 %copy-done.2 = f32[16,128,128]{2,1,0:T(8,128)S(1)} copy-done((f32[16,128,128]{2,1,0:T(8,128)S(1)}, f32[16,128,128]{2,1,0:T(8,128)}, u32[]{:S(2)}) %copy-start.2) | copy-done | bytes 1048600
  4.0 0.0 copy-start.3
  4.0 1.2 %copy-done.3 = s32[16,128,128]{2,1,0:T(8,128)S(1)} copy-done((s32[16,128,128]{2,1,0:T(8,128)S(1)}, s32[16,128,128]{2,1,0:T(8,128)}, u32[]{:S(2)}) %copy-start.3) | copy-done | bytes 1048600
  5.3 1.2 %copy-done.5 = f32[16,128,128]{2,1,0:T(8,128)S(1)} copy-done((f32[16,128,128]{2,1,0:T(8,128)S(1)}, f32[16,128,128]{2,1,0:T(8,128)}, u32[]{:S(2)}) %copy-start.5) | copy-done | bytes 1048600
  6.5 0.7 copy-done.8
  7.2 2.8 %edges.1 = (f32[16,16,8,128]{3,2,1,0:T(8,128)S(1)}, f32[24,8,128]{2,1,0:T(8,128)S(1)}, bf16[256,256]{1,0:T(8,128)(2,1)S(1)}) custom-call(f32[4,16,128,128]{3,2,1,0:T(8,128)S(1)} %copy-done, f32[16,128,128]{2,1,0:T(8,128)S(1)} %copy-done.2, s32[16,128,128]{2,1,0:T(8,128)S(1)} %copy-done.3, f32[16,128,128]{2,1,0:T(8,128)S(1)} %copy-done.5, s32[1,128]{1,0:T(1,128)S(1)} %bitcast.6), custom_call_target="tpu_custom_call" | custom-call | flops 60000000 | bytes 11534336 | tf_op jit(solution)/shard_map/edges/pallas_call | solution.py:172
  10.0 0.0 copy-start.1
  10.0 0.0 copy-start.4
  10.0 0.0 copy-start.6
  10.0 0.0 copy-start.7
  10.1 4.1 %collective-permute-start.1 = (f32[24,8,128]{2,1,0:T(8,128)S(1)}, f32[24,8,128]{2,1,0:T(8,128)S(1)}, u32[]{:S(2)}, u32[]{:S(2)}) collective-permute-start(f32[24,8,128]{2,1,0:T(8,128)S(1)} %get-tuple-element.18.ew), channel_id=1, source_target_pairs={{16,32},{32,16},{48,64},{64,48},{80,96},{96,80},{112,0},{0,112},{1... | collective-permute-start | bytes 294920 | tf_op jit(solution)/shard_map/ppermute | solution.py:675
  14.2 0.0 collective-permute-start
  14.2 1.2 %rows.1 = (f32[96,128]{1,0:T(8,128)S(1)}, f32[96,128]{1,0:T(8,128)S(1)}) custom-call(f32[4,16,128,128]{3,2,1,0:T(8,128)} %tr.3, f32[16,128,128]{2,1,0:T(8,128)} %fill.3, s32[16,128,128]{2,1,0:T(8,128)} %mask.3, f32[16,128,128]{2,1,0:T(8,128)} %north.3), custom_call_target="tpu_custom_call" | custom-call | flops 1000000 | bytes 1048576 | tf_op jit(solution)/shard_map/rows/pallas_call | solution.py:111
  15.4 0.1 collective-permute-start.2
  15.5 0.7 collective-permute-start.3
  16.2 0.0 copy-done.1
  16.2 0.0 copy-done.4
  16.2 0.0 copy-done.6
  16.2 0.0 copy-done.7
  16.3 5.2 %first.1 = (f32[4,512,128]{2,1,0:T(8,128)S(1)}, f32[512,128]{1,0:T(8,128)S(1)}) custom-call(f32[4,16,128,128]{3,2,1,0:T(8,128)S(1)} %copy-done.1, f32[16,16,8,128]{3,2,1,0:T(8,128)S(1)} %get-tuple-element.15.h_v, f32[16,128,128]{2,1,0:T(8,128)S(1)} %copy-done.6, f32[16,128,128]{2,1,0:T(8,128)S(1)} %copy-done.4, f32[128,128]{1,0:T(8,128)S(1)} %copy-done.7, ...), custom_call_target="tpu_custom_call" | custom-call | flops 60000000 | bytes 11534336 | tf_op jit(solution)/shard_map/first/pallas_call | solution.py:303
  21.5 0.0 collective-permute-done.2.got_one
  21.5 0.0 collective-permute-done.3.got_two
  21.5 0.0 collective-permute-done.1.ew_two
  21.5 0.0 collective-permute-done.ew_one
  21.5 5.4 %second.1 = (f32[5120,128]{1,0:T(8,128)}, f32[16,8,128]{2,1,0:T(8,128)S(1)}, f32[2,64,128]{2,1,0:T(8,128)S(1)}) custom-call(f32[4,512,128]{2,1,0:T(8,128)S(1)} %get-tuple-element.16.num2, f32[512,128]{1,0:T(8,128)S(1)} %get-tuple-element.17.den2, f32[24,8,128]{2,1,0:T(8,128)S(1)} %get-tuple-element.18.ew, f32[24,8,128]{2,1,0:T(8,128)S(1)} %collective-permute-done.ew_one, ...), custom_call_target="tpu_custom_call" | custom-call | flops 60000000 | bytes 6291456 | tf_op jit(solution)/shard_map/second/pallas_call | solution.py:470
  26.9 13.3 %all-to-all-start = ((f32[128,40,128]{2,1,0:T(8,128)}), f32[128,40,128]{2,1,0:T(8,128)S(1)}, u32[]{:S(2)}, u32[]{:S(2)}) async-start(f32[128,40,128]{2,1,0:T(8,128)} %bitcast.7), calls=%async_computation | async-start | bytes 5242880 | tf_op jit(solution)/shard_map/all_to_all | solution.py:682
  40.2 13.5 %third.1 = f32[4,16,128,128]{3,2,1,0:T(8,128)} custom-call(f32[4,16,128,128]{3,2,1,0:T(8,128)} %tr.3, f32[16,128,128]{2,1,0:T(8,128)} %fill.3, s32[16,128,128]{2,1,0:T(8,128)} %mask.3, f32[16,128,128]{2,1,0:T(8,128)} %east.1, f32[16,128,128]{2,1,0:T(8,128)} %north.3, f32[16]{0:T(128)} %diff.5, f32[128,128]{1,0:T(8,128)} %area.1, ...), custom_call_target="tpu_custom_call" | custom-call | flops 60000000 | bytes 12582912 | tf_op jit(solution)/shard_map/third/pallas_call | solution.py:588
  53.7 22.2 %all-to-all-done = f32[128,40,128]{2,1,0:T(8,128)S(1)} async-done(((f32[128,40,128]{2,1,0:T(8,128)}), f32[128,40,128]{2,1,0:T(8,128)S(1)}, u32[]{:S(2)}, u32[]{:S(2)}) %all-to-all-start) | async-done | bytes 2621472 | tf_op jit(solution)/shard_map/all_to_all | solution.py:682
  75.9 2.0 %last.1 = (f32[256,2048]{1,0:T(8,128)}, f32[256,512]{1,0:T(8,128)}) custom-call(f32[5120,128]{1,0:T(8,128)S(1)} %bitcast.5), custom_call_target="tpu_custom_call" | custom-call | tf_op jit(solution)/shard_map/last/pallas_call | solution.py:626
  (2 shorter events, 0.0 us)
Async XLA Ops:
  0.6 2.2 %copy-start = (f32[4,16,128,128]{3,2,1,0:T(8,128)S(1)}, f32[4,16,128,128]{3,2,1,0:T(8,128)}, u32[]{:S(2)}) copy-start(f32[4,16,128,128]{3,2,1,0:T(8,128)} %tr.3) | copy-start | bytes 12582916
  2.8 1.2 %copy-start.2 = (f32[16,128,128]{2,1,0:T(8,128)S(1)}, f32[16,128,128]{2,1,0:T(8,128)}, u32[]{:S(2)}) copy-start(f32[16,128,128]{2,1,0:T(8,128)} %fill.3) | copy-start | bytes 3145732
  4.0 1.2 %copy-start.3 = (s32[16,128,128]{2,1,0:T(8,128)S(1)}, s32[16,128,128]{2,1,0:T(8,128)}, u32[]{:S(2)}) copy-start(s32[16,128,128]{2,1,0:T(8,128)} %mask.3) | copy-start | bytes 3145732
  5.3 1.2 %copy-start.5 = (f32[16,128,128]{2,1,0:T(8,128)S(1)}, f32[16,128,128]{2,1,0:T(8,128)}, u32[]{:S(2)}) copy-start(f32[16,128,128]{2,1,0:T(8,128)} %east.1) | copy-start | bytes 3145732
  6.5 0.7 copy-start.8
  10.0 6.2 %copy-start.1 = (f32[4,16,128,128]{3,2,1,0:T(8,128)S(1)}, f32[4,16,128,128]{3,2,1,0:T(8,128)}, u32[]{:S(2)}) copy-start(f32[4,16,128,128]{3,2,1,0:T(8,128)} %tr.3) | copy-start | bytes 12582916
  10.0 6.2 %copy-start.4 = (f32[16,128,128]{2,1,0:T(8,128)S(1)}, f32[16,128,128]{2,1,0:T(8,128)}, u32[]{:S(2)}) copy-start(f32[16,128,128]{2,1,0:T(8,128)} %north.3) | copy-start | bytes 3145732
  10.0 6.2 %copy-start.6 = (f32[16,128,128]{2,1,0:T(8,128)S(1)}, f32[16,128,128]{2,1,0:T(8,128)}, u32[]{:S(2)}) copy-start(f32[16,128,128]{2,1,0:T(8,128)} %east.1) | copy-start | bytes 3145732
  10.0 6.2 %copy-start.7 = (f32[128,128]{1,0:T(8,128)S(1)}, f32[128,128]{1,0:T(8,128)}, u32[]{:S(2)}) copy-start(f32[128,128]{1,0:T(8,128)} %area.1) | copy-start | bytes 196612
  10.1 11.4 %collective-permute-start.1 = (f32[24,8,128]{2,1,0:T(8,128)S(1)}, f32[24,8,128]{2,1,0:T(8,128)S(1)}, u32[]{:S(2)}, u32[]{:S(2)}) collective-permute-start(f32[24,8,128]{2,1,0:T(8,128)S(1)} %get-tuple-element.18.ew), channel_id=1, source_target_pairs={{16,32},{32,16},{48,64},{64,48},{80,96},{96,80},{112,0},{0,112},{1... | collective-permute-start | bytes 294920 | tf_op jit(solution)/shard_map/ppermute | solution.py:675
  14.2 7.3 %collective-permute-start = (f32[24,8,128]{2,1,0:T(8,128)S(1)}, f32[24,8,128]{2,1,0:T(8,128)S(1)}, u32[]{:S(2)}, u32[]{:S(2)}) collective-permute-start(f32[24,8,128]{2,1,0:T(8,128)S(1)} %get-tuple-element.18.ew), channel_id=1, source_target_pairs={{0,16},{16,0},{32,48},{48,32},{64,80},{80,64},{96,112},{112,96},{1... | collective-permute-start | bytes 294920 | tf_op jit(solution)/shard_map/ppermute | solution.py:674
  15.4 6.0 %collective-permute-start.2 = (f32[96,128]{1,0:T(8,128)S(1)}, f32[96,128]{1,0:T(8,128)S(1)}, u32[]{:S(2)}, u32[]{:S(2)}) collective-permute-start(f32[96,128]{1,0:T(8,128)S(1)} %get-tuple-element.19.ns_one), channel_id=1, source_target_pairs={{0,1},{1,0},{2,3},{3,2},{4,5},{5,4},{6,7},{7,6},{8,9},{9,8},{10,11... | collective-permute-start | bytes 147464 | tf_op jit(solution)/shard_map/ppermute | solution.py:669
  15.5 5.9 %collective-permute-start.3 = (f32[96,128]{1,0:T(8,128)S(1)}, f32[96,128]{1,0:T(8,128)S(1)}, u32[]{:S(2)}, u32[]{:S(2)}) collective-permute-start(f32[96,128]{1,0:T(8,128)S(1)} %get-tuple-element.20.ns_two), channel_id=1, source_target_pairs={{1,2},{2,1},{3,4},{4,3},{5,6},{6,5},{7,8},{8,7},{9,10},{10,9},{11,... | collective-permute-start | bytes 147464 | tf_op jit(solution)/shard_map/ppermute | solution.py:670
  26.9 49.1 %all-to-all-start = ((f32[128,40,128]{2,1,0:T(8,128)}), f32[128,40,128]{2,1,0:T(8,128)S(1)}, u32[]{:S(2)}, u32[]{:S(2)}) async-start(f32[128,40,128]{2,1,0:T(8,128)} %bitcast.7), calls=%async_computation | async-start | bytes 5242880 | tf_op jit(solution)/shard_map/all_to_all | solution.py:682

commit v7 on v6

--- a/solution.py
+++ b/solution.py
@@ -16,6 +16,7 @@
 DEV, CAP = 128, 2
 CHUNKS = 20
 PARTS = 2
+EACH = 16
 F32, BF16 = jnp.float32, jnp.bfloat16
 MIB = 1 << 20
 
@@ -361,23 +362,31 @@
             pending = value
         else:
             value = pending + value
-            work[v // 2] = jnp.where(is_east, value, pltpu.roll(value, 64, 1))
-
-    low_ends = (lane == 0) | (lane == 63)
-    high_ends = (lane == 64) | (lane == 127)
-
-    def add_ends(k, carry):
-        for t in range(TR):
-            for q in range(4):
-                rows = pl.ds(pl.multiple_of(k * 32 + q * 8, 8), 8)
-                shift = 127 - 2 * k + (128 - 32 * t)
-                low = pltpu.roll(work[2 * q], shift - 64, 1)
-                high = pltpu.roll(work[2 * q + 1], shift, 1)
-                edge = jnp.where(low_ends, low, jnp.where(high_ends, high, 0.0))
-                acc[t, rows, :] = num2[t, rows, :] + edge
+            far_value = pltpu.roll(value, 64, 1)
+            q, par = v // 4, (v // 2) % 2
+            plain = jnp.where(is_east, value, far_value)
+            moved = jnp.where(is_east, far_value, value)
+            if par == 0:
+                lower = plain, moved
+            else:
+                for half in range(2):
+                    first_lanes = (lane < 64) == is_east
+                    mine = first_lanes if half == 0 else ~first_lanes
+                    work[half, q] = jnp.where(mine, lower[0], moved)
+
+    ends = ((lane & 63) == 0) | ((lane & 63) == 63)
+
+    def add_ends(step, carry):
+        for n in range(EACH):
+            k = step * EACH + n
+            for t in range(TR):
+                for q in range(4):
+                    rows = pl.ds(pl.multiple_of(k * 32 + q * 8, 8), 8)
+                    moved = pltpu.roll(work[t // 2, q], 63 - 2 * k + (128 - 32 * t), 1)
+                    acc[t, rows, :] = num2[t, rows, :] + jnp.where(ends, moved, 0.0)
         return carry
 
-    lax.fori_loop(0, LV, add_ends, 0)
+    lax.fori_loop(0, LV // EACH, add_ends, 0)
 
     source = sub_iota((128, 128))
     target = lane_iota((128, 128))
@@ -478,7 +487,7 @@
         in_specs=[vmem] * 9 + [pl.BlockSpec(memory_space=pltpu.SMEM), vmem],
         out_specs=(pl.BlockSpec(memory_space=pltpu.HBM), vmem, vmem),
         scratch_shapes=[
-            pltpu.VMEM((8, 8, 128), F32),
+            pltpu.VMEM((2, 4, 8, 128), F32),
             pltpu.VMEM((TR, 512, 128), F32),
             pltpu.VMEM((256, 2560), BF16),
             pltpu.VMEM((DEV * CAP * CHUNKS, 128), F32),

time: 78.3 us -> 76.5 us (0.977)
  Pallas kernels: 30.1 us -> 28.3 us
    pallas_call x1, Pallas kernels: 5.36 us -> 3.58 us  [kernel_second_call(): pl.pallas_call(kernel_second, name='second', out_shape=(pltpu.HBM((DEV *...]
where the time goes in v7:
time: 76.5 us; the launch traced here: 76.1 us
  Pallas kernels  28.3 us (37%)
  waiting for transfers between devices  22.2 us (29%)
  starting transfers between devices  18.2 us (24%)
  local copies, waits for them, and re-layouts  6.54 us (9%)
  between operations  0.8 us (1%)
    all_to_all x1, waiting for transfers between devices, local(): lax.all_to_all(send.reshape(DEV, CAP * CHUNKS, 128), both, split_axis=0,...  22.2 us
    pallas_call x1, Pallas kernels, kernel_third_call(): pl.pallas_call(kernel_third, name='third', out_shape=jax.ShapeDtypeStruct...  13.5 us
    all_to_all x1, starting transfers between devices, local(): lax.all_to_all(send.reshape(DEV, CAP * CHUNKS, 128), both, split_axis=0,...  13.3 us
    unnamed x18, local copies, waits for them, and re-layouts  6.54 us
    pallas_call x1, Pallas kernels, kernel_first_call(): pl.pallas_call(kernel_first, name='first', out_shape=(jax.ShapeDtypeStruc...  5.21 us
    ppermute x1, starting transfers between devices, local(): lax.ppermute(ew, 'lon', swapped([(n, (n + 1) % lon_count) for n in range(...  4.13 us
    pallas_call x1, Pallas kernels, kernel_second_call(): pl.pallas_call(kernel_second, name='second', out_shape=(pltpu.HBM((DEV *...  3.58 us
    pallas_call x1, Pallas kernels, kernel_edges_call(): pl.pallas_call(kernel_edges, name='edges', out_shape=(jax.ShapeDtypeStruc...  2.85 us
  transfers between devices with their start and end apart: 5, of which 1 were waited for; matrix products, arithmetic and copies ran while one was open for 0% of the time, Pallas kernels for 26%

profile of v7, /device:TPU:0, one launch (start us, length us, event | category | flops | bytes accessed | tf_op | source)
XLA Modules:
  0.0 76.1 jit_solution(7274915933862722384)
XLA Ops:
  0.6 0.0 copy-start
  0.6 2.2 %copy-done = f32[4,16,128,128]{3,2,1,0:T(8,128)S(1)} copy-done((f32[4,16,128,128]{3,2,1,0:T(8,128)S(1)}, f32[4,16,128,128]{3,2,1,0:T(8,128)}, u32[]{:S(2)}) %copy-start) | copy-done | bytes 4194328
  2.8 0.0 copy-start.2
  2.8 1.2 %copy-done.2 = f32[16,128,128]{2,1,0:T(8,128)S(1)} copy-done((f32[16,128,128]{2,1,0:T(8,128)S(1)}, f32[16,128,128]{2,1,0:T(8,128)}, u32[]{:S(2)}) %copy-start.2) | copy-done | bytes 1048600
  4.0 0.0 copy-start.3
  4.0 1.2 %copy-done.3 = s32[16,128,128]{2,1,0:T(8,128)S(1)} copy-done((s32[16,128,128]{2,1,0:T(8,128)S(1)}, s32[16,128,128]{2,1,0:T(8,128)}, u32[]{:S(2)}) %copy-start.3) | copy-done | bytes 1048600
  5.3 1.2 %copy-done.5 = f32[16,128,128]{2,1,0:T(8,128)S(1)} copy-done((f32[16,128,128]{2,1,0:T(8,128)S(1)}, f32[16,128,128]{2,1,0:T(8,128)}, u32[]{:S(2)}) %copy-start.5) | copy-done | bytes 1048600
  6.5 0.7 copy-done.8
  7.2 2.8 %edges.1 = (f32[16,16,8,128]{3,2,1,0:T(8,128)S(1)}, f32[24,8,128]{2,1,0:T(8,128)S(1)}, bf16[256,256]{1,0:T(8,128)(2,1)S(1)}) custom-call(f32[4,16,128,128]{3,2,1,0:T(8,128)S(1)} %copy-done, f32[16,128,128]{2,1,0:T(8,128)S(1)} %copy-done.2, s32[16,128,128]{2,1,0:T(8,128)S(1)} %copy-done.3, f32[16,128,128]{2,1,0:T(8,128)S(1)} %copy-done.5, s32[1,128]{1,0:T(1,128)S(1)} %bitcast.6), custom_call_target="tpu_custom_call" | custom-call | flops 60000000 | bytes 11534336 | tf_op jit(solution)/shard_map/edges/pallas_call | solution.py:173
  10.0 0.0 copy-start.1
  10.0 0.0 copy-start.4
  10.0 0.0 copy-start.6
  10.0 0.0 copy-start.7
  10.1 4.1 %collective-permute-start.1 = (f32[24,8,128]{2,1,0:T(8,128)S(1)}, f32[24,8,128]{2,1,0:T(8,128)S(1)}, u32[]{:S(2)}, u32[]{:S(2)}) collective-permute-start(f32[24,8,128]{2,1,0:T(8,128)S(1)} %get-tuple-element.18.ew), channel_id=1, source_target_pairs={{16,32},{32,16},{48,64},{64,48},{80,96},{96,80},{112,0},{0,112},{1... | collective-permute-start | bytes 294920 | tf_op jit(solution)/shard_map/ppermute | solution.py:684
  14.2 0.0 collective-permute-start
  14.2 1.2 %rows.1 = (f32[96,128]{1,0:T(8,128)S(1)}, f32[96,128]{1,0:T(8,128)S(1)}) custom-call(f32[4,16,128,128]{3,2,1,0:T(8,128)} %tr.3, f32[16,128,128]{2,1,0:T(8,128)} %fill.3, s32[16,128,128]{2,1,0:T(8,128)} %mask.3, f32[16,128,128]{2,1,0:T(8,128)} %north.3), custom_call_target="tpu_custom_call" | custom-call | flops 1000000 | bytes 1048576 | tf_op jit(solution)/shard_map/rows/pallas_call | solution.py:112
  15.4 0.1 collective-permute-start.2
  15.5 0.7 collective-permute-start.3
  16.2 0.0 copy-done.1
  16.2 0.0 copy-done.4
  16.2 0.0 copy-done.6
  16.2 0.0 copy-done.7
  16.3 5.2 %first.1 = (f32[4,512,128]{2,1,0:T(8,128)S(1)}, f32[512,128]{1,0:T(8,128)S(1)}) custom-call(f32[4,16,128,128]{3,2,1,0:T(8,128)S(1)} %copy-done.1, f32[16,16,8,128]{3,2,1,0:T(8,128)S(1)} %get-tuple-element.15.h_v, f32[16,128,128]{2,1,0:T(8,128)S(1)} %copy-done.6, f32[16,128,128]{2,1,0:T(8,128)S(1)} %copy-done.4, f32[128,128]{1,0:T(8,128)S(1)} %copy-done.7, ...), custom_call_target="tpu_custom_call" | custom-call | flops 60000000 | bytes 11534336 | tf_op jit(solution)/shard_map/first/pallas_call | solution.py:304
  21.5 0.0 collective-permute-done.2.got_one
  21.5 0.0 collective-permute-done.3.got_two
  21.5 0.0 collective-permute-done.1.ew_two
  21.5 0.0 collective-permute-done.ew_one
  21.5 3.6 %second.1 = (f32[5120,128]{1,0:T(8,128)}, f32[16,8,128]{2,1,0:T(8,128)S(1)}, f32[2,64,128]{2,1,0:T(8,128)S(1)}) custom-call(f32[4,512,128]{2,1,0:T(8,128)S(1)} %get-tuple-element.16.num2, f32[512,128]{1,0:T(8,128)S(1)} %get-tuple-element.17.den2, f32[24,8,128]{2,1,0:T(8,128)S(1)} %get-tuple-element.18.ew, f32[24,8,128]{2,1,0:T(8,128)S(1)} %collective-permute-done.ew_one, ...), custom_call_target="tpu_custom_call" | custom-call | flops 60000000 | bytes 6291456 | tf_op jit(solution)/shard_map/second/pallas_call | solution.py:479
  25.1 13.3 %all-to-all-start = ((f32[128,40,128]{2,1,0:T(8,128)}), f32[128,40,128]{2,1,0:T(8,128)S(1)}, u32[]{:S(2)}, u32[]{:S(2)}) async-start(f32[128,40,128]{2,1,0:T(8,128)} %bitcast.7), calls=%async_computation | async-start | bytes 5242880 | tf_op jit(solution)/shard_map/all_to_all | solution.py:691
  38.4 13.5 %third.1 = f32[4,16,128,128]{3,2,1,0:T(8,128)} custom-call(f32[4,16,128,128]{3,2,1,0:T(8,128)} %tr.3, f32[16,128,128]{2,1,0:T(8,128)} %fill.3, s32[16,128,128]{2,1,0:T(8,128)} %mask.3, f32[16,128,128]{2,1,0:T(8,128)} %east.1, f32[16,128,128]{2,1,0:T(8,128)} %north.3, f32[16]{0:T(128)} %diff.5, f32[128,128]{1,0:T(8,128)} %area.1, ...), custom_call_target="tpu_custom_call" | custom-call | flops 60000000 | bytes 12582912 | tf_op jit(solution)/shard_map/third/pallas_call | solution.py:597
  51.9 22.2 %all-to-all-done = f32[128,40,128]{2,1,0:T(8,128)S(1)} async-done(((f32[128,40,128]{2,1,0:T(8,128)}), f32[128,40,128]{2,1,0:T(8,128)S(1)}, u32[]{:S(2)}, u32[]{:S(2)}) %all-to-all-start) | async-done | bytes 2621472 | tf_op jit(solution)/shard_map/all_to_all | solution.py:691
  74.1 2.0 %last.1 = (f32[256,2048]{1,0:T(8,128)}, f32[256,512]{1,0:T(8,128)}) custom-call(f32[5120,128]{1,0:T(8,128)S(1)} %bitcast.5), custom_call_target="tpu_custom_call" | custom-call | tf_op jit(solution)/shard_map/last/pallas_call | solution.py:635
  (2 shorter events, 0.0 us)
Async XLA Ops:
  0.6 2.2 %copy-start = (f32[4,16,128,128]{3,2,1,0:T(8,128)S(1)}, f32[4,16,128,128]{3,2,1,0:T(8,128)}, u32[]{:S(2)}) copy-start(f32[4,16,128,128]{3,2,1,0:T(8,128)} %tr.3) | copy-start | bytes 12582916
  2.8 1.2 %copy-start.2 = (f32[16,128,128]{2,1,0:T(8,128)S(1)}, f32[16,128,128]{2,1,0:T(8,128)}, u32[]{:S(2)}) copy-start(f32[16,128,128]{2,1,0:T(8,128)} %fill.3) | copy-start | bytes 3145732
  4.0 1.2 %copy-start.3 = (s32[16,128,128]{2,1,0:T(8,128)S(1)}, s32[16,128,128]{2,1,0:T(8,128)}, u32[]{:S(2)}) copy-start(s32[16,128,128]{2,1,0:T(8,128)} %mask.3) | copy-start | bytes 3145732
  5.3 1.2 %copy-start.5 = (f32[16,128,128]{2,1,0:T(8,128)S(1)}, f32[16,128,128]{2,1,0:T(8,128)}, u32[]{:S(2)}) copy-start(f32[16,128,128]{2,1,0:T(8,128)} %east.1) | copy-start | bytes 3145732
  6.5 0.7 copy-start.8
  10.0 6.2 %copy-start.1 = (f32[4,16,128,128]{3,2,1,0:T(8,128)S(1)}, f32[4,16,128,128]{3,2,1,0:T(8,128)}, u32[]{:S(2)}) copy-start(f32[4,16,128,128]{3,2,1,0:T(8,128)} %tr.3) | copy-start | bytes 12582916
  10.0 6.2 %copy-start.4 = (f32[16,128,128]{2,1,0:T(8,128)S(1)}, f32[16,128,128]{2,1,0:T(8,128)}, u32[]{:S(2)}) copy-start(f32[16,128,128]{2,1,0:T(8,128)} %north.3) | copy-start | bytes 3145732
  10.0 6.2 %copy-start.6 = (f32[16,128,128]{2,1,0:T(8,128)S(1)}, f32[16,128,128]{2,1,0:T(8,128)}, u32[]{:S(2)}) copy-start(f32[16,128,128]{2,1,0:T(8,128)} %east.1) | copy-start | bytes 3145732
  10.0 6.2 %copy-start.7 = (f32[128,128]{1,0:T(8,128)S(1)}, f32[128,128]{1,0:T(8,128)}, u32[]{:S(2)}) copy-start(f32[128,128]{1,0:T(8,128)} %area.1) | copy-start | bytes 196612
  10.1 11.4 %collective-permute-start.1 = (f32[24,8,128]{2,1,0:T(8,128)S(1)}, f32[24,8,128]{2,1,0:T(8,128)S(1)}, u32[]{:S(2)}, u32[]{:S(2)}) collective-permute-start(f32[24,8,128]{2,1,0:T(8,128)S(1)} %get-tuple-element.18.ew), channel_id=1, source_target_pairs={{16,32},{32,16},{48,64},{64,48},{80,96},{96,80},{112,0},{0,112},{1... | collective-permute-start | bytes 294920 | tf_op jit(solution)/shard_map/ppermute | solution.py:684
  14.2 7.3 %collective-permute-start = (f32[24,8,128]{2,1,0:T(8,128)S(1)}, f32[24,8,128]{2,1,0:T(8,128)S(1)}, u32[]{:S(2)}, u32[]{:S(2)}) collective-permute-start(f32[24,8,128]{2,1,0:T(8,128)S(1)} %get-tuple-element.18.ew), channel_id=1, source_target_pairs={{0,16},{16,0},{32,48},{48,32},{64,80},{80,64},{96,112},{112,96},{1... | collective-permute-start | bytes 294920 | tf_op jit(solution)/shard_map/ppermute | solution.py:683
  15.4 6.0 %collective-permute-start.2 = (f32[96,128]{1,0:T(8,128)S(1)}, f32[96,128]{1,0:T(8,128)S(1)}, u32[]{:S(2)}, u32[]{:S(2)}) collective-permute-start(f32[96,128]{1,0:T(8,128)S(1)} %get-tuple-element.19.ns_one), channel_id=1, source_target_pairs={{0,1},{1,0},{2,3},{3,2},{4,5},{5,4},{6,7},{7,6},{8,9},{9,8},{10,11... | collective-permute-start | bytes 147464 | tf_op jit(solution)/shard_map/ppermute | solution.py:678
  15.5 5.9 %collective-permute-start.3 = (f32[96,128]{1,0:T(8,128)S(1)}, f32[96,128]{1,0:T(8,128)S(1)}, u32[]{:S(2)}, u32[]{:S(2)}) collective-permute-start(f32[96,128]{1,0:T(8,128)S(1)} %get-tuple-element.20.ns_two), channel_id=1, source_target_pairs={{1,2},{2,1},{3,4},{4,3},{5,6},{6,5},{7,8},{8,7},{9,10},{10,9},{11,... | collective-permute-start | bytes 147464 | tf_op jit(solution)/shard_map/ppermute | solution.py:679
  25.1 49.1 %all-to-all-start = ((f32[128,40,128]{2,1,0:T(8,128)}), f32[128,40,128]{2,1,0:T(8,128)S(1)}, u32[]{:S(2)}, u32[]{:S(2)}) async-start(f32[128,40,128]{2,1,0:T(8,128)} %bitcast.7), calls=%async_computation | async-start | bytes 5242880 | tf_op jit(solution)/shard_map/all_to_all | solution.py:691

commit v8 on v7

--- a/solution.py
+++ b/solution.py
@@ -39,6 +39,20 @@
     return open_depth * (ahead + mixing), open_depth * (back + mixing)
 
 
+def half_face(lower_half, upper_half, lower_speed, upper_speed, twice_mixing, keep=None):
+    open_half = jnp.minimum(lower_half, upper_half)
+    if keep is not None:
+        open_half = jnp.where(keep, open_half, 0.0)
+    speeds = lower_speed + upper_speed
+    ahead = jnp.maximum(speeds, 0.0)
+    back = ahead - speeds
+    return open_half * (ahead + twice_mixing), open_half * (back + twice_mixing)
+
+
+def depth_gain(h):
+    return time_step * jnp.minimum(h * (1.0 / depth_floor), 1.0)
+
+
 def halves(values):
     high = values.astype(BF16)
     return high, (values - high.astype(F32)).astype(BF16)
@@ -70,7 +84,11 @@
     return (pl.ds(start, 8, stride=4), slice(None))
 
 
-def kernel_rows(tr, fill, mask, north, ns_one, ns_two, tr_s, fill_s, mask_s, north_s, sems):
+def kernel_rows(
+    tr, fill, mask, north, owner,
+    ns_one, ns_two, placing, pool,
+    tr_s, fill_s, mask_s, north_s, owner_s, sems, owner_sem,
+):
     copies = []
     for n, (src, dst) in enumerate(((tr, tr_s), (fill, fill_s), (mask, mask_s), (north, north_s))):
         for side in range(2):
@@ -84,6 +102,24 @@
                     pltpu.make_async_copy(src.at[:, rows], dst.at[side], sems.at[n, side])
                 )
             copies[-1].start()
+    owner_copy = pltpu.make_async_copy(owner, owner_s, owner_sem)
+    owner_copy.start()
+    source = sub_iota((256, 128))
+    match = lane_iota((256, 128)) == (source >> 7) * 64 + ((source & 127) >> 1)
+    for term in range(2):
+        pool[pl.ds(256 * term, 256), :] = jnp.where(match, 1.0, 0.0).astype(BF16)
+    across = lane_iota((DEV, DEV))
+    down = sub_iota((DEV, DEV))
+    owner_copy.wait()
+    who_row = owner_s[...]
+    who = jnp.sum(jnp.where(down == across, who_row, 0), axis=1, keepdims=True)
+    same = jnp.where((who == who_row) & (down < across), 1, 0)
+    rank = jnp.sum(same, axis=0, keepdims=True)
+    row_of = who_row * CAP + rank
+    for part in range(CAP):
+        here = jnp.where(down + part * DEV == row_of, 1.0, 0.0).astype(BF16)
+        placing[pl.ds(part * DEV, DEV), 0:DEV] = here
+        placing[pl.ds(part * DEV, DEV), DEV : 2 * DEV] = here
     for copy in copies:
         copy.wait()
     odd = lax.axis_index("lat") % 2 == 1
@@ -106,47 +142,43 @@
             ns_two[at, :] = jnp.where(odd, lines[1], lines[0])
 
 
-def kernel_rows_call(tracers, fill, mask, north):
+def kernel_rows_call(tracers, fill, mask, north, owner):
     hbm = pl.BlockSpec(memory_space=pltpu.HBM)
     vmem = pl.BlockSpec(memory_space=pltpu.VMEM)
     return pl.pallas_call(
         kernel_rows,
         name="rows",
-        out_shape=(jax.ShapeDtypeStruct((96, 128), F32),) * 2,
-        in_specs=[hbm] * 4,
-        out_specs=(vmem,) * 2,
+        out_shape=(
+            jax.ShapeDtypeStruct((96, 128), F32),
+            jax.ShapeDtypeStruct((96, 128), F32),
+            jax.ShapeDtypeStruct((CAP * DEV, 2 * DEV), BF16),
+            jax.ShapeDtypeStruct((512, 128), BF16),
+        ),
+        in_specs=[hbm] * 5,
+        out_specs=(vmem,) * 4,
         scratch_shapes=[
             pltpu.VMEM((2, TR, LV, 8, LANES), F32),
             pltpu.VMEM((2, LV, 8, LANES), F32),
             pltpu.VMEM((2, LV, 8, LANES), jnp.int32),
             pltpu.VMEM((2, LV, 8, LANES), F32),
+            pltpu.VMEM((1, DEV), jnp.int32),
             pltpu.SemaphoreType.DMA((4, 2)),
+            pltpu.SemaphoreType.DMA,
         ],
         compiler_params=pltpu.CompilerParams(vmem_limit_bytes=4 * MIB),
         cost_estimate=pl.CostEstimate(flops=1_000_000, bytes_accessed=MIB, transcendentals=0),
-    )(tracers, fill, mask, north)
-
-
-def kernel_edges(tr_v, fill_v, mask_v, east_v, owner, h_v, ew, placing):
-    across = lane_iota((DEV, DEV))
-    down = sub_iota((DEV, DEV))
-    who_row = owner[...]
-    who = jnp.sum(jnp.where(down == across, who_row, 0), axis=1, keepdims=True)
-    same = jnp.where((who == who_row) & (down < across), 1, 0)
-    rank = jnp.sum(same, axis=0, keepdims=True)
-    row_of = who_row * CAP + rank
-    for part in range(CAP):
-        here = jnp.where(down + part * DEV == row_of, 1.0, 0.0).astype(BF16)
-        placing[pl.ds(part * DEV, DEV), 0:DEV] = here
-        placing[pl.ds(part * DEV, DEV), DEV : 2 * DEV] = here
-
+    )(tracers, fill, mask, north, owner)
+
+
+def kernel_edges(tr_v, fill_v, mask_v, east_v, h_v, ew):
     lane = lane_iota()
 
     def level(k, carry):
         where_t = [(lane >> 1) == t * 16 + k for t in range(TR)]
+
         for v in range(16):
             at = row_set(32 * (v // 4) + v % 4)
-            h = fill_v[(k, *at)] * mask_v[(k, *at)].astype(F32)
+            h = 0.5 * (fill_v[(k, *at)] * mask_v[(k, *at)].astype(F32))
             h_v[k, v] = h
             base = 64 * (v % 2)
             packed = ew[16 + v // 2]
@@ -168,7 +200,7 @@
     lax.fori_loop(0, LV, level, 0)
 
 
-def kernel_edges_call(tracers, fill, mask, east, owner):
+def kernel_edges_call(tracers, fill, mask, east):
     vmem = pl.BlockSpec(memory_space=pltpu.VMEM)
     return pl.pallas_call(
         kernel_edges,
@@ -176,61 +208,54 @@
         out_shape=(
             jax.ShapeDtypeStruct((LV, 16, 8, LANES), F32),
             jax.ShapeDtypeStruct((24, 8, 128), F32),
-            jax.ShapeDtypeStruct((CAP * DEV, 2 * DEV), BF16),
         ),
-        in_specs=[vmem] * 5,
-        out_specs=(vmem,) * 3,
+        in_specs=[vmem] * 4,
+        out_specs=(vmem,) * 2,
         compiler_params=pltpu.CompilerParams(vmem_limit_bytes=16 * MIB),
         cost_estimate=pl.CostEstimate(flops=60_000_000, bytes_accessed=11 * MIB, transcendentals=0),
-    )(tracers, fill, mask, east, owner)
+    )(tracers, fill, mask, east)
 
 
 def kernel_first(
-    tr_s, h_v, east_s, north_s, area_s, diff,
+    tr_s, h_v, east_s, north_s, area_v, diff, pool,
     num2, den2,
-    g_s, face_s, coef, store, cross,
+    area_s, g_s, face_s, coef, store,
 ):
-    source = sub_iota((256, 128))
-    target = lane_iota((256, 128))
-    pool = jnp.where(target == (source >> 7) * 64 + ((source & 127) >> 1), 1.0, 0.0).astype(BF16)
-    beside = (source >> 7) * 64 + (((source & 127) + 1) >> 1) - jnp.where((source & 1) == 0, 1, 0)
-    inside = ((source & 127) != 0) & ((source & 127) != 127)
-    pool_cross = jnp.where((target == beside) & inside, 1.0, 0.0).astype(BF16)
     lane, sub = lane_iota(), sub_iota()
     is_even = (lane & 1) == 0
-    not_last = lane < 127
-    not_top = sub < 7
+    not_last, not_top = lane < 127, sub < 7
+    swap = jnp.where(is_even, lane + 127, lane + 1) & 127
+    for v in range(16):
+        area_s[v] = 2.0 * area_v[row_set(32 * (v // 4) + v % 4)]
 
     def level(k):
-        mixing = diff[k]
-
-        def load(ref, start):
-            return ref[(k, *row_set(start))]
+        twice_mixing = 2.0 * diff[k]
+
+        for v in range(16):
+            h, u = h_v[k, v], east_s[(k, *row_set(32 * (v // 4) + v % 4))]
+            p_e, q_e = half_face(
+                h, pltpu.roll(h, 127, 1), u, pltpu.roll(u, 127, 1), twice_mixing, keep=not_last
+            )
+            g_s[v] = depth_gain(2.0 * h)
+            face_s[0, v] = p_e
+            face_s[1, v] = q_e
 
         for v in range(16):
             start = 32 * (v // 4) + v % 4
-            h, u = h_v[k, v], load(east_s, start)
-            p_e, q_e = face(
-                h, pltpu.roll(h, 127, 1), u, pltpu.roll(u, 127, 1), mixing, keep=not_last
-            )
-            g_s[v] = (time_step * h) / jnp.maximum(h, depth_floor)
-            face_s[0, v] = p_e
-            face_s[1, v] = q_e
-
-        for v in range(16):
-            q, j = v // 4, v % 4
-            start = 32 * q + j
-            h, speed = h_v[k, v], load(north_s, start)
-            if j < 3:
-                p_n, q_n = face(h, h_v[k, v + 1], speed, load(north_s, start + 1), mixing)
-            elif q < 3:
-                h_up = jnp.where(
-                    sub < 7, pltpu.roll(h_v[k, v - 3], 7, 0), pltpu.roll(h_v[k, v + 1], 7, 0)
-                )
-                p_n, q_n = face(h, h_up, speed, load(north_s, start + 1), mixing)
+            h, speed = h_v[k, v], north_s[(k, *row_set(start))]
+            keep = None
+            if v == 15:
+                h_up, keep = pltpu.roll(h_v[k, 12], 7, 0), not_top
+                speed_up = pltpu.roll(north_s[(k, *row_set(96))], 7, 0)
             else:
-                h_up, speed_up = pltpu.roll(h_v[k, 12], 7, 0), pltpu.roll(load(north_s, 96), 7, 0)
-                p_n, q_n = face(h, h_up, speed, speed_up, mixing, keep=not_top)
+                speed_up = north_s[(k, *row_set(start + 1))]
+                if v % 4 < 3:
+                    h_up = h_v[k, v + 1]
+                else:
+                    h_up = jnp.where(
+                        not_top, pltpu.roll(h_v[k, v - 3], 7, 0), pltpu.roll(h_v[k, v + 1], 7, 0)
+                    )
+            p_n, q_n = half_face(h, h_up, speed, speed_up, twice_mixing, keep)
             face_s[2, v] = p_n
             face_s[3, v] = q_n
 
@@ -245,10 +270,12 @@
                 for n in range(2):
                     v = 4 * q + 2 * par + n
                     h, g = h_v[k, v], g_s[v]
-                    w = area_s[row_set(32 * q + 2 * par + n)] * h
+                    w = area_s[v] * h
                     p_e, q_w = face_s[0, v], pltpu.roll(face_s[1, v], 1, 1)
                     p_n, q_n = face_s[2, v], face_s[3, v]
-                    p_s, q_s = south if v % 4 == 0 else (face_s[2, v - 1], face_s[3, v - 1])
+                    p_s, q_s = south if v % 4 == 0 else (
+                        face_s[2, v - 1], face_s[3, v - 1]
+                    )
                     to_west = pltpu.roll(g, 1, 1) * q_w
                     to_east = pltpu.roll(g, 127, 1) * p_e
                     own = w - g * ((p_e + q_w) + (p_n + q_s))
@@ -276,16 +303,15 @@
                     high = cell(start + 2) if start < 98 else pltpu.roll(cell(96), 7, 0)
                     side = a_x * a + b_x * b
                     value = (a_c * a + b_c * b) + (low_c * low + high_c * high)
-                    cross[pl.ds(t * 32 + q * 8, 8), pl.ds(par * 128, 128)] = side
+                    value = value + jnp.take_along_axis(side, swap, axis=1)
                     store[pl.ds(t * 32 + q * 8, 8), pl.ds(par * 128, 128)] = value
 
     def pooled(k):
-        values = split_dot(store[...], pool)
-        sides = split_dot(cross[...], pool_cross)
+        both = jnp.concatenate(halves(store[...]), axis=1)
+        values = jnp.dot(both, pool[...], preferred_element_type=F32)
         rows = pl.ds(pl.multiple_of(k * 32, 32), 32)
         for t in range(TR):
-            part = slice(t * 32, t * 32 + 32)
-            num2[t, rows, :] = values[part] + sides[part]
+            num2[t, rows, :] = values[t * 32 : t * 32 + 32]
         den2[rows, :] = values[128:160]
 
     def group_body(k, carry):
@@ -294,12 +320,11 @@
         return carry
 
     store[...] = jnp.zeros_like(store)
-    cross[...] = jnp.zeros_like(cross)
     lax.fori_loop(0, LV, group_body, 0)
     pooled(LV - 1)
 
 
-def kernel_first_call(tr_v, h_v, east_v, north_v, area_v, diff):
+def kernel_first_call(tr_v, h_v, east_v, north_v, area_v, diff, pool):
     vmem = pl.BlockSpec(memory_space=pltpu.VMEM)
     return pl.pallas_call(
         kernel_first,
@@ -308,18 +333,18 @@
             jax.ShapeDtypeStruct((TR, 512, 128), F32),
             jax.ShapeDtypeStruct((512, 128), F32),
         ),
-        in_specs=[vmem] * 5 + [pl.BlockSpec(memory_space=pltpu.SMEM)],
+        in_specs=[vmem] * 5 + [pl.BlockSpec(memory_space=pltpu.SMEM), vmem],
         out_specs=(vmem,) * 2,
         scratch_shapes=[
+            pltpu.VMEM((16, 8, 128), F32),
             pltpu.VMEM((16, 8, 128), F32),
             pltpu.VMEM((4, 16, 8, 128), F32),
             pltpu.VMEM((6, 8, 8, 128), F32),
             pltpu.VMEM((160, 256), F32),
-            pltpu.VMEM((128, 256), F32),
         ],
         compiler_params=pltpu.CompilerParams(vmem_limit_bytes=16 * MIB),
         cost_estimate=pl.CostEstimate(flops=60_000_000, bytes_accessed=11 * MIB, transcendentals=0),
-    )(tr_v, h_v, east_v, north_v, area_v, diff)
+    )(tr_v, h_v, east_v, north_v, area_v, diff, pool)
 
 
 def spread(values, offset):
@@ -340,7 +365,7 @@
     level_of = (lane >> 1) & 15
     mixing = jnp.zeros((8, 128), F32)
     for k in range(LV):
-        mixing = jnp.where(level_of == k, diff[k], mixing)
+        mixing = jnp.where(level_of == k, 2.0 * diff[k], mixing)
 
     def neighbour(n):
         one, two = ew_one[n], ew_two[n]
@@ -352,12 +377,12 @@
         own_hu, near_hu = ew[16 + v // 2], neighbour(16 + v // 2)
         base = 64 * (v % 2)
         h = spread(own_hu, base)
-        p, q = face(
+        p, q = half_face(
             h, spread(near_hu, base), spread(own_hu, base + 32), spread(near_hu, base + 32), mixing
         )
         div = jnp.where(is_east, q, p) * neighbour(v) - jnp.where(is_east, p, q) * ew[v]
         d_ew[v] = div
-        value = (time_step * h) / jnp.maximum(h, depth_floor) * div
+        value = depth_gain(2.0 * h) * div
         if v % 2 == 0:
             pending = value
         else:
@@ -420,7 +445,7 @@
         for top in (False, True):
             h = own(4, top)
             p, q = face(h, near(4, top), own(5, top), near(5, top, -1.0), mix)
-            gain = (time_step * h) / jnp.maximum(h, depth_floor)
+            gain = depth_gain(h)
             for t in range(TR):
                 if top:
                     div = q * near(t, top) - p * own(t, top)
@@ -654,13 +679,16 @@
 ):
     lon_count = lax.axis_size("lon")
     lat_count = lax.axis_size("lat")
-    *in_hbm, diffusivity, area_hbm = (
+    *in_hbm, diffusivity, area_hbm, owners = (
         pltpu.with_memory_space_constraint(x, pltpu.HBM)
         for x in (
-            tracers, fill_fraction, ocean_mask, east_speed, north_speed, diffusivity, cell_area
+            tracers, fill_fraction, ocean_mask, east_speed, north_speed, diffusivity, cell_area,
+            owner_map.reshape(1, DEV),
         )
     )
-    ns_one, ns_two = kernel_rows_call(in_hbm[0], in_hbm[1], in_hbm[2], in_hbm[4])
+    ns_one, ns_two, placing, pool = kernel_rows_call(
+        in_hbm[0], in_hbm[1], in_hbm[2], in_hbm[4], owners
+    )
     both = ("lon", "lat")
 
     def swapped(pairs):
@@ -677,14 +705,14 @@
     ]
     got_one = lax.ppermute(ns_one, both, swapped(step_one))
     got_two = lax.ppermute(ns_two, both, swapped(step_two + fold))
-    h_v, ew, placing = kernel_edges_call(
-        tracers, fill_fraction, ocean_mask, east_speed, owner_map.reshape(1, DEV)
-    )
+    h_v, ew = kernel_edges_call(tracers, fill_fraction, ocean_mask, east_speed)
     ew_one = lax.ppermute(ew, "lon", swapped([(n, n + 1) for n in range(0, lon_count, 2)]))
     ew_two = lax.ppermute(
         ew, "lon", swapped([(n, (n + 1) % lon_count) for n in range(1, lon_count, 2)])
     )
-    num2, den2 = kernel_first_call(tracers, h_v, east_speed, north_speed, cell_area, diffusivity)
+    num2, den2 = kernel_first_call(
+        tracers, h_v, east_speed, north_speed, cell_area, diffusivity, pool
+    )
     send, d_ew, d_ns = kernel_second_call(
         num2, den2, ew, ew_one, ew_two, ns_one, ns_two, got_one, got_two, diffusivity, placing
     )

time: 76.5 us -> 75.9 us (level)
    all_to_all x1, starting transfers between devices: 13.3 us -> 12.5 us  [local(): lax.all_to_all(send.reshape(DEV, CAP * CHUNKS, 128), both, split_axis=0,...]
    unnamed x18 -> x16, local copies, waits for them, and re-layouts: 6.54 us -> 6.62 us
  transfers between devices with their start and end apart: 5 -> 5, of which waited for: 1 -> 1; matrix products, arithmetic and copies ran while one was open for 0% -> 0% of each run, Pallas kernels for 26% -> 27%
where the time goes in v8:
time: 75.9 us; the launch traced here: 75.5 us
  Pallas kernels  28.4 us (37%)
  waiting for transfers between devices  22.2 us (29%)
  starting transfers between devices  17.5 us (23%)
  local copies, waits for them, and re-layouts  6.62 us (9%)
    all_to_all x1, waiting for transfers between devices, local(): lax.all_to_all(send.reshape(DEV, CAP * CHUNKS, 128), both, split_axis=0,...  22.2 us
    pallas_call x1, Pallas kernels, kernel_third_call(): pl.pallas_call(kernel_third, name='third', out_shape=jax.ShapeDtypeStruct...  13.5 us
    all_to_all x1, starting transfers between devices, local(): lax.all_to_all(send.reshape(DEV, CAP * CHUNKS, 128), both, split_axis=0,...  12.5 us
    unnamed x16, local copies, waits for them, and re-layouts  6.62 us
    pallas_call x1, Pallas kernels, kernel_first_call(): pl.pallas_call(kernel_first, name='first', out_shape=(jax.ShapeDtypeStruc...  5.29 us
    ppermute x1, starting transfers between devices, local(): lax.ppermute(ew, 'lon', swapped([(n, (n + 1) % lon_count) for n in range(...  4.13 us
    pallas_call x1, Pallas kernels, kernel_second_call(): pl.pallas_call(kernel_second, name='second', out_shape=(pltpu.HBM((DEV *...  3.58 us
    pallas_call x1, Pallas kernels, kernel_edges_call(): pl.pallas_call(kernel_edges, name='edges', out_shape=(jax.ShapeDtypeStruc...  2.71 us
  transfers between devices with their start and end apart: 5, of which 1 were waited for; matrix products, arithmetic and copies ran while one was open for 0% of the time, Pallas kernels for 27%

profile of v8, /device:TPU:0, one launch (start us, length us, event | category | flops | bytes accessed | tf_op | source)
XLA Modules:
  0.0 75.5 jit_solution(15843191830510465397)
XLA Ops:
  0.6 0.0 copy-start
  0.6 2.2 %copy-done = f32[4,16,128,128]{3,2,1,0:T(8,128)S(1)} copy-done((f32[4,16,128,128]{3,2,1,0:T(8,128)S(1)}, f32[4,16,128,128]{3,2,1,0:T(8,128)}, u32[]{:S(2)}) %copy-start) | copy-done | bytes 4194328
  2.8 0.0 copy-start.2
  2.8 1.2 %copy-done.2 = f32[16,128,128]{2,1,0:T(8,128)S(1)} copy-done((f32[16,128,128]{2,1,0:T(8,128)S(1)}, f32[16,128,128]{2,1,0:T(8,128)}, u32[]{:S(2)}) %copy-start.2) | copy-done | bytes 1048600
  4.0 0.0 copy-start.3
  4.0 1.2 %copy-done.3 = s32[16,128,128]{2,1,0:T(8,128)S(1)} copy-done((s32[16,128,128]{2,1,0:T(8,128)S(1)}, s32[16,128,128]{2,1,0:T(8,128)}, u32[]{:S(2)}) %copy-start.3) | copy-done | bytes 1048600
  5.3 0.0 copy-start.4
  5.3 1.2 %copy-done.4 = f32[16,128,128]{2,1,0:T(8,128)S(1)} copy-done((f32[16,128,128]{2,1,0:T(8,128)S(1)}, f32[16,128,128]{2,1,0:T(8,128)}, u32[]{:S(2)}) %copy-start.4) | copy-done | bytes 1048600
  6.5 2.7 %edges.1 = (f32[16,16,8,128]{3,2,1,0:T(8,128)S(1)}, f32[24,8,128]{2,1,0:T(8,128)S(1)}) custom-call(f32[4,16,128,128]{3,2,1,0:T(8,128)S(1)} %copy-done, f32[16,128,128]{2,1,0:T(8,128)S(1)} %copy-done.2, s32[16,128,128]{2,1,0:T(8,128)S(1)} %copy-done.3, f32[16,128,128]{2,1,0:T(8,128)S(1)} %copy-done.4), custom_call_target="tpu_custom_call" | custom-call | flops 60000000 | bytes 11534336 | tf_op jit(solution)/shard_map/edges/pallas_call | solution.py:205
  9.2 4.1 %collective-permute-start.1 = (f32[24,8,128]{2,1,0:T(8,128)S(1)}, f32[24,8,128]{2,1,0:T(8,128)S(1)}, u32[]{:S(2)}, u32[]{:S(2)}) collective-permute-start(f32[24,8,128]{2,1,0:T(8,128)S(1)} %get-tuple-element.20.ew), channel_id=1, source_target_pairs={{16,32},{32,16},{48,64},{64,48},{80,96},{96,80},{112,0},{0,112},{1... | collective-permute-start | bytes 294920 | tf_op jit(solution)/shard_map/ppermute | solution.py:710
  13.3 0.0 collective-permute-start
  13.3 0.0 copy-start.1
  13.4 0.0 copy-start.5
  13.4 0.0 copy-start.6
  13.4 0.0 copy-start.7
  13.4 1.4 %rows.1 = (f32[96,128]{1,0:T(8,128)S(1)}, f32[96,128]{1,0:T(8,128)S(1)}, bf16[256,256]{1,0:T(8,128)(2,1)S(1)}, bf16[512,128]{1,0:T(8,128)(2,1)S(1)}) custom-call(f32[4,16,128,128]{3,2,1,0:T(8,128)} %tr.3, f32[16,128,128]{2,1,0:T(8,128)} %fill.3, s32[16,128,128]{2,1,0:T(8,128)} %mask.3, f32[16,128,128]{2,1,0:T(8,128)} %north.3, s32[1,128]{1,0:T(1,128)} %bitcast.7), custom_call_target="tpu_custom_call" | custom-call | flops 1000000 | bytes 1048576 | tf_op jit(solution)/shard_map/rows/pallas_call | solution.py:148
  14.8 0.1 collective-permute-start.2
  14.9 0.8 %collective-permute-start.3 = (f32[96,128]{1,0:T(8,128)S(1)}, f32[96,128]{1,0:T(8,128)S(1)}, u32[]{:S(2)}, u32[]{:S(2)}) collective-permute-start(f32[96,128]{1,0:T(8,128)S(1)} %get-tuple-element.22.ns_two), channel_id=1, source_target_pairs={{1,2},{2,1},{3,4},{4,3},{5,6},{6,5},{7,8},{8,7},{9,10},{10,9},{11,... | collective-permute-start | bytes 147464 | tf_op jit(solution)/shard_map/ppermute | solution.py:707
  15.7 0.1 copy-done.1
  15.8 0.3 copy-done.5
  16.1 0.3 copy-done.6
  16.4 0.0 copy-done.7
  16.4 5.3 %first.1 = (f32[4,512,128]{2,1,0:T(8,128)S(1)}, f32[512,128]{1,0:T(8,128)S(1)}) custom-call(f32[4,16,128,128]{3,2,1,0:T(8,128)S(1)} %copy-done.1, f32[16,16,8,128]{3,2,1,0:T(8,128)S(1)} %get-tuple-element.16.h_v, f32[16,128,128]{2,1,0:T(8,128)S(1)} %copy-done.5, f32[16,128,128]{2,1,0:T(8,128)S(1)} %copy-done.6, f32[128,128]{1,0:T(8,128)S(1)} %copy-done.7, ...), custom_call_target="tpu_custom_call" | custom-call | flops 60000000 | bytes 11534336 | tf_op jit(solution)/shard_map/first/pallas_call | solution.py:329
  21.7 0.0 collective-permute-done.2.got_one
  21.7 0.0 collective-permute-done.3.got_two
  21.8 0.0 collective-permute-done.1.ew_two
  21.8 0.0 collective-permute-done.ew_one
  21.8 3.6 %second.1 = (f32[5120,128]{1,0:T(8,128)}, f32[16,8,128]{2,1,0:T(8,128)S(1)}, f32[2,64,128]{2,1,0:T(8,128)S(1)}) custom-call(f32[4,512,128]{2,1,0:T(8,128)S(1)} %get-tuple-element.18.num2, f32[512,128]{1,0:T(8,128)S(1)} %get-tuple-element.19.den2, f32[24,8,128]{2,1,0:T(8,128)S(1)} %get-tuple-element.20.ew, f32[24,8,128]{2,1,0:T(8,128)S(1)} %collective-permute-done.ew_one, ...), custom_call_target="tpu_custom_call" | custom-call | flops 60000000 | bytes 6291456 | tf_op jit(solution)/shard_map/second/pallas_call | solution.py:504
  25.4 12.5 %all-to-all-start = ((f32[128,40,128]{2,1,0:T(8,128)}), f32[128,40,128]{2,1,0:T(8,128)S(1)}, u32[]{:S(2)}, u32[]{:S(2)}) async-start(f32[128,40,128]{2,1,0:T(8,128)} %bitcast.6), calls=%async_computation | async-start | bytes 5242880 | tf_op jit(solution)/shard_map/all_to_all | solution.py:719
  37.8 13.5 %third.1 = f32[4,16,128,128]{3,2,1,0:T(8,128)} custom-call(f32[4,16,128,128]{3,2,1,0:T(8,128)} %tr.3, f32[16,128,128]{2,1,0:T(8,128)} %fill.3, s32[16,128,128]{2,1,0:T(8,128)} %mask.3, f32[16,128,128]{2,1,0:T(8,128)} %east.1, f32[16,128,128]{2,1,0:T(8,128)} %north.3, f32[16]{0:T(128)} %diff.5, f32[128,128]{1,0:T(8,128)} %area.1, ...), custom_call_target="tpu_custom_call" | custom-call | flops 60000000 | bytes 12582912 | tf_op jit(solution)/shard_map/third/pallas_call | solution.py:622
  51.4 22.2 %all-to-all-done = f32[128,40,128]{2,1,0:T(8,128)S(1)} async-done(((f32[128,40,128]{2,1,0:T(8,128)}), f32[128,40,128]{2,1,0:T(8,128)S(1)}, u32[]{:S(2)}, u32[]{:S(2)}) %all-to-all-start) | async-done | bytes 2621472 | tf_op jit(solution)/shard_map/all_to_all | solution.py:719
  73.6 2.0 %last.1 = (f32[256,2048]{1,0:T(8,128)}, f32[256,512]{1,0:T(8,128)}) custom-call(f32[5120,128]{1,0:T(8,128)S(1)} %bitcast.5), custom_call_target="tpu_custom_call" | custom-call | tf_op jit(solution)/shard_map/last/pallas_call | solution.py:660
Async XLA Ops:
  0.6 2.2 %copy-start = (f32[4,16,128,128]{3,2,1,0:T(8,128)S(1)}, f32[4,16,128,128]{3,2,1,0:T(8,128)}, u32[]{:S(2)}) copy-start(f32[4,16,128,128]{3,2,1,0:T(8,128)} %tr.3) | copy-start | bytes 12582916
  2.8 1.2 %copy-start.2 = (f32[16,128,128]{2,1,0:T(8,128)S(1)}, f32[16,128,128]{2,1,0:T(8,128)}, u32[]{:S(2)}) copy-start(f32[16,128,128]{2,1,0:T(8,128)} %fill.3) | copy-start | bytes 3145732
  4.0 1.2 %copy-start.3 = (s32[16,128,128]{2,1,0:T(8,128)S(1)}, s32[16,128,128]{2,1,0:T(8,128)}, u32[]{:S(2)}) copy-start(s32[16,128,128]{2,1,0:T(8,128)} %mask.3) | copy-start | bytes 3145732
  5.3 1.2 %copy-start.4 = (f32[16,128,128]{2,1,0:T(8,128)S(1)}, f32[16,128,128]{2,1,0:T(8,128)}, u32[]{:S(2)}) copy-start(f32[16,128,128]{2,1,0:T(8,128)} %east.1) | copy-start | bytes 3145732
  9.2 12.5 %collective-permute-start.1 = (f32[24,8,128]{2,1,0:T(8,128)S(1)}, f32[24,8,128]{2,1,0:T(8,128)S(1)}, u32[]{:S(2)}, u32[]{:S(2)}) collective-permute-start(f32[24,8,128]{2,1,0:T(8,128)S(1)} %get-tuple-element.20.ew), channel_id=1, source_target_pairs={{16,32},{32,16},{48,64},{64,48},{80,96},{96,80},{112,0},{0,112},{1... | collective-permute-start | bytes 294920 | tf_op jit(solution)/shard_map/ppermute | solution.py:710
  13.3 8.4 %collective-permute-start = (f32[24,8,128]{2,1,0:T(8,128)S(1)}, f32[24,8,128]{2,1,0:T(8,128)S(1)}, u32[]{:S(2)}, u32[]{:S(2)}) collective-permute-start(f32[24,8,128]{2,1,0:T(8,128)S(1)} %get-tuple-element.20.ew), channel_id=1, source_target_pairs={{0,16},{16,0},{32,48},{48,32},{64,80},{80,64},{96,112},{112,96},{1... | collective-permute-start | bytes 294920 | tf_op jit(solution)/shard_map/ppermute | solution.py:709
  13.3 2.5 %copy-start.1 = (f32[4,16,128,128]{3,2,1,0:T(8,128)S(1)}, f32[4,16,128,128]{3,2,1,0:T(8,128)}, u32[]{:S(2)}) copy-start(f32[4,16,128,128]{3,2,1,0:T(8,128)} %tr.3) | copy-start | bytes 12582916
  13.4 2.8 %copy-start.5 = (f32[16,128,128]{2,1,0:T(8,128)S(1)}, f32[16,128,128]{2,1,0:T(8,128)}, u32[]{:S(2)}) copy-start(f32[16,128,128]{2,1,0:T(8,128)} %east.1) | copy-start | bytes 3145732
  13.4 3.1 %copy-start.6 = (f32[16,128,128]{2,1,0:T(8,128)S(1)}, f32[16,128,128]{2,1,0:T(8,128)}, u32[]{:S(2)}) copy-start(f32[16,128,128]{2,1,0:T(8,128)} %north.3) | copy-start | bytes 3145732
  13.4 3.1 %copy-start.7 = (f32[128,128]{1,0:T(8,128)S(1)}, f32[128,128]{1,0:T(8,128)}, u32[]{:S(2)}) copy-start(f32[128,128]{1,0:T(8,128)} %area.1) | copy-start | bytes 196612
  14.8 7.0 %collective-permute-start.2 = (f32[96,128]{1,0:T(8,128)S(1)}, f32[96,128]{1,0:T(8,128)S(1)}, u32[]{:S(2)}, u32[]{:S(2)}) collective-permute-start(f32[96,128]{1,0:T(8,128)S(1)} %get-tuple-element.21.ns_one), channel_id=1, source_target_pairs={{0,1},{1,0},{2,3},{3,2},{4,5},{5,4},{6,7},{7,6},{8,9},{9,8},{10,11... | collective-permute-start | bytes 147464 | tf_op jit(solution)/shard_map/ppermute | solution.py:706
  14.9 6.9 %collective-permute-start.3 = (f32[96,128]{1,0:T(8,128)S(1)}, f32[96,128]{1,0:T(8,128)S(1)}, u32[]{:S(2)}, u32[]{:S(2)}) collective-permute-start(f32[96,128]{1,0:T(8,128)S(1)} %get-tuple-element.22.ns_two), channel_id=1, source_target_pairs={{1,2},{2,1},{3,4},{4,3},{5,6},{6,5},{7,8},{8,7},{9,10},{10,9},{11,... | collective-permute-start | bytes 147464 | tf_op jit(solution)/shard_map/ppermute | solution.py:707
  25.4 48.2 %all-to-all-start = ((f32[128,40,128]{2,1,0:T(8,128)}), f32[128,40,128]{2,1,0:T(8,128)S(1)}, u32[]{:S(2)}, u32[]{:S(2)}) async-start(f32[128,40,128]{2,1,0:T(8,128)} %bitcast.6), calls=%async_computation | async-start | bytes 5242880 | tf_op jit(solution)/shard_map/all_to_all | solution.py:719

commit v9 on v8

--- a/solution.py
+++ b/solution.py
@@ -17,6 +17,8 @@
 CHUNKS = 20
 PARTS = 2
 EACH = 16
+PAIR = 2
+STEP = 8
 F32, BF16 = jnp.float32, jnp.bfloat16
 MIB = 1 << 20
 
@@ -197,7 +199,12 @@
             ew[v] = packed
         return carry
 
-    lax.fori_loop(0, LV, level, 0)
+    def step(n, carry):
+        for m in range(STEP):
+            level(n * STEP + m, carry)
+        return carry
+
+    lax.fori_loop(0, LV // STEP, step, 0)
 
 
 def kernel_edges_call(tracers, fill, mask, east):
@@ -219,7 +226,7 @@
 def kernel_first(
     tr_s, h_v, east_s, north_s, area_v, diff, pool,
     num2, den2,
-    area_s, g_s, face_s, coef, store,
+    area_s, gains, all_faces, coefs, stores,
 ):
     lane, sub = lane_iota(), sub_iota()
     is_even = (lane & 1) == 0
@@ -228,8 +235,9 @@
     for v in range(16):
         area_s[v] = 2.0 * area_v[row_set(32 * (v // 4) + v % 4)]
 
-    def level(k):
+    def level(k, n):
         twice_mixing = 2.0 * diff[k]
+        g_s, face_s, coef, store = gains.at[n], all_faces.at[n], coefs.at[n], stores.at[n]
 
         for v in range(16):
             h, u = h_v[k, v], east_s[(k, *row_set(32 * (v // 4) + v % 4))]
@@ -306,8 +314,8 @@
                     value = value + jnp.take_along_axis(side, swap, axis=1)
                     store[pl.ds(t * 32 + q * 8, 8), pl.ds(par * 128, 128)] = value
 
-    def pooled(k):
-        both = jnp.concatenate(halves(store[...]), axis=1)
+    def pooled(k, n):
+        both = jnp.concatenate(halves(stores[n]), axis=1)
         values = jnp.dot(both, pool[...], preferred_element_type=F32)
         rows = pl.ds(pl.multiple_of(k * 32, 32), 32)
         for t in range(TR):
@@ -315,13 +323,16 @@
         den2[rows, :] = values[128:160]
 
     def group_body(k, carry):
-        pooled((k + LV - 1) % LV)
-        level(k)
+        for n in range(PAIR):
+            pooled((k * PAIR + n + LV - PAIR) % LV, n)
+        for n in range(PAIR):
+            level(k * PAIR + n, n)
         return carry
 
-    store[...] = jnp.zeros_like(store)
-    lax.fori_loop(0, LV, group_body, 0)
-    pooled(LV - 1)
+    stores[...] = jnp.zeros_like(stores)
+    lax.fori_loop(0, LV // PAIR, group_body, 0)
+    for n in range(PAIR):
+        pooled(LV - PAIR + n, n)
 
 
 def kernel_first_call(tr_v, h_v, east_v, north_v, area_v, diff, pool):
@@ -337,10 +348,10 @@
         out_specs=(vmem,) * 2,
         scratch_shapes=[
             pltpu.VMEM((16, 8, 128), F32),
-            pltpu.VMEM((16, 8, 128), F32),
-            pltpu.VMEM((4, 16, 8, 128), F32),
-            pltpu.VMEM((6, 8, 8, 128), F32),
-            pltpu.VMEM((160, 256), F32),
+            pltpu.VMEM((PAIR, 16, 8, 128), F32),
+            pltpu.VMEM((PAIR, 4, 16, 8, 128), F32),
+            pltpu.VMEM((PAIR, 6, 8, 8, 128), F32),
+            pltpu.VMEM((PAIR, 160, 256), F32),
         ],
         compiler_params=pltpu.CompilerParams(vmem_limit_bytes=16 * MIB),
         cost_estimate=pl.CostEstimate(flops=60_000_000, bytes_accessed=11 * MIB, transcendentals=0),

time: 75.9 us -> 74.1 us (0.976)
  Pallas kernels: 28.4 us -> 26.7 us
    pallas_call x1, Pallas kernels: 2.71 us -> 1.77 us  [kernel_edges_call(): pl.pallas_call(kernel_edges, name='edges', out_shape=(jax.ShapeDtypeStruc...]
    pallas_call x1, Pallas kernels: 5.29 us -> 4.46 us  [kernel_first_call(): pl.pallas_call(kernel_first, name='first', out_shape=(jax.ShapeDtypeStruc...]
  transfers between devices with their start and end apart: 5 -> 5, of which waited for: 1 -> 1; matrix products, arithmetic and copies ran while one was open for 0% -> 0% of each run, Pallas kernels for 27% -> 26%
where the time goes in v9:
time: 74.1 us; the launch traced here: 73.7 us
  Pallas kernels  26.7 us (36%)
  waiting for transfers between devices  22.2 us (30%)
  starting transfers between devices  17.5 us (24%)
  local copies, waits for them, and re-layouts  6.62 us (9%)
  between operations  0.75 us (1%)
    all_to_all x1, waiting for transfers between devices, local(): lax.all_to_all(send.reshape(DEV, CAP * CHUNKS, 128), both, split_axis=0,...  22.2 us
    pallas_call x1, Pallas kernels, kernel_third_call(): pl.pallas_call(kernel_third, name='third', out_shape=jax.ShapeDtypeStruct...  13.5 us
    all_to_all x1, starting transfers between devices, local(): lax.all_to_all(send.reshape(DEV, CAP * CHUNKS, 128), both, split_axis=0,...  12.5 us
    unnamed x16, local copies, waits for them, and re-layouts  6.62 us
    pallas_call x1, Pallas kernels, kernel_first_call(): pl.pallas_call(kernel_first, name='first', out_shape=(jax.ShapeDtypeStruc...  4.46 us
    ppermute x1, starting transfers between devices, local(): lax.ppermute(ew, 'lon', swapped([(n, (n + 1) % lon_count) for n in range(...  4.13 us
    pallas_call x1, Pallas kernels, kernel_second_call(): pl.pallas_call(kernel_second, name='second', out_shape=(pltpu.HBM((DEV *...  3.58 us
    pallas_call x1, Pallas kernels, kernel_last_call(): pl.pallas_call(kernel_last, name='last', grid=(SPLITS,), out_shape=(jax.S...  1.96 us
  transfers between devices with their start and end apart: 5, of which 1 were waited for; matrix products, arithmetic and copies ran while one was open for 0% of the time, Pallas kernels for 26%

profile of v9, /device:TPU:0, one launch (start us, length us, event | category | flops | bytes accessed | tf_op | source)
XLA Modules:
  0.0 73.7 jit_solution(5863048651244209584)
XLA Ops:
  0.6 0.0 copy-start
  0.6 2.2 %copy-done = f32[4,16,128,128]{3,2,1,0:T(8,128)S(1)} copy-done((f32[4,16,128,128]{3,2,1,0:T(8,128)S(1)}, f32[4,16,128,128]{3,2,1,0:T(8,128)}, u32[]{:S(2)}) %copy-start) | copy-done | bytes 4194328
  2.8 0.0 copy-start.2
  2.8 1.2 %copy-done.2 = f32[16,128,128]{2,1,0:T(8,128)S(1)} copy-done((f32[16,128,128]{2,1,0:T(8,128)S(1)}, f32[16,128,128]{2,1,0:T(8,128)}, u32[]{:S(2)}) %copy-start.2) | copy-done | bytes 1048600
  4.0 0.0 copy-start.3
  4.0 1.2 %copy-done.3 = s32[16,128,128]{2,1,0:T(8,128)S(1)} copy-done((s32[16,128,128]{2,1,0:T(8,128)S(1)}, s32[16,128,128]{2,1,0:T(8,128)}, u32[]{:S(2)}) %copy-start.3) | copy-done | bytes 1048600
  5.3 0.0 copy-start.4
  5.3 1.2 %copy-done.4 = f32[16,128,128]{2,1,0:T(8,128)S(1)} copy-done((f32[16,128,128]{2,1,0:T(8,128)S(1)}, f32[16,128,128]{2,1,0:T(8,128)}, u32[]{:S(2)}) %copy-start.4) | copy-done | bytes 1048600
  6.5 1.8 %edges.1 = (f32[16,16,8,128]{3,2,1,0:T(8,128)S(1)}, f32[24,8,128]{2,1,0:T(8,128)S(1)}) custom-call(f32[4,16,128,128]{3,2,1,0:T(8,128)S(1)} %copy-done, f32[16,128,128]{2,1,0:T(8,128)S(1)} %copy-done.2, s32[16,128,128]{2,1,0:T(8,128)S(1)} %copy-done.3, f32[16,128,128]{2,1,0:T(8,128)S(1)} %copy-done.4), custom_call_target="tpu_custom_call" | custom-call | flops 60000000 | bytes 11534336 | tf_op jit(solution)/shard_map/edges/pallas_call | solution.py:212
  8.3 4.1 %collective-permute-start.1 = (f32[24,8,128]{2,1,0:T(8,128)S(1)}, f32[24,8,128]{2,1,0:T(8,128)S(1)}, u32[]{:S(2)}, u32[]{:S(2)}) collective-permute-start(f32[24,8,128]{2,1,0:T(8,128)S(1)} %get-tuple-element.20.ew), channel_id=1, source_target_pairs={{16,32},{32,16},{48,64},{64,48},{80,96},{96,80},{112,0},{0,112},{1... | collective-permute-start | bytes 294920 | tf_op jit(solution)/shard_map/ppermute | solution.py:721
  12.4 0.0 collective-permute-start
  12.4 0.0 copy-start.1
  12.4 0.0 copy-start.5
  12.4 0.0 copy-start.6
  12.4 0.0 copy-start.7
  12.4 1.4 %rows.1 = (f32[96,128]{1,0:T(8,128)S(1)}, f32[96,128]{1,0:T(8,128)S(1)}, bf16[256,256]{1,0:T(8,128)(2,1)S(1)}, bf16[512,128]{1,0:T(8,128)(2,1)S(1)}) custom-call(f32[4,16,128,128]{3,2,1,0:T(8,128)} %tr.3, f32[16,128,128]{2,1,0:T(8,128)} %fill.3, s32[16,128,128]{2,1,0:T(8,128)} %mask.3, f32[16,128,128]{2,1,0:T(8,128)} %north.3, s32[1,128]{1,0:T(1,128)} %bitcast.7), custom_call_target="tpu_custom_call" | custom-call | flops 1000000 | bytes 1048576 | tf_op jit(solution)/shard_map/rows/pallas_call | solution.py:150
  13.8 0.1 collective-permute-start.2
  13.9 0.8 %collective-permute-start.3 = (f32[96,128]{1,0:T(8,128)S(1)}, f32[96,128]{1,0:T(8,128)S(1)}, u32[]{:S(2)}, u32[]{:S(2)}) collective-permute-start(f32[96,128]{1,0:T(8,128)S(1)} %get-tuple-element.22.ns_two), channel_id=1, source_target_pairs={{1,2},{2,1},{3,4},{4,3},{5,6},{6,5},{7,8},{8,7},{9,10},{10,9},{11,... | collective-permute-start | bytes 147464 | tf_op jit(solution)/shard_map/ppermute | solution.py:718
  14.7 0.1 copy-done.1
  14.9 0.3 copy-done.5
  15.2 0.3 copy-done.6
  15.5 0.0 copy-done.7
  15.5 4.5 %first.1 = (f32[4,512,128]{2,1,0:T(8,128)S(1)}, f32[512,128]{1,0:T(8,128)S(1)}) custom-call(f32[4,16,128,128]{3,2,1,0:T(8,128)S(1)} %copy-done.1, f32[16,16,8,128]{3,2,1,0:T(8,128)S(1)} %get-tuple-element.16.h_v, f32[16,128,128]{2,1,0:T(8,128)S(1)} %copy-done.5, f32[16,128,128]{2,1,0:T(8,128)S(1)} %copy-done.6, f32[128,128]{1,0:T(8,128)S(1)} %copy-done.7, ...), custom_call_target="tpu_custom_call" | custom-call | flops 60000000 | bytes 11534336 | tf_op jit(solution)/shard_map/first/pallas_call | solution.py:340
  20.0 0.0 collective-permute-done.2.got_one
  20.0 0.0 collective-permute-done.3.got_two
  20.0 0.0 collective-permute-done.1.ew_two
  20.0 0.0 collective-permute-done.ew_one
  20.0 3.6 %second.1 = (f32[5120,128]{1,0:T(8,128)}, f32[16,8,128]{2,1,0:T(8,128)S(1)}, f32[2,64,128]{2,1,0:T(8,128)S(1)}) custom-call(f32[4,512,128]{2,1,0:T(8,128)S(1)} %get-tuple-element.18.num2, f32[512,128]{1,0:T(8,128)S(1)} %get-tuple-element.19.den2, f32[24,8,128]{2,1,0:T(8,128)S(1)} %get-tuple-element.20.ew, f32[24,8,128]{2,1,0:T(8,128)S(1)} %collective-permute-done.ew_one, ...), custom_call_target="tpu_custom_call" | custom-call | flops 60000000 | bytes 6291456 | tf_op jit(solution)/shard_map/second/pallas_call | solution.py:515
  23.6 12.5 %all-to-all-start = ((f32[128,40,128]{2,1,0:T(8,128)}), f32[128,40,128]{2,1,0:T(8,128)S(1)}, u32[]{:S(2)}, u32[]{:S(2)}) async-start(f32[128,40,128]{2,1,0:T(8,128)} %bitcast.6), calls=%async_computation | async-start | bytes 5242880 | tf_op jit(solution)/shard_map/all_to_all | solution.py:730
  36.1 13.5 %third.1 = f32[4,16,128,128]{3,2,1,0:T(8,128)} custom-call(f32[4,16,128,128]{3,2,1,0:T(8,128)} %tr.3, f32[16,128,128]{2,1,0:T(8,128)} %fill.3, s32[16,128,128]{2,1,0:T(8,128)} %mask.3, f32[16,128,128]{2,1,0:T(8,128)} %east.1, f32[16,128,128]{2,1,0:T(8,128)} %north.3, f32[16]{0:T(128)} %diff.5, f32[128,128]{1,0:T(8,128)} %area.1, ...), custom_call_target="tpu_custom_call" | custom-call | flops 60000000 | bytes 12582912 | tf_op jit(solution)/shard_map/third/pallas_call | solution.py:633
  49.6 22.2 %all-to-all-done = f32[128,40,128]{2,1,0:T(8,128)S(1)} async-done(((f32[128,40,128]{2,1,0:T(8,128)}), f32[128,40,128]{2,1,0:T(8,128)S(1)}, u32[]{:S(2)}, u32[]{:S(2)}) %all-to-all-start) | async-done | bytes 2621472 | tf_op jit(solution)/shard_map/all_to_all | solution.py:730
  71.8 2.0 %last.1 = (f32[256,2048]{1,0:T(8,128)}, f32[256,512]{1,0:T(8,128)}) custom-call(f32[5120,128]{1,0:T(8,128)S(1)} %bitcast.5), custom_call_target="tpu_custom_call" | custom-call | tf_op jit(solution)/shard_map/last/pallas_call | solution.py:671
Async XLA Ops:
  0.6 2.2 %copy-start = (f32[4,16,128,128]{3,2,1,0:T(8,128)S(1)}, f32[4,16,128,128]{3,2,1,0:T(8,128)}, u32[]{:S(2)}) copy-start(f32[4,16,128,128]{3,2,1,0:T(8,128)} %tr.3) | copy-start | bytes 12582916
  2.8 1.2 %copy-start.2 = (f32[16,128,128]{2,1,0:T(8,128)S(1)}, f32[16,128,128]{2,1,0:T(8,128)}, u32[]{:S(2)}) copy-start(f32[16,128,128]{2,1,0:T(8,128)} %fill.3) | copy-start | bytes 3145732
  4.0 1.2 %copy-start.3 = (s32[16,128,128]{2,1,0:T(8,128)S(1)}, s32[16,128,128]{2,1,0:T(8,128)}, u32[]{:S(2)}) copy-start(s32[16,128,128]{2,1,0:T(8,128)} %mask.3) | copy-start | bytes 3145732
  5.3 1.2 %copy-start.4 = (f32[16,128,128]{2,1,0:T(8,128)S(1)}, f32[16,128,128]{2,1,0:T(8,128)}, u32[]{:S(2)}) copy-start(f32[16,128,128]{2,1,0:T(8,128)} %east.1) | copy-start | bytes 3145732
  8.3 11.7 %collective-permute-start.1 = (f32[24,8,128]{2,1,0:T(8,128)S(1)}, f32[24,8,128]{2,1,0:T(8,128)S(1)}, u32[]{:S(2)}, u32[]{:S(2)}) collective-permute-start(f32[24,8,128]{2,1,0:T(8,128)S(1)} %get-tuple-element.20.ew), channel_id=1, source_target_pairs={{16,32},{32,16},{48,64},{64,48},{80,96},{96,80},{112,0},{0,112},{1... | collective-permute-start | bytes 294920 | tf_op jit(solution)/shard_map/ppermute | solution.py:721
  12.4 7.6 %collective-permute-start = (f32[24,8,128]{2,1,0:T(8,128)S(1)}, f32[24,8,128]{2,1,0:T(8,128)S(1)}, u32[]{:S(2)}, u32[]{:S(2)}) collective-permute-start(f32[24,8,128]{2,1,0:T(8,128)S(1)} %get-tuple-element.20.ew), channel_id=1, source_target_pairs={{0,16},{16,0},{32,48},{48,32},{64,80},{80,64},{96,112},{112,96},{1... | collective-permute-start | bytes 294920 | tf_op jit(solution)/shard_map/ppermute | solution.py:720
  12.4 2.5 %copy-start.1 = (f32[4,16,128,128]{3,2,1,0:T(8,128)S(1)}, f32[4,16,128,128]{3,2,1,0:T(8,128)}, u32[]{:S(2)}) copy-start(f32[4,16,128,128]{3,2,1,0:T(8,128)} %tr.3) | copy-start | bytes 12582916
  12.4 2.8 %copy-start.5 = (f32[16,128,128]{2,1,0:T(8,128)S(1)}, f32[16,128,128]{2,1,0:T(8,128)}, u32[]{:S(2)}) copy-start(f32[16,128,128]{2,1,0:T(8,128)} %east.1) | copy-start | bytes 3145732
  12.4 3.1 %copy-start.6 = (f32[16,128,128]{2,1,0:T(8,128)S(1)}, f32[16,128,128]{2,1,0:T(8,128)}, u32[]{:S(2)}) copy-start(f32[16,128,128]{2,1,0:T(8,128)} %north.3) | copy-start | bytes 3145732
  12.4 3.1 %copy-start.7 = (f32[128,128]{1,0:T(8,128)S(1)}, f32[128,128]{1,0:T(8,128)}, u32[]{:S(2)}) copy-start(f32[128,128]{1,0:T(8,128)} %area.1) | copy-start | bytes 196612
  13.8 6.1 %collective-permute-start.2 = (f32[96,128]{1,0:T(8,128)S(1)}, f32[96,128]{1,0:T(8,128)S(1)}, u32[]{:S(2)}, u32[]{:S(2)}) collective-permute-start(f32[96,128]{1,0:T(8,128)S(1)} %get-tuple-element.21.ns_one), channel_id=1, source_target_pairs={{0,1},{1,0},{2,3},{3,2},{4,5},{5,4},{6,7},{7,6},{8,9},{9,8},{10,11... | collective-permute-start | bytes 147464 | tf_op jit(solution)/shard_map/ppermute | solution.py:717
  13.9 6.0 %collective-permute-start.3 = (f32[96,128]{1,0:T(8,128)S(1)}, f32[96,128]{1,0:T(8,128)S(1)}, u32[]{:S(2)}, u32[]{:S(2)}) collective-permute-start(f32[96,128]{1,0:T(8,128)S(1)} %get-tuple-element.22.ns_two), channel_id=1, source_target_pairs={{1,2},{2,1},{3,4},{4,3},{5,6},{6,5},{7,8},{8,7},{9,10},{10,9},{11,... | collective-permute-start | bytes 147464 | tf_op jit(solution)/shard_map/ppermute | solution.py:718
  23.6 48.2 %all-to-all-start = ((f32[128,40,128]{2,1,0:T(8,128)}), f32[128,40,128]{2,1,0:T(8,128)S(1)}, u32[]{:S(2)}, u32[]{:S(2)}) async-start(f32[128,40,128]{2,1,0:T(8,128)} %bitcast.6), calls=%async_computation | async-start | bytes 5242880 | tf_op jit(solution)/shard_map/all_to_all | solution.py:730

commit v10 on v9

--- a/solution.py
+++ b/solution.py
@@ -88,7 +88,7 @@
 
 def kernel_rows(
     tr, fill, mask, north, owner,
-    ns_one, ns_two, placing, pool,
+    ns_one, ns_two, placing, pool, shares,
     tr_s, fill_s, mask_s, north_s, owner_s, sems, owner_sem,
 ):
     copies = []
@@ -110,6 +110,10 @@
     match = lane_iota((256, 128)) == (source >> 7) * 64 + ((source & 127) >> 1)
     for term in range(2):
         pool[pl.ds(256 * term, 256), :] = jnp.where(match, 1.0, 0.0).astype(BF16)
+    source, target = sub_iota((128, 128)), lane_iota((128, 128))
+    for n in range(6):
+        place = n * 64 + (source >> 1) if n < 2 else (n - 2) * 32 + ((source & 63) >> 1)
+        shares[n] = jnp.where(target == place, 1.0, 0.0).astype(BF16)
     across = lane_iota((DEV, DEV))
     down = sub_iota((DEV, DEV))
     owner_copy.wait()
@@ -155,9 +159,10 @@
             jax.ShapeDtypeStruct((96, 128), F32),
             jax.ShapeDtypeStruct((CAP * DEV, 2 * DEV), BF16),
             jax.ShapeDtypeStruct((512, 128), BF16),
+            jax.ShapeDtypeStruct((6, 128, 128), BF16),
         ),
         in_specs=[hbm] * 5,
-        out_specs=(vmem,) * 4,
+        out_specs=(vmem,) * 5,
         scratch_shapes=[
             pltpu.VMEM((2, TR, LV, 8, LANES), F32),
             pltpu.VMEM((2, LV, 8, LANES), F32),
@@ -364,7 +369,7 @@
 
 
 def kernel_second(
-    num2, den2, ew, ew_one, ew_two, ns_one, ns_two, got_one, got_two, diff, placing,
+    num2, den2, ew, ew_one, ew_two, ns_one, ns_two, got_one, got_two, diff, placing, shares,
     send, d_ew, d_ns,
     work, acc, chunks, send_s, sems,
 ):
@@ -424,14 +429,8 @@
 
     lax.fori_loop(0, LV // EACH, add_ends, 0)
 
-    source = sub_iota((128, 128))
-    target = lane_iota((128, 128))
-    pools = [
-        jnp.where(target == par * 64 + (source >> 1), 1.0, 0.0).astype(BF16) for par in range(2)
-    ]
-    quarter = [
-        jnp.where(target == j * 32 + ((source & 63) >> 1), 1.0, 0.0).astype(BF16) for j in range(4)
-    ]
+    pools = [shares[par] for par in range(2)]
+    quarter = [shares[2 + j] for j in range(4)]
 
     back = 127 - lane
     for half in range(2):
@@ -520,7 +519,7 @@
             jax.ShapeDtypeStruct((16, 8, 128), F32),
             jax.ShapeDtypeStruct((2, 64, 128), F32),
         ),
-        in_specs=[vmem] * 9 + [pl.BlockSpec(memory_space=pltpu.SMEM), vmem],
+        in_specs=[vmem] * 9 + [pl.BlockSpec(memory_space=pltpu.SMEM), vmem, vmem],
         out_specs=(pl.BlockSpec(memory_space=pltpu.HBM), vmem, vmem),
         scratch_shapes=[
             pltpu.VMEM((2, 4, 8, 128), F32),
@@ -657,30 +656,38 @@
 SPLITS = 4
 
 
-def kernel_last(got, two, four):
-    for m in range(32 // SPLITS):
-        for n in range(CHUNKS):
-            value = got[pl.ds(m * 8 * CHUNKS + n, 8, stride=CHUNKS), :]
-            if n < 16:
-                two[pl.ds(m * 8, 8), pl.ds(n * 128, 128)] = value
-            else:
-                four[pl.ds(m * 8, 8), pl.ds((n - 16) * 128, 128)] = value
+def kernel_last(got, two, four, two_s, four_s, sems):
+    each = DEV * CAP // SPLITS
+    copies = []
+    for part in range(SPLITS):
+        for m in range(part * each // 8, (part + 1) * each // 8):
+            for n in range(CHUNKS):
+                value = got[pl.ds(m * 8 * CHUNKS + n, 8, stride=CHUNKS), :]
+                if n < 16:
+                    two_s[pl.ds(m * 8, 8), pl.ds(n * 128, 128)] = value
+                else:
+                    four_s[pl.ds(m * 8, 8), pl.ds((n - 16) * 128, 128)] = value
+        rows = pl.ds(part * each, each)
+        for n, (src, dst) in enumerate(((two_s, two), (four_s, four))):
+            copies.append(pltpu.make_async_copy(src.at[rows], dst.at[rows], sems.at[n, part]))
+            copies[-1].start()
+    for copy in copies:
+        copy.wait()
 
 
 def kernel_last_call(got):
+    hbm = pl.BlockSpec(memory_space=pltpu.HBM)
     return pl.pallas_call(
         kernel_last,
         name="last",
-        grid=(SPLITS,),
-        out_shape=(
-            jax.ShapeDtypeStruct((DEV * CAP, 2048), F32),
-            jax.ShapeDtypeStruct((DEV * CAP, 512), F32),
-        ),
-        in_specs=[pl.BlockSpec((DEV * 40 // SPLITS, 128), lambda s: (s, 0))],
-        out_specs=(
-            pl.BlockSpec((DEV * CAP // SPLITS, 2048), lambda s: (s, 0)),
-            pl.BlockSpec((DEV * CAP // SPLITS, 512), lambda s: (s, 0)),
-        ),
+        out_shape=(pltpu.HBM((DEV * CAP, 2048), F32), pltpu.HBM((DEV * CAP, 512), F32)),
+        in_specs=[pl.BlockSpec(memory_space=pltpu.VMEM)],
+        out_specs=(hbm, hbm),
+        scratch_shapes=[
+            pltpu.VMEM((DEV * CAP, 2048), F32),
+            pltpu.VMEM((DEV * CAP, 512), F32),
+            pltpu.SemaphoreType.DMA((2, SPLITS)),
+        ],
         compiler_params=pltpu.CompilerParams(vmem_limit_bytes=8 * MIB),
     )(got)
 
@@ -697,7 +704,7 @@
             owner_map.reshape(1, DEV),
         )
     )
-    ns_one, ns_two, placing, pool = kernel_rows_call(
+    ns_one, ns_two, placing, pool, shares = kernel_rows_call(
         in_hbm[0], in_hbm[1], in_hbm[2], in_hbm[4], owners
     )
     both = ("lon", "lat")
@@ -725,7 +732,8 @@
         tracers, h_v, east_speed, north_speed, cell_area, diffusivity, pool
     )
     send, d_ew, d_ns = kernel_second_call(
-        num2, den2, ew, ew_one, ew_two, ns_one, ns_two, got_one, got_two, diffusivity, placing
+        num2, den2, ew, ew_one, ew_two, ns_one, ns_two, got_one, got_two, diffusivity, placing,
+        shares,
     )
     got = lax.all_to_all(
         send.reshape(DEV, CAP * CHUNKS, 128), both, split_axis=0, concat_axis=0, tiled=True

time: 74.1 us -> 73.7 us (level)
  no operation moved by 1% of the time
where the time goes in v10:
time: 73.7 us; the launch traced here: 73.4 us
  Pallas kernels  26.3 us (36%)
  waiting for transfers between devices  22.2 us (30%)
  starting transfers between devices  17.5 us (24%)
  local copies, waits for them, and re-layouts  6.62 us (9%)
  between operations  0.75 us (1%)
    all_to_all x1, waiting for transfers between devices, local(): lax.all_to_all(send.reshape(DEV, CAP * CHUNKS, 128), both, split_axis=0,...  22.2 us
    pallas_call x1, Pallas kernels, kernel_third_call(): pl.pallas_call(kernel_third, name='third', out_shape=jax.ShapeDtypeStruct...  13.5 us
    all_to_all x1, starting transfers between devices, local(): lax.all_to_all(send.reshape(DEV, CAP * CHUNKS, 128), both, split_axis=0,...  12.5 us
    unnamed x16, local copies, waits for them, and re-layouts  6.62 us
    pallas_call x1, Pallas kernels, kernel_first_call(): pl.pallas_call(kernel_first, name='first', out_shape=(jax.ShapeDtypeStruc...  4.46 us
    ppermute x1, starting transfers between devices, local(): lax.ppermute(ew, 'lon', swapped([(n, (n + 1) % lon_count) for n in range(...  4.13 us
    pallas_call x1, Pallas kernels, kernel_second_call(): pl.pallas_call(kernel_second, name='second', out_shape=(pltpu.HBM((DEV *...  3.58 us
    pallas_call x1, Pallas kernels, kernel_edges_call(): pl.pallas_call(kernel_edges, name='edges', out_shape=(jax.ShapeDtypeStruc...  1.77 us
  transfers between devices with their start and end apart: 5, of which 1 were waited for; matrix products, arithmetic and copies ran while one was open for 0% of the time, Pallas kernels for 26%

profile of v10, /device:TPU:0, one launch (start us, length us, event | category | flops | bytes accessed | tf_op | source)
XLA Modules:
  0.0 73.4 jit_solution(11876094231405079984)
XLA Ops:
  0.6 0.0 copy-start
  0.6 2.2 %copy-done = f32[4,16,128,128]{3,2,1,0:T(8,128)S(1)} copy-done((f32[4,16,128,128]{3,2,1,0:T(8,128)S(1)}, f32[4,16,128,128]{3,2,1,0:T(8,128)}, u32[]{:S(2)}) %copy-start) | copy-done | bytes 4194328
  2.8 0.0 copy-start.2
  2.8 1.2 %copy-done.2 = f32[16,128,128]{2,1,0:T(8,128)S(1)} copy-done((f32[16,128,128]{2,1,0:T(8,128)S(1)}, f32[16,128,128]{2,1,0:T(8,128)}, u32[]{:S(2)}) %copy-start.2) | copy-done | bytes 1048600
  4.0 0.0 copy-start.3
  4.0 1.2 %copy-done.3 = s32[16,128,128]{2,1,0:T(8,128)S(1)} copy-done((s32[16,128,128]{2,1,0:T(8,128)S(1)}, s32[16,128,128]{2,1,0:T(8,128)}, u32[]{:S(2)}) %copy-start.3) | copy-done | bytes 1048600
  5.3 0.0 copy-start.4
  5.3 1.2 %copy-done.4 = f32[16,128,128]{2,1,0:T(8,128)S(1)} copy-done((f32[16,128,128]{2,1,0:T(8,128)S(1)}, f32[16,128,128]{2,1,0:T(8,128)}, u32[]{:S(2)}) %copy-start.4) | copy-done | bytes 1048600
  6.5 1.8 %edges.1 = (f32[16,16,8,128]{3,2,1,0:T(8,128)S(1)}, f32[24,8,128]{2,1,0:T(8,128)S(1)}) custom-call(f32[4,16,128,128]{3,2,1,0:T(8,128)S(1)} %copy-done, f32[16,128,128]{2,1,0:T(8,128)S(1)} %copy-done.2, s32[16,128,128]{2,1,0:T(8,128)S(1)} %copy-done.3, f32[16,128,128]{2,1,0:T(8,128)S(1)} %copy-done.4), custom_call_target="tpu_custom_call" | custom-call | flops 60000000 | bytes 11534336 | tf_op jit(solution)/shard_map/edges/pallas_call | solution.py:217
  8.3 4.1 %collective-permute-start.1 = (f32[24,8,128]{2,1,0:T(8,128)S(1)}, f32[24,8,128]{2,1,0:T(8,128)S(1)}, u32[]{:S(2)}, u32[]{:S(2)}) collective-permute-start(f32[24,8,128]{2,1,0:T(8,128)S(1)} %get-tuple-element.21.ew), channel_id=1, source_target_pairs={{16,32},{32,16},{48,64},{64,48},{80,96},{96,80},{112,0},{0,112},{1... | collective-permute-start | bytes 294920 | tf_op jit(solution)/shard_map/ppermute | solution.py:728
  12.4 0.0 collective-permute-start
  12.4 0.0 copy-start.1
  12.4 0.0 copy-start.5
  12.4 0.0 copy-start.6
  12.4 0.0 copy-start.7
  12.4 1.4 %rows.1 = (f32[96,128]{1,0:T(8,128)S(1)}, f32[96,128]{1,0:T(8,128)S(1)}, bf16[256,256]{1,0:T(8,128)(2,1)S(1)}, bf16[512,128]{1,0:T(8,128)(2,1)S(1)}, bf16[6,128,128]{2,1,0:T(8,128)(2,1)S(1)}) custom-call(f32[4,16,128,128]{3,2,1,0:T(8,128)} %tr.3, f32[16,128,128]{2,1,0:T(8,128)} %fill.3, s32[16,128,128]{2,1,0:T(8,128)} %mask.3, f32[16,128,128]{2,1,0:T(8,128)} %north.3, ...), custom_call_target="tpu_custom_call" | custom-call | flops 1000000 | bytes 1048576 | tf_op jit(solution)/shard_map/rows/pallas_call | solution.py:154
  13.8 0.1 collective-permute-start.2
  13.9 0.8 %collective-permute-start.3 = (f32[96,128]{1,0:T(8,128)S(1)}, f32[96,128]{1,0:T(8,128)S(1)}, u32[]{:S(2)}, u32[]{:S(2)}) collective-permute-start(f32[96,128]{1,0:T(8,128)S(1)} %get-tuple-element.23.ns_two), channel_id=1, source_target_pairs={{1,2},{2,1},{3,4},{4,3},{5,6},{6,5},{7,8},{8,7},{9,10},{10,9},{11,... | collective-permute-start | bytes 147464 | tf_op jit(solution)/shard_map/ppermute | solution.py:725
  14.7 0.1 copy-done.1
  14.9 0.3 copy-done.5
  15.2 0.3 copy-done.6
  15.5 0.0 copy-done.7
  15.5 4.5 %first.1 = (f32[4,512,128]{2,1,0:T(8,128)S(1)}, f32[512,128]{1,0:T(8,128)S(1)}) custom-call(f32[4,16,128,128]{3,2,1,0:T(8,128)S(1)} %copy-done.1, f32[16,16,8,128]{3,2,1,0:T(8,128)S(1)} %get-tuple-element.17.h_v, f32[16,128,128]{2,1,0:T(8,128)S(1)} %copy-done.5, f32[16,128,128]{2,1,0:T(8,128)S(1)} %copy-done.6, f32[128,128]{1,0:T(8,128)S(1)} %copy-done.7, ...), custom_call_target="tpu_custom_call" | custom-call | flops 60000000 | bytes 11534336 | tf_op jit(solution)/shard_map/first/pallas_call | solution.py:345
  20.0 0.0 collective-permute-done.2.got_one
  20.0 0.0 collective-permute-done.3.got_two
  20.0 0.0 collective-permute-done.1.ew_two
  20.0 0.0 collective-permute-done.ew_one
  20.0 3.6 %second.1 = (f32[5120,128]{1,0:T(8,128)}, f32[16,8,128]{2,1,0:T(8,128)S(1)}, f32[2,64,128]{2,1,0:T(8,128)S(1)}) custom-call(f32[4,512,128]{2,1,0:T(8,128)S(1)} %get-tuple-element.19.num2, f32[512,128]{1,0:T(8,128)S(1)} %get-tuple-element.20.den2, f32[24,8,128]{2,1,0:T(8,128)S(1)} %get-tuple-element.21.ew, f32[24,8,128]{2,1,0:T(8,128)S(1)} %collective-permute-done.ew_one, ...), custom_call_target="tpu_custom_call" | custom-call | flops 60000000 | bytes 6291456 | tf_op jit(solution)/shard_map/second/pallas_call | solution.py:514
  23.6 12.5 %all-to-all-start = ((f32[128,40,128]{2,1,0:T(8,128)}), f32[128,40,128]{2,1,0:T(8,128)S(1)}, u32[]{:S(2)}, u32[]{:S(2)}) async-start(f32[128,40,128]{2,1,0:T(8,128)} %bitcast.6), calls=%async_computation | async-start | bytes 5242880 | tf_op jit(solution)/shard_map/all_to_all | solution.py:738
  36.1 13.5 %third.1 = f32[4,16,128,128]{3,2,1,0:T(8,128)} custom-call(f32[4,16,128,128]{3,2,1,0:T(8,128)} %tr.3, f32[16,128,128]{2,1,0:T(8,128)} %fill.3, s32[16,128,128]{2,1,0:T(8,128)} %mask.3, f32[16,128,128]{2,1,0:T(8,128)} %east.1, f32[16,128,128]{2,1,0:T(8,128)} %north.3, f32[16]{0:T(128)} %diff.5, f32[128,128]{1,0:T(8,128)} %area.1, ...), custom_call_target="tpu_custom_call" | custom-call | flops 60000000 | bytes 12582912 | tf_op jit(solution)/shard_map/third/pallas_call | solution.py:632
  49.6 22.2 %all-to-all-done = f32[128,40,128]{2,1,0:T(8,128)S(1)} async-done(((f32[128,40,128]{2,1,0:T(8,128)}), f32[128,40,128]{2,1,0:T(8,128)S(1)}, u32[]{:S(2)}, u32[]{:S(2)}) %all-to-all-start) | async-done | bytes 2621472 | tf_op jit(solution)/shard_map/all_to_all | solution.py:738
  71.8 1.6 %last.1 = (f32[256,2048]{1,0:T(8,128)}, f32[256,512]{1,0:T(8,128)}) custom-call(f32[5120,128]{1,0:T(8,128)S(1)} %bitcast.5), custom_call_target="tpu_custom_call" | custom-call | tf_op jit(solution)/shard_map/last/pallas_call | solution.py:680
Async XLA Ops:
  0.6 2.2 %copy-start = (f32[4,16,128,128]{3,2,1,0:T(8,128)S(1)}, f32[4,16,128,128]{3,2,1,0:T(8,128)}, u32[]{:S(2)}) copy-start(f32[4,16,128,128]{3,2,1,0:T(8,128)} %tr.3) | copy-start | bytes 12582916
  2.8 1.2 %copy-start.2 = (f32[16,128,128]{2,1,0:T(8,128)S(1)}, f32[16,128,128]{2,1,0:T(8,128)}, u32[]{:S(2)}) copy-start(f32[16,128,128]{2,1,0:T(8,128)} %fill.3) | copy-start | bytes 3145732
  4.0 1.2 %copy-start.3 = (s32[16,128,128]{2,1,0:T(8,128)S(1)}, s32[16,128,128]{2,1,0:T(8,128)}, u32[]{:S(2)}) copy-start(s32[16,128,128]{2,1,0:T(8,128)} %mask.3) | copy-start | bytes 3145732
  5.3 1.2 %copy-start.4 = (f32[16,128,128]{2,1,0:T(8,128)S(1)}, f32[16,128,128]{2,1,0:T(8,128)}, u32[]{:S(2)}) copy-start(f32[16,128,128]{2,1,0:T(8,128)} %east.1) | copy-start | bytes 3145732
  8.3 11.7 %collective-permute-start.1 = (f32[24,8,128]{2,1,0:T(8,128)S(1)}, f32[24,8,128]{2,1,0:T(8,128)S(1)}, u32[]{:S(2)}, u32[]{:S(2)}) collective-permute-start(f32[24,8,128]{2,1,0:T(8,128)S(1)} %get-tuple-element.21.ew), channel_id=1, source_target_pairs={{16,32},{32,16},{48,64},{64,48},{80,96},{96,80},{112,0},{0,112},{1... | collective-permute-start | bytes 294920 | tf_op jit(solution)/shard_map/ppermute | solution.py:728
  12.4 7.6 %collective-permute-start = (f32[24,8,128]{2,1,0:T(8,128)S(1)}, f32[24,8,128]{2,1,0:T(8,128)S(1)}, u32[]{:S(2)}, u32[]{:S(2)}) collective-permute-start(f32[24,8,128]{2,1,0:T(8,128)S(1)} %get-tuple-element.21.ew), channel_id=1, source_target_pairs={{0,16},{16,0},{32,48},{48,32},{64,80},{80,64},{96,112},{112,96},{1... | collective-permute-start | bytes 294920 | tf_op jit(solution)/shard_map/ppermute | solution.py:727
  12.4 2.5 %copy-start.1 = (f32[4,16,128,128]{3,2,1,0:T(8,128)S(1)}, f32[4,16,128,128]{3,2,1,0:T(8,128)}, u32[]{:S(2)}) copy-start(f32[4,16,128,128]{3,2,1,0:T(8,128)} %tr.3) | copy-start | bytes 12582916
  12.4 2.8 %copy-start.5 = (f32[16,128,128]{2,1,0:T(8,128)S(1)}, f32[16,128,128]{2,1,0:T(8,128)}, u32[]{:S(2)}) copy-start(f32[16,128,128]{2,1,0:T(8,128)} %east.1) | copy-start | bytes 3145732
  12.4 3.1 %copy-start.6 = (f32[16,128,128]{2,1,0:T(8,128)S(1)}, f32[16,128,128]{2,1,0:T(8,128)}, u32[]{:S(2)}) copy-start(f32[16,128,128]{2,1,0:T(8,128)} %north.3) | copy-start | bytes 3145732
  12.4 3.1 %copy-start.7 = (f32[128,128]{1,0:T(8,128)S(1)}, f32[128,128]{1,0:T(8,128)}, u32[]{:S(2)}) copy-start(f32[128,128]{1,0:T(8,128)} %area.1) | copy-start | bytes 196612
  13.8 6.1 %collective-permute-start.2 = (f32[96,128]{1,0:T(8,128)S(1)}, f32[96,128]{1,0:T(8,128)S(1)}, u32[]{:S(2)}, u32[]{:S(2)}) collective-permute-start(f32[96,128]{1,0:T(8,128)S(1)} %get-tuple-element.22.ns_one), channel_id=1, source_target_pairs={{0,1},{1,0},{2,3},{3,2},{4,5},{5,4},{6,7},{7,6},{8,9},{9,8},{10,11... | collective-permute-start | bytes 147464 | tf_op jit(solution)/shard_map/ppermute | solution.py:724
  13.9 6.0 %collective-permute-start.3 = (f32[96,128]{1,0:T(8,128)S(1)}, f32[96,128]{1,0:T(8,128)S(1)}, u32[]{:S(2)}, u32[]{:S(2)}) collective-permute-start(f32[96,128]{1,0:T(8,128)S(1)} %get-tuple-element.23.ns_two), channel_id=1, source_target_pairs={{1,2},{2,1},{3,4},{4,3},{5,6},{6,5},{7,8},{8,7},{9,10},{10,9},{11,... | collective-permute-start | bytes 147464 | tf_op jit(solution)/shard_map/ppermute | solution.py:725
  23.6 48.2 %all-to-all-start = ((f32[128,40,128]{2,1,0:T(8,128)}), f32[128,40,128]{2,1,0:T(8,128)S(1)}, u32[]{:S(2)}, u32[]{:S(2)}) async-start(f32[128,40,128]{2,1,0:T(8,128)} %bitcast.6), calls=%async_computation | async-start | bytes 5242880 | tf_op jit(solution)/shard_map/all_to_all | solution.py:738

commit v11 on v10

--- a/solution.py
+++ b/solution.py
@@ -15,8 +15,6 @@
 GROUPS = 16
 DEV, CAP = 128, 2
 CHUNKS = 20
-PARTS = 2
-EACH = 16
 PAIR = 2
 STEP = 8
 F32, BF16 = jnp.float32, jnp.bfloat16
@@ -121,7 +119,7 @@
     who = jnp.sum(jnp.where(down == across, who_row, 0), axis=1, keepdims=True)
     same = jnp.where((who == who_row) & (down < across), 1, 0)
     rank = jnp.sum(same, axis=0, keepdims=True)
-    row_of = who_row * CAP + rank
+    row_of = rank * DEV + who_row
     for part in range(CAP):
         here = jnp.where(down + part * DEV == row_of, 1.0, 0.0).astype(BF16)
         placing[pl.ds(part * DEV, DEV), 0:DEV] = here
@@ -371,7 +369,7 @@
 def kernel_second(
     num2, den2, ew, ew_one, ew_two, ns_one, ns_two, got_one, got_two, diff, placing, shares,
     send, d_ew, d_ns,
-    work, acc, chunks, send_s, sems,
+    work, pooled_rows, acc, chunks, send_s, sems,
 ):
     lane, sub = lane_iota(), sub_iota()
     odd = lax.axis_index("lat") % 2 == 1
@@ -417,17 +415,16 @@
 
     ends = ((lane & 63) == 0) | ((lane & 63) == 63)
 
-    def add_ends(step, carry):
-        for n in range(EACH):
-            k = step * EACH + n
-            for t in range(TR):
-                for q in range(4):
-                    rows = pl.ds(pl.multiple_of(k * 32 + q * 8, 8), 8)
-                    moved = pltpu.roll(work[t // 2, q], 63 - 2 * k + (128 - 32 * t), 1)
-                    acc[t, rows, :] = num2[t, rows, :] + jnp.where(ends, moved, 0.0)
-        return carry
-
-    lax.fori_loop(0, LV // EACH, add_ends, 0)
+    def add_ends(t):
+        for k in range(LV):
+            for q in range(4):
+                rows = pl.ds(k * 32 + q * 8, 8)
+                moved = pltpu.roll(work[t // 2, q], (63 - 2 * k - 32 * t) % 128, 1)
+                acc[t, rows, :] = num2[t, rows, :] + jnp.where(ends, moved, 0.0)
+        for top in range(2):
+            for half in range(2):
+                at = (t, pl.ds(256 * half + 31 * top, 8, stride=32), slice(None))
+                acc[at] = acc[at] + pooled_rows[top, t, pl.ds(8 * half, 8), :]
 
     pools = [shares[par] for par in range(2)]
     quarter = [shares[2 + j] for j in range(4)]
@@ -462,8 +459,9 @@
                 else:
                     div = p * near(t, top) - q * own(t, top)
                 d_ns[int(top), pl.ds(t * 16 + 8 * half, 8), :] = div
-                at = (t, pl.ds(256 * half + 31 * int(top), 8, stride=32), slice(None))
-                acc[at] = acc[at] + split_dot(gain * div, pools[int(top)])
+                pooled_rows[int(top), t, pl.ds(8 * half, 8), :] = split_dot(
+                    gain * div, pools[int(top)]
+                )
 
     def keep(n, values):
         high, low = halves(values)
@@ -474,6 +472,25 @@
         return jnp.concatenate(
             [ref[(*lead, pl.ds(32 * m + j, 8, stride=4), slice(None))] for m in range(16)], axis=0
         )
+
+    copies = []
+
+    def place(group):
+        placed = jnp.dot(
+            placing[...], chunks[:, pl.ds(group * 512, 512)], preferred_element_type=F32
+        )
+        for c in range(4):
+            for slot in range(CAP):
+                for m in range(DEV // 8):
+                    start = m * 8 * 40 + (4 * group + c) * CAP + slot
+                    send_s[pl.ds(start, 8, stride=40), :] = placed[
+                        slot * DEV + m * 8 : slot * DEV + m * 8 + 8, c * 128 : c * 128 + 128
+                    ]
+        part = send_s.reshape(DEV, 40, 128).at[:, pl.ds(8 * group, 8), :]
+        copies.append(
+            pltpu.make_async_copy(part, send.at[:, pl.ds(8 * group, 8), :], sems.at[group])
+        )
+        copies[-1].start()
 
     gains = []
     den4 = jnp.zeros((128, 128), F32)
@@ -483,28 +500,15 @@
         den4 = den4 + split_dot(den, quarter[j])
     gain4 = 1.0 / jnp.maximum(den4, weight_floor)
     for t in range(TR):
+        add_ends(t)
         num4 = jnp.zeros((128, 128), F32)
         for j in range(4):
             num = every_fourth(acc, t, j=j)
             keep(t * 4 + j, num * gains[j])
             num4 = num4 + split_dot(num, quarter[j])
         keep(16 + t, num4 * gain4)
-
-    each = CAP * DEV // PARTS
-    copies = []
-    for part in range(PARTS):
-        left = placing[pl.ds(part * each, each), :]
-        for n in range(CHUNKS // 2):
-            placed = jnp.dot(left, chunks[:, pl.ds(n * 256, 256)], preferred_element_type=F32)
-            for c in range(2):
-                for m in range(each // 8):
-                    start = (part * each + m * 8) * CHUNKS + 2 * n + c
-                    send_s[pl.ds(start, 8, stride=CHUNKS), :] = placed[
-                        m * 8 : m * 8 + 8, c * 128 : c * 128 + 128
-                    ]
-        rows = pl.ds(part * each * CHUNKS, each * CHUNKS)
-        copies.append(pltpu.make_async_copy(send_s.at[rows], send.at[rows], sems.at[part]))
-        copies[-1].start()
+        place(t)
+    place(TR)
     for copy in copies:
         copy.wait()
 
@@ -515,7 +519,7 @@
         kernel_second,
         name="second",
         out_shape=(
-            pltpu.HBM((DEV * CAP * CHUNKS, 128), F32),
+            pltpu.HBM((DEV, CAP * CHUNKS, 128), F32),
             jax.ShapeDtypeStruct((16, 8, 128), F32),
             jax.ShapeDtypeStruct((2, 64, 128), F32),
         ),
@@ -523,10 +527,11 @@
         out_specs=(pl.BlockSpec(memory_space=pltpu.HBM), vmem, vmem),
         scratch_shapes=[
             pltpu.VMEM((2, 4, 8, 128), F32),
+            pltpu.VMEM((2, TR, 16, 128), F32),
             pltpu.VMEM((TR, 512, 128), F32),
             pltpu.VMEM((256, 2560), BF16),
             pltpu.VMEM((DEV * CAP * CHUNKS, 128), F32),
-            pltpu.SemaphoreType.DMA((PARTS,)),
+            pltpu.SemaphoreType.DMA((TR + 1,)),
         ],
         compiler_params=pltpu.CompilerParams(vmem_limit_bytes=16 * MIB),
         cost_estimate=pl.CostEstimate(flops=60_000_000, bytes_accessed=6 * MIB, transcendentals=0),
@@ -653,24 +658,17 @@
     )(tracers, fill, mask, east, north, diff, area, d_ew, d_ns)
 
 
-SPLITS = 4
-
-
-def kernel_last(got, two, four, two_s, four_s, sems):
-    each = DEV * CAP // SPLITS
+def kernel_last(got, two, four, rows_s, sems):
     copies = []
-    for part in range(SPLITS):
-        for m in range(part * each // 8, (part + 1) * each // 8):
-            for n in range(CHUNKS):
-                value = got[pl.ds(m * 8 * CHUNKS + n, 8, stride=CHUNKS), :]
-                if n < 16:
-                    two_s[pl.ds(m * 8, 8), pl.ds(n * 128, 128)] = value
-                else:
-                    four_s[pl.ds(m * 8, 8), pl.ds((n - 16) * 128, 128)] = value
-        rows = pl.ds(part * each, each)
-        for n, (src, dst) in enumerate(((two_s, two), (four_s, four))):
-            copies.append(pltpu.make_async_copy(src.at[rows], dst.at[rows], sems.at[n, part]))
-            copies[-1].start()
+    for n in range(CHUNKS):
+        for slot in range(CAP):
+            for m in range(DEV // 8):
+                rows_s[n, pl.ds(m * 16 + slot, 8, stride=CAP), :] = got[
+                    pl.ds(m * 8 * 40 + n * CAP + slot, 8, stride=40), :
+                ]
+        out = two.at[:, pl.ds(n * 128, 128)] if n < 16 else four.at[:, pl.ds((n - 16) * 128, 128)]
+        copies.append(pltpu.make_async_copy(rows_s.at[n], out, sems.at[n]))
+        copies[-1].start()
     for copy in copies:
         copy.wait()
 
@@ -684,9 +682,8 @@
         in_specs=[pl.BlockSpec(memory_space=pltpu.VMEM)],
         out_specs=(hbm, hbm),
         scratch_shapes=[
-            pltpu.VMEM((DEV * CAP, 2048), F32),
-            pltpu.VMEM((DEV * CAP, 512), F32),
-            pltpu.SemaphoreType.DMA((2, SPLITS)),
+            pltpu.VMEM((CHUNKS, DEV * CAP, 128), F32),
+            pltpu.SemaphoreType.DMA((CHUNKS,)),
         ],
         compiler_params=pltpu.CompilerParams(vmem_limit_bytes=8 * MIB),
     )(got)
@@ -736,7 +733,7 @@
         shares,
     )
     got = lax.all_to_all(
-        send.reshape(DEV, CAP * CHUNKS, 128), both, split_axis=0, concat_axis=0, tiled=True
+        send, both, split_axis=0, concat_axis=0, tiled=True
     )
     updated = kernel_third_call(*in_hbm, diffusivity, area_hbm, d_ew, d_ns)
     two, four = kernel_last_call(got.reshape(DEV * CAP * CHUNKS, 128))

time: 73.7 us -> 73.6 us (level)
  no operation moved by 1% of the time
where the time goes in v11:
time: 73.6 us; the launch traced here: 73.2 us
  Pallas kernels  26.1 us (35%)
  waiting for transfers between devices  22.2 us (30%)
  starting transfers between devices  17.5 us (24%)
  local copies, waits for them, and re-layouts  6.62 us (9%)
  between operations  0.75 us (1%)
    all_to_all x1, waiting for transfers between devices, local(): got = lax.all_to_all(send, both, split_axis=0, concat_axis=0, tiled=True)  22.2 us
    pallas_call x1, Pallas kernels, kernel_third_call(): pl.pallas_call(kernel_third, name='third', out_shape=jax.ShapeDtypeStruct...  13.5 us
    all_to_all x1, starting transfers between devices, local(): got = lax.all_to_all(send, both, split_axis=0, concat_axis=0, tiled=True)  12.5 us
    unnamed x16, local copies, waits for them, and re-layouts  6.62 us
    pallas_call x1, Pallas kernels, kernel_first_call(): pl.pallas_call(kernel_first, name='first', out_shape=(jax.ShapeDtypeStruc...  4.46 us
    ppermute x1, starting transfers between devices, local(): lax.ppermute(ew, 'lon', swapped([(n, (n + 1) % lon_count) for n in range(...  4.13 us
    pallas_call x1, Pallas kernels, kernel_second_call(): pl.pallas_call(kernel_second, name='second', out_shape=(pltpu.HBM((DEV, C...  3.31 us
    pallas_call x1, Pallas kernels, kernel_edges_call(): pl.pallas_call(kernel_edges, name='edges', out_shape=(jax.ShapeDtypeStruc...  1.77 us
  transfers between devices with their start and end apart: 5, of which 1 were waited for; matrix products, arithmetic and copies ran while one was open for 0% of the time, Pallas kernels for 26%

profile of v11, /device:TPU:0, one launch (start us, length us, event | category | flops | bytes accessed | tf_op | source)
XLA Modules:
  0.0 73.2 jit_solution(14055501647529682615)
XLA Ops:
  0.6 0.0 copy-start
  0.6 2.2 %copy-done = f32[4,16,128,128]{3,2,1,0:T(8,128)S(1)} copy-done((f32[4,16,128,128]{3,2,1,0:T(8,128)S(1)}, f32[4,16,128,128]{3,2,1,0:T(8,128)}, u32[]{:S(2)}) %copy-start) | copy-done | bytes 4194328
  2.8 0.0 copy-start.2
  2.8 1.2 %copy-done.2 = f32[16,128,128]{2,1,0:T(8,128)S(1)} copy-done((f32[16,128,128]{2,1,0:T(8,128)S(1)}, f32[16,128,128]{2,1,0:T(8,128)}, u32[]{:S(2)}) %copy-start.2) | copy-done | bytes 1048600
  4.0 0.0 copy-start.3
  4.0 1.2 %copy-done.3 = s32[16,128,128]{2,1,0:T(8,128)S(1)} copy-done((s32[16,128,128]{2,1,0:T(8,128)S(1)}, s32[16,128,128]{2,1,0:T(8,128)}, u32[]{:S(2)}) %copy-start.3) | copy-done | bytes 1048600
  5.3 0.0 copy-start.4
  5.3 1.2 %copy-done.4 = f32[16,128,128]{2,1,0:T(8,128)S(1)} copy-done((f32[16,128,128]{2,1,0:T(8,128)S(1)}, f32[16,128,128]{2,1,0:T(8,128)}, u32[]{:S(2)}) %copy-start.4) | copy-done | bytes 1048600
  6.5 1.8 %edges.1 = (f32[16,16,8,128]{3,2,1,0:T(8,128)S(1)}, f32[24,8,128]{2,1,0:T(8,128)S(1)}) custom-call(f32[4,16,128,128]{3,2,1,0:T(8,128)S(1)} %copy-done, f32[16,128,128]{2,1,0:T(8,128)S(1)} %copy-done.2, s32[16,128,128]{2,1,0:T(8,128)S(1)} %copy-done.3, f32[16,128,128]{2,1,0:T(8,128)S(1)} %copy-done.4), custom_call_target="tpu_custom_call" | custom-call | flops 60000000 | bytes 11534336 | tf_op jit(solution)/shard_map/edges/pallas_call | solution.py:215
  8.3 4.1 %collective-permute-start.1 = (f32[24,8,128]{2,1,0:T(8,128)S(1)}, f32[24,8,128]{2,1,0:T(8,128)S(1)}, u32[]{:S(2)}, u32[]{:S(2)}) collective-permute-start(f32[24,8,128]{2,1,0:T(8,128)S(1)} %get-tuple-element.21.ew), channel_id=1, source_target_pairs={{16,32},{32,16},{48,64},{64,48},{80,96},{96,80},{112,0},{0,112},{1... | collective-permute-start | bytes 294920 | tf_op jit(solution)/shard_map/ppermute | solution.py:725
  12.4 0.0 collective-permute-start
  12.4 0.0 copy-start.1
  12.4 0.0 copy-start.5
  12.4 0.0 copy-start.6
  12.4 0.0 copy-start.7
  12.4 1.4 %rows.1 = (f32[96,128]{1,0:T(8,128)S(1)}, f32[96,128]{1,0:T(8,128)S(1)}, bf16[256,256]{1,0:T(8,128)(2,1)S(1)}, bf16[512,128]{1,0:T(8,128)(2,1)S(1)}, bf16[6,128,128]{2,1,0:T(8,128)(2,1)S(1)}) custom-call(f32[4,16,128,128]{3,2,1,0:T(8,128)} %tr.3, f32[16,128,128]{2,1,0:T(8,128)} %fill.3, s32[16,128,128]{2,1,0:T(8,128)} %mask.3, f32[16,128,128]{2,1,0:T(8,128)} %north.3, ...), custom_call_target="tpu_custom_call" | custom-call | flops 1000000 | bytes 1048576 | tf_op jit(solution)/shard_map/rows/pallas_call | solution.py:152
  13.8 0.1 collective-permute-start.2
  13.9 0.8 %collective-permute-start.3 = (f32[96,128]{1,0:T(8,128)S(1)}, f32[96,128]{1,0:T(8,128)S(1)}, u32[]{:S(2)}, u32[]{:S(2)}) collective-permute-start(f32[96,128]{1,0:T(8,128)S(1)} %get-tuple-element.23.ns_two), channel_id=1, source_target_pairs={{1,2},{2,1},{3,4},{4,3},{5,6},{6,5},{7,8},{8,7},{9,10},{10,9},{11,... | collective-permute-start | bytes 147464 | tf_op jit(solution)/shard_map/ppermute | solution.py:722
  14.7 0.1 copy-done.1
  14.9 0.3 copy-done.5
  15.2 0.3 copy-done.6
  15.5 0.0 copy-done.7
  15.5 4.5 %first.1 = (f32[4,512,128]{2,1,0:T(8,128)S(1)}, f32[512,128]{1,0:T(8,128)S(1)}) custom-call(f32[4,16,128,128]{3,2,1,0:T(8,128)S(1)} %copy-done.1, f32[16,16,8,128]{3,2,1,0:T(8,128)S(1)} %get-tuple-element.17.h_v, f32[16,128,128]{2,1,0:T(8,128)S(1)} %copy-done.5, f32[16,128,128]{2,1,0:T(8,128)S(1)} %copy-done.6, f32[128,128]{1,0:T(8,128)S(1)} %copy-done.7, ...), custom_call_target="tpu_custom_call" | custom-call | flops 60000000 | bytes 11534336 | tf_op jit(solution)/shard_map/first/pallas_call | solution.py:343
  20.0 0.0 collective-permute-done.2.got_one
  20.0 0.0 collective-permute-done.3.got_two
  20.0 0.0 collective-permute-done.1.ew_two
  20.0 0.0 collective-permute-done.ew_one
  20.0 3.3 %second.1 = (f32[128,40,128]{2,1,0:T(8,128)}, f32[16,8,128]{2,1,0:T(8,128)S(1)}, f32[2,64,128]{2,1,0:T(8,128)S(1)}) custom-call(f32[4,512,128]{2,1,0:T(8,128)S(1)} %get-tuple-element.19.num2, f32[512,128]{1,0:T(8,128)S(1)} %get-tuple-element.20.den2, f32[24,8,128]{2,1,0:T(8,128)S(1)} %get-tuple-element.21.ew, f32[24,8,128]{2,1,0:T(8,128)S(1)} %collective-permute-done.ew_one, ...), custom_call_target="tpu_custom_call" | custom-call | flops 60000000 | bytes 6291456 | tf_op jit(solution)/shard_map/second/pallas_call | solution.py:518
  23.3 12.5 %all-to-all-start = ((f32[128,40,128]{2,1,0:T(8,128)}), f32[128,40,128]{2,1,0:T(8,128)S(1)}, u32[]{:S(2)}, u32[]{:S(2)}) async-start(f32[128,40,128]{2,1,0:T(8,128)} %get-tuple-element.28), calls=%async_computation | async-start | bytes 5242880 | tf_op jit(solution)/shard_map/all_to_all | solution.py:735
  35.8 13.5 %third.1 = f32[4,16,128,128]{3,2,1,0:T(8,128)} custom-call(f32[4,16,128,128]{3,2,1,0:T(8,128)} %tr.3, f32[16,128,128]{2,1,0:T(8,128)} %fill.3, s32[16,128,128]{2,1,0:T(8,128)} %mask.3, f32[16,128,128]{2,1,0:T(8,128)} %east.1, f32[16,128,128]{2,1,0:T(8,128)} %north.3, f32[16]{0:T(128)} %diff.5, f32[128,128]{1,0:T(8,128)} %area.1, ...), custom_call_target="tpu_custom_call" | custom-call | flops 60000000 | bytes 12582912 | tf_op jit(solution)/shard_map/third/pallas_call | solution.py:637
  49.3 22.2 %all-to-all-done = f32[128,40,128]{2,1,0:T(8,128)S(1)} async-done(((f32[128,40,128]{2,1,0:T(8,128)}), f32[128,40,128]{2,1,0:T(8,128)S(1)}, u32[]{:S(2)}, u32[]{:S(2)}) %all-to-all-start) | async-done | bytes 2621472 | tf_op jit(solution)/shard_map/all_to_all | solution.py:735
  71.5 1.7 %last.1 = (f32[256,2048]{1,0:T(8,128)}, f32[256,512]{1,0:T(8,128)}) custom-call(f32[5120,128]{1,0:T(8,128)S(1)} %bitcast.4), custom_call_target="tpu_custom_call" | custom-call | tf_op jit(solution)/shard_map/last/pallas_call | solution.py:678
Async XLA Ops:
  0.6 2.2 %copy-start = (f32[4,16,128,128]{3,2,1,0:T(8,128)S(1)}, f32[4,16,128,128]{3,2,1,0:T(8,128)}, u32[]{:S(2)}) copy-start(f32[4,16,128,128]{3,2,1,0:T(8,128)} %tr.3) | copy-start | bytes 12582916
  2.8 1.2 %copy-start.2 = (f32[16,128,128]{2,1,0:T(8,128)S(1)}, f32[16,128,128]{2,1,0:T(8,128)}, u32[]{:S(2)}) copy-start(f32[16,128,128]{2,1,0:T(8,128)} %fill.3) | copy-start | bytes 3145732
  4.0 1.2 %copy-start.3 = (s32[16,128,128]{2,1,0:T(8,128)S(1)}, s32[16,128,128]{2,1,0:T(8,128)}, u32[]{:S(2)}) copy-start(s32[16,128,128]{2,1,0:T(8,128)} %mask.3) | copy-start | bytes 3145732
  5.3 1.2 %copy-start.4 = (f32[16,128,128]{2,1,0:T(8,128)S(1)}, f32[16,128,128]{2,1,0:T(8,128)}, u32[]{:S(2)}) copy-start(f32[16,128,128]{2,1,0:T(8,128)} %east.1) | copy-start | bytes 3145732
  8.3 11.7 %collective-permute-start.1 = (f32[24,8,128]{2,1,0:T(8,128)S(1)}, f32[24,8,128]{2,1,0:T(8,128)S(1)}, u32[]{:S(2)}, u32[]{:S(2)}) collective-permute-start(f32[24,8,128]{2,1,0:T(8,128)S(1)} %get-tuple-element.21.ew), channel_id=1, source_target_pairs={{16,32},{32,16},{48,64},{64,48},{80,96},{96,80},{112,0},{0,112},{1... | collective-permute-start | bytes 294920 | tf_op jit(solution)/shard_map/ppermute | solution.py:725
  12.4 7.6 %collective-permute-start = (f32[24,8,128]{2,1,0:T(8,128)S(1)}, f32[24,8,128]{2,1,0:T(8,128)S(1)}, u32[]{:S(2)}, u32[]{:S(2)}) collective-permute-start(f32[24,8,128]{2,1,0:T(8,128)S(1)} %get-tuple-element.21.ew), channel_id=1, source_target_pairs={{0,16},{16,0},{32,48},{48,32},{64,80},{80,64},{96,112},{112,96},{1... | collective-permute-start | bytes 294920 | tf_op jit(solution)/shard_map/ppermute | solution.py:724
  12.4 2.5 %copy-start.1 = (f32[4,16,128,128]{3,2,1,0:T(8,128)S(1)}, f32[4,16,128,128]{3,2,1,0:T(8,128)}, u32[]{:S(2)}) copy-start(f32[4,16,128,128]{3,2,1,0:T(8,128)} %tr.3) | copy-start | bytes 12582916
  12.4 2.8 %copy-start.5 = (f32[16,128,128]{2,1,0:T(8,128)S(1)}, f32[16,128,128]{2,1,0:T(8,128)}, u32[]{:S(2)}) copy-start(f32[16,128,128]{2,1,0:T(8,128)} %east.1) | copy-start | bytes 3145732
  12.4 3.1 %copy-start.6 = (f32[16,128,128]{2,1,0:T(8,128)S(1)}, f32[16,128,128]{2,1,0:T(8,128)}, u32[]{:S(2)}) copy-start(f32[16,128,128]{2,1,0:T(8,128)} %north.3) | copy-start | bytes 3145732
  12.4 3.1 %copy-start.7 = (f32[128,128]{1,0:T(8,128)S(1)}, f32[128,128]{1,0:T(8,128)}, u32[]{:S(2)}) copy-start(f32[128,128]{1,0:T(8,128)} %area.1) | copy-start | bytes 196612
  13.8 6.1 %collective-permute-start.2 = (f32[96,128]{1,0:T(8,128)S(1)}, f32[96,128]{1,0:T(8,128)S(1)}, u32[]{:S(2)}, u32[]{:S(2)}) collective-permute-start(f32[96,128]{1,0:T(8,128)S(1)} %get-tuple-element.22.ns_one), channel_id=1, source_target_pairs={{0,1},{1,0},{2,3},{3,2},{4,5},{5,4},{6,7},{7,6},{8,9},{9,8},{10,11... | collective-permute-start | bytes 147464 | tf_op jit(solution)/shard_map/ppermute | solution.py:721
  13.9 6.0 %collective-permute-start.3 = (f32[96,128]{1,0:T(8,128)S(1)}, f32[96,128]{1,0:T(8,128)S(1)}, u32[]{:S(2)}, u32[]{:S(2)}) collective-permute-start(f32[96,128]{1,0:T(8,128)S(1)} %get-tuple-element.23.ns_two), channel_id=1, source_target_pairs={{1,2},{2,1},{3,4},{4,3},{5,6},{6,5},{7,8},{8,7},{9,10},{10,9},{11,... | collective-permute-start | bytes 147464 | tf_op jit(solution)/shard_map/ppermute | solution.py:722
  23.3 48.2 %all-to-all-start = ((f32[128,40,128]{2,1,0:T(8,128)}), f32[128,40,128]{2,1,0:T(8,128)S(1)}, u32[]{:S(2)}, u32[]{:S(2)}) async-start(f32[128,40,128]{2,1,0:T(8,128)} %get-tuple-element.28), calls=%async_computation | async-start | bytes 5242880 | tf_op jit(solution)/shard_map/all_to_all | solution.py:735
